TPU v7x, 32 devices: a whole 2x2x4 slice. The times are simulated.
32 devices in a mesh: ctx: 16 (over z, y, core), fsdp: 2 (over x).
Axes of the slice: x: 2, y: 2, z: 4, core: 2. Of those that a mesh axis runs over, the one named last changes fastest.
Arguments:
- residual_in: bfloat16 [4096, 1024], P(('ctx', 'fsdp')), may hold values from -6 to 6
- first_gain: bfloat16 [1024], P(('ctx', 'fsdp')), may hold values from 0.5 to 1.5
- first_shift: bfloat16 [1024], P(('ctx', 'fsdp')), may hold values from -3 to 3
- attend_weight: bfloat16 [1024, 3072], P(('ctx', 'fsdp')), may hold values from -0.1875 to 0.1875
- attend_bias: bfloat16 [2048], P(('ctx', 'fsdp')), may hold values from -0.59765625 to 0.59765625
- merge_weight: bfloat16 [1024, 1024], P(('ctx', 'fsdp')), may hold values from -3 to 3
- merge_bias: bfloat16 [1024], P(('ctx', 'fsdp')), may hold values from -3 to 3
- second_gain: bfloat16 [1024], P(('ctx', 'fsdp')), may hold values from 0.5 to 1.5
- second_shift: bfloat16 [1024], P(('ctx', 'fsdp')), may hold values from -3 to 3
- expand_weight: bfloat16 [1024, 4096], P(('ctx', 'fsdp')), may hold values from -0.1875 to 0.1875
- expand_bias: bfloat16 [4096], P(('ctx', 'fsdp')), may hold values from -3 to 3
- shrink_weight: bfloat16 [4096, 1024], P(('ctx', 'fsdp')), may hold values from -0.09375 to 0.09375
- shrink_bias: bfloat16 [1024], P(('ctx', 'fsdp')), may hold values from -3 to 3
- cotangent: bfloat16 [4096, 1024], P(('ctx', 'fsdp')), may hold values from -6 to 6
Outputs:
- residual_out: bfloat16 [4096, 1024], P(('ctx', 'fsdp'))
- input_grad: float32 [4096, 1024], P(('ctx', 'fsdp'))
- grad_first_gain: float32 [1024], P(('ctx', 'fsdp'))
- grad_first_shift: float32 [1024], P(('ctx', 'fsdp'))
- grad_attend_weight: float32 [1024, 3072], P(('ctx', 'fsdp'))
- grad_attend_bias: float32 [2048], P(('ctx', 'fsdp'))
- grad_merge_weight: float32 [1024, 1024], P(('ctx', 'fsdp'))
- grad_merge_bias: float32 [1024], P(('ctx', 'fsdp'))
- grad_second_gain: float32 [1024], P(('ctx', 'fsdp'))
- grad_second_shift: float32 [1024], P(('ctx', 'fsdp'))
- grad_expand_weight: float32 [1024, 4096], P(('ctx', 'fsdp'))
- grad_expand_bias: float32 [4096], P(('ctx', 'fsdp'))
- grad_shrink_weight: float32 [4096, 1024], P(('ctx', 'fsdp'))
- grad_shrink_bias: float32 [1024], P(('ctx', 'fsdp'))
All inputs are finite; a program needn't handle non-finite values.
Results may differ from a plain program's by a relative error of at most 0.014.
Values may be sent and summed in bfloat16 or wider, within the bound.
A program may use at most 384 MiB of HBM per device.

v0:
```python
import math

import jax
import jax.numpy as jnp
from jax import lax
from jax.sharding import PartitionSpec as P

H = 16


EPSILON = 1e-05
GELU_SCALE = 0.7978845608028654
GELU_CUBIC = 0.044715


def normalize(inputs, gain_row, shift_row):
    centred = inputs - jnp.mean(inputs, axis=1, keepdims=True)
    inverse = lax.rsqrt(jnp.mean(centred * centred, axis=1, keepdims=True) + EPSILON)
    scaled = centred * inverse
    return (scaled, inverse, scaled * gain_row + shift_row)


def normalize_back(grad_norm, scaled, inverse, gain_row):
    grad_scaled = grad_norm * gain_row
    mean_one = jnp.mean(grad_scaled, axis=1, keepdims=True)
    mean_two = jnp.mean(grad_scaled * scaled, axis=1, keepdims=True)
    grad_inputs = inverse * (grad_scaled - mean_one - scaled * mean_two)
    return (grad_inputs, jnp.sum(grad_norm * scaled, axis=0), jnp.sum(grad_norm, axis=0))


def gelu_pair(pre_act):
    tangent = jnp.tanh(GELU_SCALE * (pre_act + GELU_CUBIC * pre_act * pre_act * pre_act))
    activated = 0.5 * pre_act * (1.0 + tangent)
    derivative = 0.5 * (1.0 + tangent) + 0.5 * pre_act * (1.0 - tangent * tangent) * GELU_SCALE * (
        1.0 + 3.0 * GELU_CUBIC * pre_act * pre_act
    )
    return (activated, derivative)


def fold_blocks(update, running, pieces):
    piece_rows = pieces[0].shape[0]
    block_size = math.gcd(piece_rows, 512)
    block_count = piece_rows // block_size
    stacked = tuple(
        (member.reshape((block_count, block_size) + member.shape[1:]) for member in pieces)
    )

    def advance(current, element):
        block_index, sub_pieces = element
        return (update(current, sub_pieces, block_index * block_size), None)

    result, unused = lax.scan(advance, running, (jnp.arange(block_count, dtype=jnp.int32), stacked))
    return result


def on_device(
    residual_in,
    first_gain,
    first_shift,
    attend_weight,
    attend_bias,
    merge_weight,
    merge_bias,
    second_gain,
    second_shift,
    expand_weight,
    expand_bias,
    shrink_weight,
    shrink_bias,
    cotangent,
):
    row_count = residual_in.shape[0]
    model_width = residual_in.shape[1]
    head_size = model_width // H
    scaling = 1.0 / math.sqrt(head_size)
    first_row = lax.axis_index(("ctx", "fsdp")) * row_count
    local_pos = first_row + jnp.arange(row_count, dtype=jnp.int32)
    parameters = (
        first_gain,
        first_shift,
        attend_weight,
        attend_bias,
        merge_weight,
        merge_bias,
        second_gain,
        second_shift,
        expand_weight,
        expand_bias,
        shrink_weight,
        shrink_bias,
    )
    gathered = (
        lax.all_gather(parameters[0], ("ctx", "fsdp"), axis=0, tiled=True),
        lax.all_gather(parameters[1], ("ctx", "fsdp"), axis=0, tiled=True),
        lax.all_gather(parameters[2], ("ctx", "fsdp"), axis=0, tiled=True),
        lax.all_gather(parameters[3], ("ctx", "fsdp"), axis=0, tiled=True),
        lax.all_gather(parameters[4], ("ctx", "fsdp"), axis=0, tiled=True),
        lax.all_gather(parameters[5], ("ctx", "fsdp"), axis=0, tiled=True),
        lax.all_gather(parameters[6], ("ctx", "fsdp"), axis=0, tiled=True),
        lax.all_gather(parameters[7], ("ctx", "fsdp"), axis=0, tiled=True),
        lax.all_gather(parameters[8], ("ctx", "fsdp"), axis=0, tiled=True),
        lax.all_gather(parameters[9], ("ctx", "fsdp"), axis=0, tiled=True),
        lax.all_gather(parameters[10], ("ctx", "fsdp"), axis=0, tiled=True),
        lax.all_gather(parameters[11], ("ctx", "fsdp"), axis=0, tiled=True),
    )
    (
        gain_one,
        shift_one,
        attend_full,
        attend_shift,
        merge_full,
        merge_shift,
        gain_two,
        shift_two,
        expand_full,
        expand_shift,
        shrink_full,
        shrink_shift,
    ) = gathered
    block_in = residual_in.astype(jnp.float32)
    scaled_one, inverse_one, normed_one = normalize(
        block_in, gain_one.astype(jnp.float32), shift_one.astype(jnp.float32)
    )
    input_one = normed_one.astype(jnp.bfloat16)
    projected = jnp.dot(input_one, attend_full, preferred_element_type=jnp.float32)
    bias_float = attend_shift.astype(jnp.float32)
    queries = (projected[:, :model_width] + bias_float[:model_width]).astype(jnp.bfloat16)
    key_rows = projected[:, model_width : 2 * model_width].astype(jnp.bfloat16)
    value_rows = (projected[:, 2 * model_width :] + bias_float[model_width:]).astype(jnp.bfloat16)
    query_heads = queries.reshape(row_count, H, head_size)
    local_keys = key_rows.reshape(row_count, H, head_size)
    local_values = value_rows.reshape(row_count, H, head_size)

    def masked_scores(query_part, key_part, query_pos, key_pos):
        scores = (
            jnp.einsum("qhd,khd->hqk", query_part, key_part, preferred_element_type=jnp.float32)
            * scaling
        )
        allowed = key_pos[None, :] <= query_pos[:, None]
        return jnp.where(allowed[None], scores, -jnp.inf)

    def attend_step(running, portion, offset):
        key_part, value_part = portion
        piece_rows = key_part.shape[0]
        key_heads = key_part.reshape(piece_rows, H, head_size)
        value_heads = value_part.reshape(piece_rows, H, head_size)
        max_old, totals_old, summed_old = running
        scores = masked_scores(
            query_heads, key_heads, local_pos, offset + jnp.arange(piece_rows, dtype=jnp.int32)
        )
        max_new = jnp.maximum(max_old, jnp.max(scores, axis=2))
        weights = jnp.exp(scores - max_new[:, :, None])
        factor = jnp.exp(max_old - max_new)
        totals_new = totals_old * factor + jnp.sum(weights, axis=2)
        summed_new = summed_old * factor[:, :, None] + jnp.einsum(
            "hqk,khd->hqd",
            weights.astype(jnp.bfloat16),
            value_heads,
            preferred_element_type=jnp.float32,
        )
        return (max_new, totals_new, summed_new)

    start_state = (
        jnp.full((H, row_count), -1e30, jnp.float32),
        jnp.zeros((H, row_count), jnp.float32),
        jnp.zeros((H, row_count, head_size), jnp.float32),
    )
    running_max, totals, summed = fold_blocks(
        attend_step,
        start_state,
        (
            lax.all_gather(key_rows, ("ctx", "fsdp"), axis=0, tiled=True),
            lax.all_gather(value_rows, ("ctx", "fsdp"), axis=0, tiled=True),
        ),
    )
    attended = (
        (summed / totals[:, :, None])
        .transpose(1, 0, 2)
        .reshape(row_count, model_width)
        .astype(jnp.bfloat16)
    )
    lse_heads = running_max + jnp.log(totals)
    log_total = lse_heads.T
    merged = jnp.dot(attended, merge_full, preferred_element_type=jnp.float32) + merge_shift.astype(
        jnp.float32
    )
    hidden = block_in + merged
    scaled_two, inverse_two, normed_two = normalize(
        hidden, gain_two.astype(jnp.float32), shift_two.astype(jnp.float32)
    )
    input_two = normed_two.astype(jnp.bfloat16)
    pre_act = jnp.dot(
        input_two, expand_full, preferred_element_type=jnp.float32
    ) + expand_shift.astype(jnp.float32)
    activated, derivative = gelu_pair(pre_act)
    act_input = activated.astype(jnp.bfloat16)
    residual_out = (
        hidden
        + jnp.dot(act_input, shrink_full, preferred_element_type=jnp.float32)
        + shrink_shift.astype(jnp.float32)
    ).astype(jnp.bfloat16)
    back_gain_one = gathered[0].astype(jnp.float32)
    back_attend = gathered[2]
    back_merge = gathered[4]
    back_gain_two = gathered[6].astype(jnp.float32)
    back_expand = gathered[8]
    back_shrink = gathered[10]
    grad_top = cotangent.astype(jnp.float32)
    grad_shrink_bias = jnp.sum(grad_top, axis=0)
    grad_shrink_weight = jnp.einsum(
        "tf,td->fd", act_input, cotangent, preferred_element_type=jnp.float32
    )
    grad_pre = (
        jnp.einsum("td,fd->tf", cotangent, back_shrink, preferred_element_type=jnp.float32)
        * derivative
    )
    grad_expand_bias = jnp.sum(grad_pre, axis=0)
    grad_pre_input = grad_pre.astype(jnp.bfloat16)
    grad_expand_weight = jnp.einsum(
        "td,tf->df", input_two, grad_pre_input, preferred_element_type=jnp.float32
    )
    grad_two = jnp.einsum(
        "tf,df->td", grad_pre_input, back_expand, preferred_element_type=jnp.float32
    )
    grad_norm_two, grad_second_gain, grad_second_shift = normalize_back(
        grad_two, scaled_two, inverse_two, back_gain_two
    )
    grad_hidden = grad_top + grad_norm_two
    grad_hidden_input = grad_hidden.astype(jnp.bfloat16)
    grad_merge_bias = jnp.sum(grad_hidden, axis=0)
    grad_merge_weight = jnp.einsum(
        "td,te->de", attended, grad_hidden_input, preferred_element_type=jnp.float32
    )
    grad_attended = jnp.einsum(
        "te,de->td", grad_hidden_input, back_merge, preferred_element_type=jnp.float32
    ).astype(jnp.bfloat16)
    row_delta = jnp.sum(
        (grad_attended.astype(jnp.float32) * attended.astype(jnp.float32)).reshape(
            row_count, H, head_size
        ),
        axis=2,
    )
    delta_heads = row_delta.T
    grad_heads = grad_attended.reshape(row_count, H, head_size)
    all_totals, all_delta = (
        lax.all_gather(log_total, ("ctx", "fsdp"), axis=0, tiled=True),
        lax.all_gather(row_delta, ("ctx", "fsdp"), axis=0, tiled=True),
    )

    def query_side(current, key_heads, value_heads, offset, piece_rows):
        scores = masked_scores(
            query_heads, key_heads, local_pos, offset + jnp.arange(piece_rows, dtype=jnp.int32)
        )
        probs_full = jnp.exp(scores - lse_heads[:, :, None])
        grad_probs = jnp.einsum(
            "qhd,khd->hqk", grad_heads, value_heads, preferred_element_type=jnp.float32
        )
        grad_scores = (probs_full * (grad_probs - delta_heads[:, :, None]) * scaling).astype(
            jnp.bfloat16
        )
        return current + jnp.einsum(
            "hqk,khd->hqd", grad_scores, key_heads, preferred_element_type=jnp.float32
        )

    def key_side(current, query_piece, grad_piece, offset, piece_rows):
        grad_key_old, grad_value_old = current
        total_part = lax.dynamic_slice_in_dim(all_totals, offset, piece_rows, 0).T
        delta_part = lax.dynamic_slice_in_dim(all_delta, offset, piece_rows, 0).T
        scores = masked_scores(
            query_piece, local_keys, offset + jnp.arange(piece_rows, dtype=jnp.int32), local_pos
        )
        probs_full = jnp.exp(scores - total_part[:, :, None])
        grad_value_new = grad_value_old + jnp.einsum(
            "hqk,qhd->khd",
            probs_full.astype(jnp.bfloat16),
            grad_piece,
            preferred_element_type=jnp.float32,
        )
        grad_probs = jnp.einsum(
            "qhd,khd->hqk", grad_piece, local_values, preferred_element_type=jnp.float32
        )
        grad_scores = (probs_full * (grad_probs - delta_part[:, :, None]) * scaling).astype(
            jnp.bfloat16
        )
        grad_key_new = grad_key_old + jnp.einsum(
            "hqk,qhd->khd", grad_scores, query_piece, preferred_element_type=jnp.float32
        )
        return (grad_key_new, grad_value_new)

    def backward_step(running, portion, offset):
        key_part, value_part, query_part, grad_part = portion
        piece_rows = key_part.shape[0]
        key_heads = key_part.reshape(piece_rows, H, head_size)
        value_heads = value_part.reshape(piece_rows, H, head_size)
        query_piece = query_part.reshape(piece_rows, H, head_size)
        grad_piece = grad_part.reshape(piece_rows, H, head_size)
        query_state = running[0]
        key_state = (running[1], running[2])
        query_state = query_side(query_state, key_heads, value_heads, offset, piece_rows)
        key_state = key_side(key_state, query_piece, grad_piece, offset, piece_rows)
        return (query_state, key_state[0], key_state[1])

    zero_heads = jnp.zeros((row_count, H, head_size), jnp.float32)
    start_back = (jnp.zeros((H, row_count, head_size), jnp.float32), zero_heads, zero_heads)
    grad_query_heads, grad_key_heads, grad_value_heads = fold_blocks(
        backward_step,
        start_back,
        (
            lax.all_gather(key_rows, ("ctx", "fsdp"), axis=0, tiled=True),
            lax.all_gather(value_rows, ("ctx", "fsdp"), axis=0, tiled=True),
            lax.all_gather(queries, ("ctx", "fsdp"), axis=0, tiled=True),
            lax.all_gather(grad_attended, ("ctx", "fsdp"), axis=0, tiled=True),
        ),
    )
    grad_queries = grad_query_heads.transpose(1, 0, 2).reshape(row_count, model_width)
    grad_keys = grad_key_heads.reshape(row_count, model_width)
    grad_values = grad_value_heads.reshape(row_count, model_width)
    grad_attend_bias = jnp.concatenate(
        [jnp.sum(grad_queries, axis=0), jnp.sum(grad_values, axis=0)]
    )
    grad_projected = jnp.concatenate([grad_queries, grad_keys, grad_values], axis=1).astype(
        jnp.bfloat16
    )
    grad_attend_weight = jnp.einsum(
        "td,te->de", input_one, grad_projected, preferred_element_type=jnp.float32
    )
    grad_one = jnp.einsum(
        "te,de->td", grad_projected, back_attend, preferred_element_type=jnp.float32
    )
    grad_norm_one, grad_first_gain, grad_first_shift = normalize_back(
        grad_one, scaled_one, inverse_one, back_gain_one
    )
    input_grad = grad_hidden + grad_norm_one
    all_sums = (
        lax.psum_scatter(grad_first_gain, ("ctx", "fsdp"), scatter_dimension=0, tiled=True),
        lax.psum_scatter(grad_first_shift, ("ctx", "fsdp"), scatter_dimension=0, tiled=True),
        lax.psum_scatter(grad_attend_weight, ("ctx", "fsdp"), scatter_dimension=0, tiled=True),
        lax.psum_scatter(grad_attend_bias, ("ctx", "fsdp"), scatter_dimension=0, tiled=True),
        lax.psum_scatter(grad_merge_weight, ("ctx", "fsdp"), scatter_dimension=0, tiled=True),
        lax.psum_scatter(grad_merge_bias, ("ctx", "fsdp"), scatter_dimension=0, tiled=True),
        lax.psum_scatter(grad_second_gain, ("ctx", "fsdp"), scatter_dimension=0, tiled=True),
        lax.psum_scatter(grad_second_shift, ("ctx", "fsdp"), scatter_dimension=0, tiled=True),
        lax.psum_scatter(grad_expand_weight, ("ctx", "fsdp"), scatter_dimension=0, tiled=True),
        lax.psum_scatter(grad_expand_bias, ("ctx", "fsdp"), scatter_dimension=0, tiled=True),
        lax.psum_scatter(grad_shrink_weight, ("ctx", "fsdp"), scatter_dimension=0, tiled=True),
        lax.psum_scatter(grad_shrink_bias, ("ctx", "fsdp"), scatter_dimension=0, tiled=True),
    )
    return (residual_out, input_grad) + tuple(all_sums)


def solution(mesh):
    placed = (
        P(("ctx", "fsdp"), None),
        P(("ctx", "fsdp")),
        P(("ctx", "fsdp")),
        P(("ctx", "fsdp"), None),
        P(("ctx", "fsdp")),
        P(("ctx", "fsdp"), None),
        P(("ctx", "fsdp")),
        P(("ctx", "fsdp")),
        P(("ctx", "fsdp")),
        P(("ctx", "fsdp"), None),
        P(("ctx", "fsdp")),
        P(("ctx", "fsdp"), None),
        P(("ctx", "fsdp")),
        P(("ctx", "fsdp"), None),
    )
    return jax.shard_map(
        on_device,
        mesh=mesh,
        in_specs=placed,
        out_specs=(
            P(("ctx", "fsdp"), None),
            P(("ctx", "fsdp"), None),
            P(("ctx", "fsdp")),
            P(("ctx", "fsdp")),
            P(("ctx", "fsdp"), None),
            P(("ctx", "fsdp")),
            P(("ctx", "fsdp"), None),
            P(("ctx", "fsdp")),
            P(("ctx", "fsdp")),
            P(("ctx", "fsdp")),
            P(("ctx", "fsdp"), None),
            P(("ctx", "fsdp")),
            P(("ctx", "fsdp"), None),
            P(("ctx", "fsdp")),
        ),
        check_vma=False,
    )
```

profile of v0, /device:TPU:0, one launch (start us, length us, event | category | flops | bytes accessed | tf_op | source)
XLA Modules:
  0.0 1751.1 jit_solution(10655309307869524012)
XLA Ops:
  13.8 42.5 %all-reduce.16 = (bf16[1024]{0:T(1024)(128)(2,1)S(1)}, bf16[1024]{0:T(1024)(128)(2,1)S(1)}, bf16[2048]{0:T(1024)(128)(2,1)S(1)}, bf16[1024]{0:T(1024)(128)(2,1)S...) all-reduce(bf16[1024]{0:T(1024)(128)(2,1)S(1)} %dynamic-update-slic, ...), channel_id=1, replica_groups=mesh['ctx'=16,'fsdp'=2] {'ctx','fsdp'}, use_global_device_ids=true, to_apply=%add.1 | all-reduce | flops 8192 | bytes 32768
  58.6 24.2 %all-gather.10.cloned.1.call-done = bf16[1024,3072]{1,0:T(8,128)(2,1)} async-done(((bf16[32,3072]{1,0:T(8,128)(2,1)}), bf16[1024,3072]{1,0:T(8,128)(2,1)}) %all-gather.10.cloned.1.call-update) | async-done | bytes 6291472 | tf_op jit(solution)/shard_map/all_gather | solution.py:95
  90.3 66.7 %all-gather = bf16[32,1,128]{2,1,0:T(2,128)(2,1)S(1)} all-gather(bf16[1,1,128]{2,1,0:T(2,128)(2,1)S(1)} %bitcast.192), channel_id=1, replica_groups=mesh['ctx'=16,'fsdp'=2] {'ctx','fsdp'}, dimensions={0}, use_global_device_ids=true | all-gather | bytes 8448 | tf_op jit(solution)/shard_map/all_gather | solution.py:102
  157.5 6.0 all-gather.12.cloned.1.call-done
  163.5 11.5 copy.58
  175.0 67.9 %all-gather.14.cloned.1.call-done = bf16[4096,1024]{1,0:T(8,128)(2,1)} async-done(((bf16[128,1024]{1,0:T(8,128)(2,1)}), bf16[4096,1024]{1,0:T(8,128)(2,1)}) %all-gather.14.cloned.1.call-update) | async-done | bytes 8388624 | tf_op jit(solution)/shard_map/all_gather | solution.py:173
  242.8 11.4 copy.59
  254.2 88.0 %while.30 = (s32[]{:T(128)}, f32[16,128]{1,0:T(8,128)S(1)}, f32[16,128]{1,0:T(8,128)S(1)}, f32[16,128,64]{1,2,0:T(8,128)S(1)}, s32[8]{0:T(128)S(1)}, /*index=5*/...) while((s32[]{:T(128)}, f32[16,128]{1,0:T(8,128)S(1)}, ...), condition=%wide.region_5.6_spmd.clone, body=%wide.region_2.5_spmd.clone.sunk | while | flops 280439424 | bytes 37360840 | solution.py:52
  345.6 33.9 %all-gather.18.cloned.1.call-done = bf16[1024,4096]{1,0:T(8,128)(2,1)} async-done(((bf16[32,4096]{1,0:T(8,128)(2,1)}), bf16[1024,4096]{1,0:T(8,128)(2,1)}) %all-gather.18.cloned.1.call-update) | async-done | bytes 8388624 | tf_op jit(solution)/shard_map/all_gather | solution.py:101
  384.3 73.8 %all-gather.20.cloned.1.call-done = bf16[4096,1024]{1,0:T(8,128)(2,1)} async-done(((bf16[128,1024]{1,0:T(8,128)(2,1)}), bf16[4096,1024]{1,0:T(8,128)(2,1)}) %all-gather.20.cloned.1.call-update) | async-done | bytes 8388624 | tf_op jit(solution)/shard_map/all_gather | solution.py:103
  458.1 7.1 fusion.90
  477.3 74.3 %all_gather.71 = f32[4096,16]{0,1:T(8,128)} all-gather(f32[128,16]{0,1:T(8,128)S(1)} %bitcast.191), channel_id=1, replica_groups=mesh['ctx'=16,'fsdp'=2] {'ctx','fsdp'}, dimensions={0}, use_global_device_ids=true | all-gather | bytes 270336 | tf_op jit(solution)/shard_map/all_gather | solution.py:246
  551.7 71.7 %all_gather.73 = f32[4096,16]{0,1:T(8,128)} all-gather(f32[128,16]{0,1:T(8,128)S(1)} %bitcast_reduce_fusion.1), channel_id=1, replica_groups=mesh['ctx'=16,'fsdp'=2] {'ctx','fsdp'}, dimensions={0}, use_global_device_ids=true | all-gather | bytes 270336 | tf_op jit(solution)/shard_map/all_gather | solution.py:247
  626.3 231.2 %while.31 = (s32[]{:T(128)}, f32[16,128,64]{1,2,0:T(8,128)}, f32[128,16,64]{0,2,1:T(8,128)}, f32[128,16,64]{0,2,1:T(8,128)}, s32[8]{0:T(128)S(1)}, /*index=5*/bf...) while((s32[]{:T(128)}, f32[16,128,64]{1,2,0:T(8,128)}, ...), condition=%wide.region_12.13_spmd.clone, body=%wide.region_11.12_spmd.clone.sunk | while | flops 959316608 | bytes 49864540 | solution.py:52
  644.8 6.2 fusion.169
  673.6 6.3 fusion.169
  689.9 5.2 fusion.167
  702.6 6.3 fusion.169
  731.5 6.3 fusion.169
  760.5 6.3 fusion.169
  789.4 6.3 fusion.169
  818.3 6.3 fusion.169
  847.2 6.3 fusion.169
  861.8 7.4 fusion.75
  870.6 9.0 fusion.71
  881.4 9.0 fusion.85
  891.1 6.1 fusion.54
  898.6 5.6 fusion.67
  904.2 41.1 %all-reduce.15 = (f32[1024]{0:T(1024)S(1)}, f32[1024]{0:T(1024)S(1)}, f32[2048]{0:T(1024)S(1)}, f32[1024]{0:T(1024)S(1)}, f32[1024]{0:T(1024)S(1)}, /*index=5*/f...) all-reduce(f32[1024]{0:T(1024)S(1)} %get-tuple-element.339, ...), channel_id=2, replica_groups=mesh['ctx'=16,'fsdp'=2] {'ctx','fsdp'}, use_global_device_ids=true, to_apply=%region_16.17.clone | all-reduce | flops 12288 | bytes 98304
  951.1 72.1 %reduce-scatter.5.cloned.1.call-done = f32[32,3072]{1,0:T(8,128)} async-done(((f32[1024,3072]{1,0:T(8,128)}), f32[32,3072]{1,0:T(8,128)}) %reduce-scatter.5.cloned.1.call-update) | async-done | bytes 393232 | tf_op jit(solution)/shard_map/reduce_scatter | solution.py:337
  1023.2 359.2 %reduce-scatter.9.cloned.1.call-done = f32[32,4096]{1,0:T(8,128)} async-done(((f32[1024,4096]{1,0:T(8,128)}), f32[32,4096]{1,0:T(8,128)}) %reduce-scatter.9.cloned.1.call-update) | async-done | bytes 524304 | tf_op jit(solution)/shard_map/reduce_scatter | solution.py:343
  1382.4 361.4 %reduce-scatter.11.cloned.1.call-done = f32[128,1024]{1,0:T(8,128)} async-done(((f32[4096,1024]{1,0:T(8,128)}), f32[128,1024]{1,0:T(8,128)}) %reduce-scatter.11.cloned.1.call-update) | async-done | bytes 524304 | tf_op jit(solution)/shard_map/reduce_scatter | solution.py:345
  (393 shorter events, 306.9 us)
Async XLA Ops:
  7.2 75.6 %all-gather.10.cloned.1.call-start = ((), (), s32[]{:S(2)}) async-start(), calls=%async_computation.4 | async-start | bytes 6488064 | tf_op jit(solution)/shard_map/all_gather | solution.py:95
  7.9 155.6 %all-gather.12.cloned.1.call-start = ((), (), s32[]{:S(2)}) async-start(), calls=%async_computation.5 | async-start | bytes 8650752 | tf_op jit(solution)/shard_map/all_gather | solution.py:172
  58.6 31.7 %copy-start.24 = (bf16[128]{0:T(256)(128)(2,1)S(1)}, bf16[128]{0:T(256)(128)(2,1)}, u32[]{:S(2)}) copy-start(bf16[128]{0:T(256)(128)(2,1)} %param.28) | copy-start | bytes 772
  87.6 155.3 %all-gather.14.cloned.1.call-start = ((), (), s32[]{:S(2)}) async-start(), calls=%async_computation.6 | async-start | bytes 8650752 | tf_op jit(solution)/shard_map/all_gather | solution.py:173
  88.4 68.8 %copy-start.15 = (bf16[128,1024]{1,0:T(8,128)(2,1)}, bf16[128,1024]{1,0:T(8,128)(2,1)S(1)}, u32[]{:S(2)}) copy-start(bf16[128,1024]{1,0:T(8,128)(2,1)S(1)} %get-tuple-element.429) | copy-start | bytes 786436
  88.5 254.7 %all-gather.16.cloned.1.call-start = ((), (), s32[]{:S(2)}) async-start(), calls=%async_computation.7 | async-start | bytes 2162688 | tf_op jit(solution)/shard_map/all_gather | solution.py:97
  89.0 290.5 %all-gather.18.cloned.1.call-start = ((), (), s32[]{:S(2)}) async-start(), calls=%async_computation.8 | async-start | bytes 8650752 | tf_op jit(solution)/shard_map/all_gather | solution.py:101
  89.6 368.5 %all-gather.20.cloned.1.call-start = ((), (), s32[]{:S(2)}) async-start(), calls=%async_computation.9 | async-start | bytes 8650752 | tf_op jit(solution)/shard_map/all_gather | solution.py:103
  90.2 536.0 %all-gather.22.cloned.1.call-start = ((), (), s32[]{:S(2)}) async-start(), calls=%async_computation.10 | async-start | bytes 8650752 | tf_op jit(solution)/shard_map/all_gather | solution.py:311
  157.2 469.0 %all-gather.24.cloned.1.call-start = ((), (), s32[]{:S(2)}) async-start(), calls=%async_computation.11 | async-start | bytes 8650752 | tf_op jit(solution)/shard_map/all_gather | solution.py:312
  254.2 88.9 %copy-start.4 = (bf16[128,1024]{1,0:T(8,128)(2,1)S(1)}, bf16[128,1024]{1,0:T(8,128)(2,1)}, u32[]{:S(2)}) copy-start(bf16[128,1024]{1,0:T(8,128)(2,1)} %param.18) | copy-start | bytes 786436
  342.3 37.2 %copy-start.13 = (bf16[16,128,64]{1,2,0:T(8,128)(2,1)}, bf16[16,128,64]{1,2,0:T(8,128)(2,1)S(1)}, u32[]{:S(2)}) copy-start(bf16[16,128,64]{1,2,0:T(8,128)(2,1)S(1)} %divide_convert_fusion) | copy-start | bytes 786436
  345.3 123.0 %copy-start.2 = (f32[128,1024]{1,0:T(8,128)}, f32[128,1024]{1,0:T(8,128)S(1)}, u32[]{:S(2)}) copy-start(f32[128,1024]{1,0:T(8,128)S(1)} %get-tuple-element.436) | copy-start | bytes 1572868
  379.5 78.6 %copy-start.16 = (bf16[128,1024]{1,0:T(8,128)(2,1)S(1)}, bf16[128,1024]{1,0:T(8,128)(2,1)}, u32[]{:S(2)}) copy-start(bf16[128,1024]{1,0:T(8,128)(2,1)} %param.31) | copy-start | bytes 786436
  384.3 80.9 %copy-start.6 = (f32[128,4096]{1,0:T(8,128)}, f32[128,4096]{1,0:T(8,128)S(1)}, u32[]{:S(2)}) copy-start(f32[128,4096]{1,0:T(8,128)S(1)} %convolution_add_fusion) | copy-start | bytes 6291460
  458.1 7.1 copy-start.1
  468.6 157.5 %copy-start.8 = (f32[128,1024]{1,0:T(8,128)}, f32[128,1024]{1,0:T(8,128)S(1)}, u32[]{:S(2)}) copy-start(f32[128,1024]{1,0:T(8,128)S(1)} %get-tuple-element.417) | copy-start | bytes 1572868
  468.6 154.8 %copy-start.14 = (bf16[16,128,64]{1,2,0:T(8,128)(2,1)S(1)}, bf16[16,128,64]{1,2,0:T(8,128)(2,1)}, u32[]{:S(2)}) copy-start(bf16[16,128,64]{1,2,0:T(8,128)(2,1)} %copy-done.13) | copy-start | bytes 786436
  470.4 480.7 %reduce-scatter.7.cloned.1.call-start = ((), (), s32[]{:S(2)}) async-start(), calls=%async_computation.13 | async-start | bytes 4325376 | tf_op jit(solution)/shard_map/reduce_scatter | solution.py:339
  626.2 397.0 %reduce-scatter.5.cloned.1.call-start = ((), (), s32[]{:S(2)}) async-start(), calls=%async_computation.12 | async-start | bytes 12976128 | tf_op jit(solution)/shard_map/reduce_scatter | solution.py:337
  644.8 6.2 copy-start.21
  673.6 6.3 copy-start.21
  702.6 6.3 copy-start.21
  731.5 6.3 copy-start.21
  760.5 6.3 copy-start.21
  789.4 6.3 copy-start.21
  818.3 6.3 copy-start.21
  847.2 6.3 copy-start.21
  869.3 513.1 %reduce-scatter.9.cloned.1.call-start = ((), (), s32[]{:S(2)}) async-start(), calls=%async_computation.14 | async-start | bytes 17301504 | tf_op jit(solution)/shard_map/reduce_scatter | solution.py:343
  879.7 864.1 %reduce-scatter.11.cloned.1.call-start = ((), (), s32[]{:S(2)}) async-start(), calls=%async_computation.15 | async-start | bytes 17301504 | tf_op jit(solution)/shard_map/reduce_scatter | solution.py:345
  891.1 7.6 copy-start.5
  898.6 51.4 %copy-start.9 = (f32[128,1024]{1,0:T(8,128)S(1)}, f32[128,1024]{1,0:T(8,128)}, u32[]{:S(2)}) copy-start(f32[128,1024]{1,0:T(8,128)} %copy-done.8) | copy-start | bytes 1572868
  (26 other events, 54.5 us)
Sparse Core Ops, SparseCore 0:
  10.9 71.9 all-gather.9
  87.7 75.7 all-gather.11
  167.1 75.6 all-gather.13
  245.7 54.9 all-gather.15
  303.5 75.9 all-gather.17
  382.3 75.7 all-gather.19
  461.1 77.8 all-gather.21
  542.0 77.0 all-gather.23
  626.3 141.8 reduce-scatter.6
  869.4 153.7 reduce-scatter.4
  1026.1 356.2 reduce-scatter.8
  1385.1 358.6 reduce-scatter.10
where the time goes:
time: 1760 us; the launch traced here: 1750 us
  waiting for transfers between devices  1000 us (57%)
  blocking collectives  296 us (17%)
  matrix products  268 us (15%)
  local copies, waits for them, and re-layouts  120 us (7%)
  other arithmetic  38.7 us (2%)
    reduce_scatter x1, waiting for transfers between devices, on_device(): lax.psum_scatter(grad_shrink_weight, ('ctx', 'fsdp'), scatter_dimension=0...  361 us
    reduce_scatter x1, waiting for transfers between devices, on_device(): lax.psum_scatter(grad_expand_weight, ('ctx', 'fsdp'), scatter_dimension=0...  359 us
    unnamed x2, blocking collectives  83.6 us
    dot_general x24, matrix products, masked_scores(): jnp.einsum('qhd,khd->hqk', query_part, key_part, preferred_element_type=j...  76.9 us
    all_gather x1, blocking collectives, on_device(): lax.all_gather(log_total, ('ctx', 'fsdp'), axis=0, tiled=True)  74.3 us
    all_gather x1, waiting for transfers between devices, on_device(): lax.all_gather(parameters[10], ('ctx', 'fsdp'), axis=0, tiled=True)  73.8 us
    reduce_scatter x1, waiting for transfers between devices, on_device(): lax.psum_scatter(grad_attend_weight, ('ctx', 'fsdp'), scatter_dimension=0...  72.1 us
    all_gather x1, blocking collectives, on_device(): lax.all_gather(row_delta, ('ctx', 'fsdp'), axis=0, tiled=True)  71.7 us
  transfers between devices with their start and end apart: 12, of which 8 were waited for; matrix products, arithmetic and copies ran while one was open for 23% of the time, Pallas kernels for 0%

commit v1 on v0

v1 whole, which is shorter than its diff:
```python
import math

import jax
import jax.numpy as jnp
from jax import lax
from jax.experimental import pallas as pl
from jax.experimental.pallas import tpu as pltpu
from jax.sharding import PartitionSpec as P

H = 16
G = 8
EPSILON = 1e-05
GELU_SCALE = 0.7978845608028654
GELU_CUBIC = 0.044715
LOG2E = 1.4426950408889634
MESH = pl.DeviceIdType.MESH
BF16 = jnp.bfloat16
F32 = jnp.float32


def position(fsdp):
    return lax.axis_index("ctx") * fsdp + lax.axis_index("fsdp")


class Wire:
    def __init__(self, n, fsdp, send, recv, local):
        self.n, self.fsdp = n, fsdp
        self.send, self.recv, self.local = send, recv, local
        self.me = position(fsdp)
        self.t, self.m = self.me // G, lax.rem(self.me, G)

    def where(self, device):
        return (device // self.fsdp, lax.rem(device, self.fsdp))

    def greet(self):
        barrier = pltpu.get_barrier_semaphore()

        def hello(step, carry):
            other = lax.rem(self.me + step, self.n)
            pl.semaphore_signal(barrier, inc=1, device_id=self.where(other), device_id_type=MESH)
            return carry

        lax.fori_loop(1, self.n, hello, 0)
        pl.semaphore_wait(barrier, self.n - 1)

    def put(self, lane, source, target, device):
        pltpu.make_async_remote_copy(
            src_ref=source,
            dst_ref=target,
            send_sem=self.send.at[lane],
            recv_sem=self.recv.at[lane],
            device_id=self.where(device),
            device_id_type=MESH,
        ).start()

    def keep(self, lane, source, target):
        pltpu.make_async_copy(source, target, self.local.at[lane]).start()

    def kept(self, lane, like):
        pltpu.make_async_copy(like, like, self.local.at[lane]).wait()

    def sent(self, lane, like):
        pltpu.make_async_copy(like, like, self.send.at[lane]).wait()

    def came(self, lane, like):
        pltpu.make_async_copy(like, like, self.recv.at[lane]).wait()

    def settle(self, lane, like):
        self.came(lane, like)
        self.sent(lane, like)

    def group(self, step):
        m = lax.rem(self.m + step, G)
        return m, self.t * G + m

    def column(self, step, groups):
        t = lax.rem(self.t + step, groups)
        return t, t * G + self.m


def exchange(body, name, number, n, fsdp, lanes, inputs, outs):
    def kernel(*refs):
        ins = refs[: len(inputs)]
        results = refs[len(inputs) : len(inputs) + len(outs)]
        wire = Wire(n, fsdp, *refs[len(inputs) + len(outs) :])
        wire.greet()
        body(wire, *ins, *results)

    kernel.__name__ = name
    return pl.pallas_call(
        kernel,
        out_shape=[jax.ShapeDtypeStruct(shape, kind) for shape, kind in outs],
        in_specs=[pl.BlockSpec(memory_space=pltpu.VMEM)] * len(inputs),
        out_specs=[pl.BlockSpec(memory_space=pl.ANY)] * len(outs),
        scratch_shapes=[pltpu.SemaphoreType.DMA((lanes,))] * 3,
        compiler_params=pltpu.CompilerParams(collective_id=number, has_side_effects=True),
        name=name,
    )(*inputs)


def loop(low, high, step):
    def turn(index, carry):
        step(index)
        return carry

    lax.fori_loop(low, high, turn, 0)


def normalize(inputs):
    centred = inputs - jnp.mean(inputs, axis=1, keepdims=True)
    inverse = lax.rsqrt(jnp.mean(centred * centred, axis=1, keepdims=True) + EPSILON)
    return centred * inverse, inverse


def normalize_back(grad_norm, scaled, inverse, gain_row):
    grad_scaled = grad_norm * gain_row
    mean_one = jnp.mean(grad_scaled, axis=1, keepdims=True)
    mean_two = jnp.mean(grad_scaled * scaled, axis=1, keepdims=True)
    return inverse * (grad_scaled - mean_one - scaled * mean_two)


def gelu_pair(pre_act):
    tangent = jnp.tanh(GELU_SCALE * (pre_act + GELU_CUBIC * pre_act * pre_act * pre_act))
    activated = 0.5 * pre_act * (1.0 + tangent)
    derivative = 0.5 * (1.0 + tangent) + 0.5 * pre_act * (1.0 - tangent * tangent) * GELU_SCALE * (
        1.0 + 3.0 * GELU_CUBIC * pre_act * pre_act
    )
    return (activated, derivative)


def dot(left, right, left_dim, right_dim):
    return lax.dot_general(
        left, right, (((left_dim,), (right_dim,)), ((), ())), preferred_element_type=F32
    )


def tiles_of(queries, keys, parts):
    wide = min(256, queries)
    deep = min(512, wide * parts)
    return wide, deep, wide * parts // deep


def query_places(tile, wide, parts, part):
    column = lax.broadcasted_iota(jnp.int32, (1, wide), 1)
    block = tile * (wide // 128) + column // 128
    return (block * parts + part) * 128 + lax.rem(column, 128)


def attend(groups, fsdp, parts, query_t, pair_t):
    width, queries = query_t.shape
    keys = pair_t.shape[2]
    wide, deep, band = tiles_of(queries, keys, parts)
    factor = LOG2E / math.sqrt(width)

    def kernel(query_ref, pair_ref, out_ref, total_ref, key_ref):
        tile = pl.program_id(0)
        part = lax.rem(position(fsdp) // G, parts)

        @pl.when(tile == 0)
        def _():
            def turn(j):
                at = pl.ds(pl.multiple_of(j * deep, deep), deep)
                key_ref[at, :] = pair_ref[0, :, at].T

            loop(0, keys // deep, turn)

        query = query_ref[...]
        places = query_places(tile, wide, parts, part)

        def step(j, carry, masked):
            best, total, summed = carry
            at = pl.ds(pl.multiple_of(j * deep, deep), deep)
            scores = dot(key_ref[at, :], query, 1, 0)
            if masked:
                key_places = j * deep + lax.broadcasted_iota(jnp.int32, (deep, wide), 0)
                scores = jnp.where(key_places <= places, scores, -1e30)
            higher = jnp.maximum(best, jnp.max(scores, axis=0, keepdims=True))
            weights = jnp.exp2((scores - higher) * factor)
            shrunk = jnp.exp2((best - higher) * factor)
            total = total * shrunk + jnp.sum(weights, axis=0, keepdims=True)
            summed = summed * shrunk + dot(pair_ref[1, :, at], weights.astype(BF16), 1, 0)
            return higher, total, summed

        carry = (
            jnp.full((1, wide), -1e30, F32),
            jnp.zeros((1, wide), F32),
            jnp.zeros((width, wide), F32),
        )
        carry = lax.fori_loop(0, tile * band, lambda j, c: step(j, c, False), carry)
        for extra in range(band):
            carry = step(tile * band + extra, carry, True)
        best, total, summed = carry
        out_ref[...] = (summed / total).astype(BF16)
        total_ref[...] = best * factor + jnp.log2(total)

    across = pl.BlockSpec((width, wide), lambda i: (0, i))
    return pl.pallas_call(
        kernel,
        grid=(queries // wide,),
        out_shape=[
            jax.ShapeDtypeStruct((width, queries), BF16),
            jax.ShapeDtypeStruct((1, queries), F32),
        ],
        in_specs=[across, pl.BlockSpec((2, width, keys), lambda i: (0, 0, 0))],
        out_specs=[across, pl.BlockSpec((1, wide), lambda i: (0, i))],
        scratch_shapes=[pltpu.VMEM((keys, width), BF16)],
        name="attend",
    )(query_t, pair_t)


def attend_back(groups, fsdp, parts, query_t, pair_t, grad_t, out_t, total):
    width, queries = query_t.shape
    keys = pair_t.shape[2]
    wide, deep, band = tiles_of(queries, keys, parts)
    scale = 1.0 / math.sqrt(width)
    factor = LOG2E * scale

    def kernel(
        query_ref, pair_ref, grad_ref, out_ref, total_ref, dq_ref, dpair_ref, key_ref, value_ref, dkey_ref, dvalue_ref
    ):
        tile = pl.program_id(0)
        part = lax.rem(position(fsdp) // G, parts)

        @pl.when(tile == 0)
        def _():
            def turn(j):
                at = pl.ds(pl.multiple_of(j * deep, deep), deep)
                key_ref[at, :] = pair_ref[0, :, at].T
                value_ref[at, :] = pair_ref[1, :, at].T
                dkey_ref[at, :] = jnp.zeros((deep, width), F32)
                dvalue_ref[at, :] = jnp.zeros((deep, width), F32)

            loop(0, keys // deep, turn)

        query, grad = query_ref[...], grad_ref[...]
        query_rows, grad_rows = query.T, grad.T
        lse = total_ref[...]
        delta = jnp.sum(grad.astype(F32) * out_ref[...].astype(F32), axis=0, keepdims=True)
        places = query_places(tile, wide, parts, part)

        def step(j, summed, masked):
            at = pl.ds(pl.multiple_of(j * deep, deep), deep)
            scores = dot(key_ref[at, :], query, 1, 0) * factor
            if masked:
                key_places = j * deep + lax.broadcasted_iota(jnp.int32, (deep, wide), 0)
                scores = jnp.where(key_places <= places, scores, -1e30)
            probs = jnp.exp2(scores - lse)
            dvalue_ref[at, :] += dot(probs.astype(BF16), grad_rows, 1, 0)
            grad_probs = dot(value_ref[at, :], grad, 1, 0)
            grad_scores = (probs * (grad_probs - delta) * scale).astype(BF16)
            dkey_ref[at, :] += dot(grad_scores, query_rows, 1, 0)
            return summed + dot(pair_ref[0, :, at], grad_scores, 1, 0)

        summed = jnp.zeros((width, wide), F32)
        summed = lax.fori_loop(0, tile * band, lambda j, c: step(j, c, False), summed)
        for extra in range(band):
            summed = step(tile * band + extra, summed, True)
        dq_ref[...] = summed.astype(BF16)

        @pl.when(tile == pl.num_programs(0) - 1)
        def _():
            def turn(j):
                at = pl.ds(pl.multiple_of(j * deep, deep), deep)
                dpair_ref[0, :, at] = dkey_ref[at, :].T.astype(BF16)
                dpair_ref[1, :, at] = dvalue_ref[at, :].T.astype(BF16)

            loop(0, keys // deep, turn)

    across = pl.BlockSpec((width, wide), lambda i: (0, i))
    line = pl.BlockSpec((1, wide), lambda i: (0, i))
    whole = pl.BlockSpec((2, width, keys), lambda i: (0, 0, 0))
    return pl.pallas_call(
        kernel,
        grid=(queries // wide,),
        out_shape=[
            jax.ShapeDtypeStruct((width, queries), BF16),
            jax.ShapeDtypeStruct((2, width, keys), BF16),
        ],
        in_specs=[across, whole, across, across, line],
        out_specs=[across, whole],
        scratch_shapes=[
            pltpu.VMEM((keys, width), BF16),
            pltpu.VMEM((keys, width), BF16),
            pltpu.VMEM((keys, width), F32),
            pltpu.VMEM((keys, width), F32),
        ],
        name="attend_back",
    )(query_t, pair_t, grad_t, out_t, total)


def layer(n, fsdp):
    groups = n // G
    parts = groups // 2

    def on_device(
        residual_in,
        first_gain,
        first_shift,
        attend_weight,
        attend_bias,
        merge_weight,
        merge_bias,
        second_gain,
        second_shift,
        expand_weight,
        expand_bias,
        shrink_weight,
        shrink_bias,
        cotangent,
    ):
        rows, width = residual_in.shape
        depth = width // n
        hidden_rows = shrink_weight.shape[0]
        hidden_units = expand_weight.shape[1]
        slice_width = width // G
        slice_units = hidden_units // G
        head = width // H
        group_rows = rows * G
        tokens = rows * n
        queries = tokens // parts
        per_group = G // parts
        me = position(fsdp)
        member = lax.rem(me, G)

        small = (first_gain, first_shift, attend_bias, merge_bias, second_gain, second_shift, expand_bias, shrink_bias)
        sizes = [s.shape[0] for s in small]
        packed_rows = -(-sum(sizes) // 2048) * 16
        packed = jnp.pad(jnp.concatenate(small), (0, packed_rows * 128 - sum(sizes))).reshape(packed_rows, 128)

        def gather_first(wire, x, attend, merge, vec, x_all, attend_all, merge_all, vec_all):
            me, t, m = wire.me, wire.t, wire.m

            def to_group(step):
                _, device = wire.group(step)
                wire.put(0, x, x_all.at[m], device)

            def to_all(step):
                device = lax.rem(me + step, n)
                other = lax.rem(device, G)
                for p in range(3):
                    columns = pl.ds(pl.multiple_of(p * width + other * slice_width, 128), slice_width)
                    wire.put(1, attend.at[:, columns], attend_all.at[me, :, pl.ds(p * slice_width, slice_width)], device)
                wire.put(3, vec, vec_all.at[me], device)

            def to_column(step):
                _, device = wire.column(step, groups)
                wire.put(2, merge, merge_all.at[t], device)

            loop(1, G, to_group)
            loop(1, n, to_all)
            loop(1, groups, to_column)
            wire.keep(0, x, x_all.at[m])
            for p in range(3):
                columns = pl.ds(pl.multiple_of(p * width + m * slice_width, 128), slice_width)
                wire.keep(1, attend.at[:, columns], attend_all.at[me, :, pl.ds(p * slice_width, slice_width)])
            wire.keep(2, merge, merge_all.at[t])
            wire.keep(3, vec, vec_all.at[me])
            wire.kept(0, x_all.at[0])
            wire.kept(1, attend_all.at[0])
            wire.kept(2, merge_all.at[0])
            wire.kept(3, vec_all.at[0])
            wire.settle(0, x_all.at[pl.ds(0, G - 1)])
            wire.settle(1, attend_all.at[pl.ds(0, n - 1)])
            wire.settle(2, merge_all.at[pl.ds(0, groups - 1)])
            wire.settle(3, vec_all.at[pl.ds(0, n - 1)])

        x_all, attend_all, merge_all, vec_all = exchange(
            gather_first,
            "gather_first",
            0,
            n,
            fsdp,
            4,
            (residual_in, attend_weight, merge_weight, packed),
            (
                ((G, rows, width), BF16),
                ((n, depth, 3 * slice_width), BF16),
                ((groups, depth, width), BF16),
                ((n, packed_rows, 128), BF16),
            ),
        )
        flat = vec_all.reshape(n, packed_rows * 128)
        spots = [sum(sizes[:k]) for k in range(len(sizes))]
        gain_one, shift_one, attend_shift, merge_shift, gain_two, shift_two, expand_shift, shrink_shift = (
            flat[:, spot : spot + size].reshape(-1).astype(F32) for spot, size in zip(spots, sizes)
        )
        attend_slice = attend_all.reshape(width, 3 * slice_width)

        scaled_group, _ = normalize(x_all.reshape(group_rows, width).astype(F32))
        input_one = (scaled_group * gain_one + shift_one).astype(BF16)
        bias_mine = jnp.concatenate(
            [
                lax.dynamic_slice_in_dim(attend_shift, member * slice_width, slice_width),
                jnp.zeros((slice_width,), F32),
                lax.dynamic_slice_in_dim(attend_shift, width + member * slice_width, slice_width),
            ]
        )
        projected = (dot(attend_slice, input_one, 0, 1) + bias_mine[:, None]).astype(BF16)
        projected = projected.reshape(3, 2, head, group_rows)

        def spread_heads(wire, qkv, merge, pair, query, merge_full):
            t, m = wire.t, wire.m

            def to_column(step, own=False):
                other, device = wire.column(step, groups)
                which, part = other // parts, lax.rem(other, parts)
                move = (lambda lane, s, d: wire.keep(lane, s, d)) if own else (lambda lane, s, d: wire.put(lane, s, d, device))
                mine = pl.ds(pl.multiple_of(t * group_rows, 128), group_rows)
                move(0, qkv.at[1, which], pair.at[0, :, mine])
                move(0, qkv.at[2, which], pair.at[1, :, mine])
                for i in range(per_group):
                    source = pl.ds(pl.multiple_of((part + i * parts) * rows, 128), rows)
                    target = pl.ds(pl.multiple_of((t * per_group + i) * rows, 128), rows)
                    move(1, qkv.at[0, which, :, source], query.at[:, target])

            def to_group(step):
                _, device = wire.group(step)
                wire.put(2, merge, merge_full.at[:, m], device)

            loop(1, groups, to_column)
            loop(1, G, to_group)
            to_column(0, own=True)
            wire.keep(2, merge, merge_full.at[:, m])
            wire.kept(0, pair.at[:, :, pl.ds(0, group_rows)])
            wire.kept(1, query.at[:, pl.ds(0, per_group * rows)])
            wire.kept(2, merge_full.at[:, 0])
            wire.settle(0, pair.at[:, :, pl.ds(0, tokens - group_rows)])
            wire.settle(1, query.at[:, pl.ds(0, queries - per_group * rows)])
            wire.settle(2, merge_full.at[:, pl.ds(0, G - 1)])

        pair_t, query_t, merge_full = exchange(
            spread_heads,
            "spread_heads",
            1,
            n,
            fsdp,
            3,
            (projected, merge_all),
            (((2, head, tokens), BF16), ((head, queries), BF16), ((groups, G, depth, width), BF16)),
        )
        merge_full = merge_full.reshape(width, width)
        out_t, log_total = attend(groups, fsdp, parts, query_t, pair_t)

        def send_attended(wire, out, attended):
            me, part = wire.me, lax.rem(wire.t, parts)
            place = pl.ds(pl.multiple_of((2 * wire.m + wire.t // parts) * head, head), head)

            def to_owner(k):
                device = k * parts + part
                source = out.at[:, pl.ds(pl.multiple_of(k * rows, 128), rows)]

                @pl.when(device != me)
                def _():
                    wire.put(0, source, attended.at[place, :], device)

                @pl.when(device == me)
                def _():
                    wire.keep(0, source, attended.at[place, :])

            loop(0, n // parts, to_owner)
            mine = lax.rem(me, parts) == part

            @pl.when(mine)
            def _():
                wire.kept(0, attended.at[pl.ds(0, head), :])
                wire.came(0, attended.at[pl.ds(0, width - head), :])
                wire.sent(0, out.at[:, pl.ds(0, queries - rows)])

            @pl.when(jnp.logical_not(mine))
            def _():
                wire.came(0, attended)
                wire.sent(0, out)

        (attended_t,) = exchange(send_attended, "send_attended", 2, n, fsdp, 1, (out_t,), (((width, rows), BF16),))

        block_in = residual_in.astype(F32)
        hidden = block_in + (dot(attended_t, merge_full, 0, 0) + merge_shift)
        scaled_two, inverse_two = normalize(hidden)
        input_two = (scaled_two * gain_two + shift_two).astype(BF16)

        def gather_second(wire, normed, cot, expand, shrink, normed_all, cot_all, expand_all, shrink_all):
            me, t, m = wire.me, wire.t, wire.m
            user = me // groups
            slot = lax.rem(me, groups)

            def to_group(step):
                _, device = wire.group(step)
                wire.put(0, normed, normed_all.at[m], device)

            def to_all(step):
                device = lax.rem(me + step, n)
                columns = pl.ds(pl.multiple_of(lax.rem(device, G) * slice_units, 128), slice_units)
                wire.put(2, expand.at[:, columns], expand_all.at[me], device)

            def to_users(step):
                other = lax.rem(t + step, groups)
                device = other * G + user

                @pl.when(device != me)
                def _():
                    wire.put(3, shrink, shrink_all.at[slot], device)

                @pl.when(device == me)
                def _():
                    wire.keep(3, shrink, shrink_all.at[slot])

            def cot_to_group(step):
                _, device = wire.group(step)
                wire.put(1, cot, cot_all.at[m], device)

            loop(1, G, to_group)
            loop(0, groups, to_users)
            loop(1, n, to_all)
            loop(1, G, cot_to_group)
            wire.keep(0, normed, normed_all.at[m])
            wire.keep(1, cot, cot_all.at[m])
            wire.keep(2, expand.at[:, pl.ds(pl.multiple_of(m * slice_units, 128), slice_units)], expand_all.at[me])
            wire.kept(0, normed_all.at[0])
            wire.kept(1, cot_all.at[0])
            wire.kept(2, expand_all.at[0])
            wire.settle(0, normed_all.at[pl.ds(0, G - 1)])
            wire.settle(1, cot_all.at[pl.ds(0, G - 1)])
            wire.settle(2, expand_all.at[pl.ds(0, n - 1)])

            @pl.when(user == m)
            def _():
                wire.kept(3, shrink_all.at[0])
                wire.settle(3, shrink_all.at[pl.ds(0, groups - 1)])

            @pl.when(user != m)
            def _():
                wire.settle(3, shrink_all)

        normed_all, cot_all, expand_all, shrink_all = exchange(
            gather_second,
            "gather_second",
            3,
            n,
            fsdp,
            4,
            (input_two, cotangent, expand_weight, shrink_weight),
            (
                ((G, rows, width), BF16),
                ((G, rows, width), BF16),
                ((n, depth, slice_units), BF16),
                ((groups, hidden_rows, width), BF16),
            ),
        )
        group_two = normed_all.reshape(group_rows, width)
        group_cot = cot_all.reshape(group_rows, width)
        expand_slice = expand_all.reshape(width, slice_units)
        shrink_slice = shrink_all.reshape(slice_units, width)
        shift_units = lax.dynamic_slice_in_dim(expand_shift, member * slice_units, slice_units)
        activated, derivative = gelu_pair(dot(group_two, expand_slice, 1, 0) + shift_units)
        act_input = activated.astype(BF16)
        shrunk_part = dot(act_input, shrink_slice, 1, 0).astype(BF16)
        grad_shrink_part = dot(act_input, group_cot, 0, 0).astype(BF16)
        grad_pre = dot(group_cot, shrink_slice, 1, 1) * derivative
        grad_expand_shift = jnp.sum(grad_pre, axis=0)
        grad_pre_input = grad_pre.astype(BF16)
        grad_expand_part = dot(group_two, grad_pre_input, 0, 0).astype(BF16)
        grad_two_part = dot(grad_pre_input, expand_slice, 1, 1).astype(BF16)

        def scatter_second(wire, two, shrunk, expand, shrink, two_all, shrunk_all, expand_all, shrink_all):
            me, t, m = wire.me, wire.t, wire.m
            columns = pl.ds(pl.multiple_of(m * slice_units, 128), slice_units)

            def to_group(step):
                other, device = wire.group(step)
                wire.put(0, two.at[other], two_all.at[m], device)

            def shrunk_to_group(step):
                other, device = wire.group(step)
                wire.put(1, shrunk.at[other], shrunk_all.at[m], device)

            def to_all(step):
                device = lax.rem(me + step, n)
                wire.put(2, expand.at[device], expand_all.at[t, :, columns], device)

            def to_owners(slot):
                device = m * groups + slot

                @pl.when(device != me)
                def _():
                    wire.put(3, shrink.at[slot], shrink_all.at[t], device)

                @pl.when(device == me)
                def _():
                    wire.keep(3, shrink.at[slot], shrink_all.at[t])

            loop(1, G, to_group)
            loop(0, groups, to_owners)
            loop(1, n, to_all)
            loop(1, G, shrunk_to_group)
            wire.keep(0, two.at[m], two_all.at[m])
            wire.keep(1, shrunk.at[m], shrunk_all.at[m])
            wire.keep(2, expand.at[me], expand_all.at[t, :, columns])
            wire.kept(0, two_all.at[0])
            wire.kept(1, shrunk_all.at[0])
            wire.kept(2, expand.at[0])
            wire.settle(0, two_all.at[pl.ds(0, G - 1)])
            wire.settle(1, shrunk_all.at[pl.ds(0, G - 1)])
            wire.settle(2, expand.at[pl.ds(0, n - 1)])

            @pl.when(me // groups == m)
            def _():
                wire.kept(3, shrink_all.at[0])
                wire.settle(3, shrink_all.at[pl.ds(0, groups - 1)])

            @pl.when(me // groups != m)
            def _():
                wire.settle(3, shrink_all)

        two_parts, shrunk_parts, expand_parts, shrink_parts = exchange(
            scatter_second,
            "scatter_second",
            4,
            n,
            fsdp,
            4,
            (
                grad_two_part.reshape(G, rows, width),
                shrunk_part.reshape(G, rows, width),
                grad_expand_part.reshape(n, depth, slice_units),
                grad_shrink_part.reshape(groups, hidden_rows, width),
            ),
            (
                ((G, rows, width), BF16),
                ((G, rows, width), BF16),
                ((groups, depth, hidden_units), BF16),
                ((groups, hidden_rows, width), BF16),
            ),
        )
        residual_out = (hidden + jnp.sum(shrunk_parts.astype(F32), axis=0) + shrink_shift).astype(BF16)
        grad_expand_weight = jnp.sum(expand_parts.astype(F32), axis=0)
        grad_shrink_weight = jnp.sum(shrink_parts.astype(F32), axis=0)

        grad_top = cotangent.astype(F32)
        grad_shrink_shift = jnp.sum(grad_top, axis=0)
        grad_two = jnp.sum(two_parts.astype(F32), axis=0)
        grad_gain_two = jnp.sum(grad_two * scaled_two, axis=0)
        grad_shift_two = jnp.sum(grad_two, axis=0)
        grad_hidden = grad_top + normalize_back(grad_two, scaled_two, inverse_two, gain_two)
        grad_merge_shift = jnp.sum(grad_hidden, axis=0)
        grad_hidden_input = grad_hidden.astype(BF16)
        grad_attended_t = dot(merge_full, grad_hidden_input, 1, 1).astype(BF16)

        def send_grad(wire, grad, grad_out):
            me = wire.me
            part, place = lax.rem(me, parts), pl.ds(pl.multiple_of(me // parts * rows, 128), rows)

            def to_head(h):
                device = (lax.rem(h, 2) * parts + part) * G + h // 2
                source = grad.at[pl.ds(pl.multiple_of(h * head, head), head), :]

                @pl.when(device != me)
                def _():
                    wire.put(0, source, grad_out.at[:, place], device)

                @pl.when(device == me)
                def _():
                    wire.keep(0, source, grad_out.at[:, place])

            loop(0, H, to_head)
            mine = lax.rem(wire.t, parts) == part

            @pl.when(mine)
            def _():
                wire.kept(0, grad.at[pl.ds(0, head), :])
                wire.came(0, grad_out.at[:, pl.ds(0, queries - rows)])
                wire.sent(0, grad.at[pl.ds(0, width - head), :])

            @pl.when(jnp.logical_not(mine))
            def _():
                wire.came(0, grad_out)
                wire.sent(0, grad)

        (grad_t,) = exchange(send_grad, "send_grad", 5, n, fsdp, 1, (grad_attended_t,), (((head, queries), BF16),))
        grad_query_t, grad_pair_t = attend_back(groups, fsdp, parts, query_t, pair_t, grad_t, out_t, log_total)

        def return_heads(wire, dq, dpair, grad, att, dq_all, dpair_all, grad_all, att_all):
            t, m = wire.t, wire.m
            which, part = t // parts, lax.rem(t, parts)

            def to_column(step, own=False):
                other, device = wire.column(step, groups)
                move = (lambda lane, s, d: wire.keep(lane, s, d)) if own else (lambda lane, s, d: wire.put(lane, s, d, device))
                theirs = pl.ds(pl.multiple_of(other * group_rows, 128), group_rows)
                move(0, dpair.at[:, :, theirs], dpair_all.at[part, which])
                for i in range(per_group):
                    source = pl.ds(pl.multiple_of((other * per_group + i) * rows, 128), rows)
                    target = pl.ds(pl.multiple_of((part + i * parts) * rows, 128), rows)
                    move(1, dq.at[:, source], dq_all.at[which, :, target])

            def to_group(step):
                other, device = wire.group(step)
                wire.put(2, grad, grad_all.at[m], device)
                wire.put(
                    3,
                    att.at[pl.ds(pl.multiple_of(other * slice_width, 128), slice_width), :],
                    att_all.at[:, pl.ds(pl.multiple_of(m * rows, 128), rows)],
                    device,
                )

            loop(1, groups, to_column)
            loop(1, G, to_group)
            to_column(0, own=True)
            wire.keep(2, grad, grad_all.at[m])
            wire.keep(
                3,
                att.at[pl.ds(pl.multiple_of(m * slice_width, 128), slice_width), :],
                att_all.at[:, pl.ds(pl.multiple_of(m * rows, 128), rows)],
            )
            wire.kept(0, dpair.at[:, :, pl.ds(0, group_rows)])
            wire.kept(1, dq.at[:, pl.ds(0, per_group * rows)])
            wire.kept(2, grad_all.at[0])
            wire.kept(3, att_all.at[:, pl.ds(0, rows)])
            wire.settle(0, dpair.at[:, :, pl.ds(0, tokens - group_rows)])
            wire.settle(1, dq.at[:, pl.ds(0, queries - per_group * rows)])
            wire.settle(2, grad_all.at[pl.ds(0, G - 1)])
            wire.settle(3, att_all.at[:, pl.ds(0, group_rows - rows)])

        dq_all, dpair_all, grad_all, att_all = exchange(
            return_heads,
            "return_heads",
            6,
            n,
            fsdp,
            4,
            (grad_query_t, grad_pair_t, grad_hidden_input, attended_t),
            (
                ((2, head, group_rows), BF16),
                ((parts, 2, 2, head, group_rows), BF16),
                ((G, rows, width), BF16),
                ((slice_width, group_rows), BF16),
            ),
        )
        grad_pair = jnp.sum(dpair_all.astype(F32), axis=0)
        grad_projected = jnp.concatenate(
            [
                dq_all.astype(F32).reshape(slice_width, group_rows),
                grad_pair[:, 0].reshape(slice_width, group_rows),
                grad_pair[:, 1].reshape(slice_width, group_rows),
            ],
            axis=0,
        )
        grad_shift_mine = jnp.sum(grad_projected, axis=1)
        grad_projected = grad_projected.astype(BF16)
        grad_attend_part = dot(input_one, grad_projected, 0, 1).astype(BF16)
        grad_one_part = dot(grad_projected, attend_slice, 0, 1)
        grad_gain_one = jnp.sum(grad_one_part * scaled_group, axis=0)
        grad_shift_one = jnp.sum(grad_one_part, axis=0)
        grad_merge_part = dot(att_all, grad_all.reshape(group_rows, width), 1, 0).astype(BF16)

        grad_attend_shift = jnp.zeros((2 * width,), F32)
        grad_attend_shift = lax.dynamic_update_slice_in_dim(
            grad_attend_shift, grad_shift_mine[:slice_width], member * slice_width, 0
        )
        grad_attend_shift = lax.dynamic_update_slice_in_dim(
            grad_attend_shift, grad_shift_mine[2 * slice_width :], width + member * slice_width, 0
        )
        grad_expand_all = lax.dynamic_update_slice_in_dim(
            jnp.zeros((hidden_units,), F32), grad_expand_shift, member * slice_units, 0
        )
        grads = (
            grad_gain_one,
            grad_shift_one,
            grad_attend_shift,
            grad_merge_shift,
            grad_gain_two,
            grad_shift_two,
            grad_expand_all,
            grad_shrink_shift,
        )
        total_size = sum(sizes)
        vec_rows = -(-total_size // 1024) * 8
        packed_grads = jnp.pad(
            jnp.concatenate([g.reshape(n, -1) for g in grads], axis=1), ((0, 0), (0, vec_rows * 128 - total_size))
        ).reshape(n, vec_rows, 128)

        def scatter_first(wire, one, attend, merge, vec, one_all, attend_all, merge_all, vec_all):
            me, t, m = wire.me, wire.t, wire.m

            def to_group(step):
                other, device = wire.group(step)
                wire.put(0, one.at[other], one_all.at[m], device)

            def attend_to(device, move):
                for p in range(3):
                    columns = pl.ds(pl.multiple_of(p * width + m * slice_width, 128), slice_width)
                    move(1, attend.at[device, :, pl.ds(p * slice_width, slice_width)], attend_all.at[t, :, columns])

            def to_all(step):
                device = lax.rem(me + step, n)
                attend_to(device, lambda lane, s, d: wire.put(lane, s, d, device))
                wire.put(3, vec.at[device], vec_all.at[me], device)

            def to_owners(slot):
                device = m * groups + slot

                @pl.when(device != me)
                def _():
                    wire.put(2, merge.at[slot], merge_all.at[t], device)

                @pl.when(device == me)
                def _():
                    wire.keep(2, merge.at[slot], merge_all.at[t])

            loop(1, G, to_group)
            loop(1, n, to_all)
            loop(0, groups, to_owners)
            wire.keep(0, one.at[m], one_all.at[m])
            attend_to(me, wire.keep)
            wire.keep(3, vec.at[me], vec_all.at[me])
            wire.kept(0, one_all.at[0])
            wire.kept(1, attend.at[0])
            wire.kept(3, vec_all.at[0])
            wire.settle(0, one_all.at[pl.ds(0, G - 1)])
            wire.settle(1, attend.at[pl.ds(0, n - 1)])
            wire.settle(3, vec_all.at[pl.ds(0, n - 1)])

            @pl.when(me // groups == m)
            def _():
                wire.kept(2, merge_all.at[0])
                wire.settle(2, merge_all.at[pl.ds(0, groups - 1)])

            @pl.when(me // groups != m)
            def _():
                wire.settle(2, merge_all)

        one_parts, attend_parts, merge_parts, vec_parts = exchange(
            scatter_first,
            "scatter_first",
            7,
            n,
            fsdp,
            4,
            (
                grad_one_part.astype(BF16).reshape(G, rows, width),
                grad_attend_part.reshape(n, depth, 3 * slice_width),
                grad_merge_part.reshape(groups, depth, width),
                packed_grads,
            ),
            (
                ((G, rows, width), BF16),
                ((groups, depth, 3 * width), BF16),
                ((groups, depth, width), BF16),
                ((n, vec_rows, 128), F32),
            ),
        )
        grad_one = jnp.sum(one_parts.astype(F32), axis=0)
        scaled_one, inverse_one = normalize(block_in)
        input_grad = grad_hidden + normalize_back(grad_one, scaled_one, inverse_one, gain_one)
        grad_attend_weight = jnp.sum(attend_parts.astype(F32), axis=0)
        grad_merge_weight = jnp.sum(merge_parts.astype(F32), axis=0)
        vec_sums = jnp.sum(vec_parts, axis=0).reshape(-1)
        (g_gain_one, g_shift_one, g_attend_bias, g_merge_bias, g_gain_two, g_shift_two, g_expand_bias, g_shrink_bias) = (
            vec_sums[spot : spot + size] for spot, size in zip(spots, sizes)
        )
        return (
            residual_out,
            input_grad,
            g_gain_one,
            g_shift_one,
            grad_attend_weight,
            g_attend_bias,
            grad_merge_weight,
            g_merge_bias,
            g_gain_two,
            g_shift_two,
            grad_expand_weight,
            g_expand_bias,
            grad_shrink_weight,
            g_shrink_bias,
        )

    return on_device


def solution(mesh):
    rows, line = P(("ctx", "fsdp"), None), P(("ctx", "fsdp"))
    n, fsdp = mesh.shape["ctx"] * mesh.shape["fsdp"], mesh.shape["fsdp"]
    return jax.shard_map(
        layer(n, fsdp),
        mesh=mesh,
        in_specs=(rows, line, line, rows, line, rows, line, line, line, rows, line, rows, line, rows),
        out_specs=(rows, rows, line, line, rows, line, rows, line, line, line, rows, line, rows, line),
        check_vma=False,
    )
```

time: 1760 us -> 475 us (0.27)
  waiting for transfers between devices: 1000 us -> 0 us
  Pallas kernels: 0 us -> 405 us
  blocking collectives: 296 us -> 0 us
  matrix products: 268 us -> 35.2 us
  local copies, waits for them, and re-layouts: 120 us -> 13.2 us
  other arithmetic: 38.7 us -> 20.4 us
    reduce_scatter x4 -> x0, waiting for transfers between devices: 793 us -> none  [the longest x1 361 us: on_device(): lax.psum_scatter(grad_shrink_weight, ('ctx', 'fsdp'), scatter_dimension=0...]
    pallas_call x0 -> x10, Pallas kernels: none -> 405 us  [the longest x8 360 us: exchange(): pl.pallas_call(kernel, out_shape=[jax.ShapeDtypeStruct(shape, kind) for s...]
    dot_general x68 -> x12, matrix products: 268 us -> 35.2 us  [dot(): lax.dot_general(left, right, (((left_dim,), (right_dim,)), ((), ())), pre...]
    all_gather x3 -> x0, blocking collectives: 213 us -> none  [the longest x1 74.3 us: on_device(): lax.all_gather(log_total, ('ctx', 'fsdp'), axis=0, tiled=True)]
    all_gather x8 -> x0, waiting for transfers between devices: 206 us -> none  [the longest x1 73.8 us: on_device(): lax.all_gather(parameters[10], ('ctx', 'fsdp'), axis=0, tiled=True)]
    unnamed x2 -> x0, blocking collectives: 83.6 us -> none
    dynamic_slice x56 -> x1, local copies, waits for them, and re-layouts: 58.7 us -> 0.08 us  [on_device(): lax.dynamic_slice_in_dim(attend_shift, member * slice_width, slice_width)]
    unnamed x68 -> x46, local copies, waits for them, and re-layouts: 37.5 us -> 3.75 us
  transfers between devices with their start and end apart: 12 -> 0, of which waited for: 8 -> 0; matrix products, arithmetic and copies ran while one was open for 23% -> 0% of each run, Pallas kernels for 0% -> 0%
where the time goes in v1:
time: 475 us
  Pallas kernels  405 us (85%)
  matrix products  35.2 us (7%)
  other arithmetic  20.4 us (4%)
  local copies, waits for them, and re-layouts  13.2 us (3%)
    pallas_call x8, Pallas kernels, exchange(): pl.pallas_call(kernel, out_shape=[jax.ShapeDtypeStruct(shape, kind) for s...  360 us
    dot_general x12, matrix products, dot(): lax.dot_general(left, right, (((left_dim,), (right_dim,)), ((), ())), pre...  35.2 us
    pallas_call x1, Pallas kernels, attend_back(): pl.pallas_call(kernel, grid=(queries // wide,), out_shape=[jax.ShapeDtype...  24.4 us
    pallas_call x1, Pallas kernels, attend(): pl.pallas_call(kernel, grid=(queries // wide,), out_shape=[jax.ShapeDtype...  20.7 us

profile of v1, /device:TPU:0, one launch (start us, length us, event | category | flops | bytes accessed | tf_op | source)
XLA Modules:
  0.0 474.5 jit_solution(14568577981747580468)
XLA Ops:
  0.7 5.4 %concatenate.12 = bf16[384]{0:T(512)(128)(2,1)S(1)} concatenate(bf16[32]{0:T(256)(128)(2,1)} %param.15, bf16[32]{0:T(256)(128)(2,1)} %param.16, bf16[64]{0:T(256)(128)(2,1)} %param.18, bf16[32]{0:T(256)(128)(2,1)} %param.20, bf16[32]{0:T(256)(128)(2,1)} %param.21, bf16[32]{0:T(256)(128)(2,1)} %param.22, bf16[128]{0:T(256)(128)(2,1)} %param.24, bf16[32]{0:T(256)(128)(2,1)} %param.26), dimensions={0} | concatenate | bytes 1536 | tf_op jit(solution)/shard_map/concatenate | solution.py:328
  6.7 43.6 %gather_first.1 = (bf16[8,128,1024]{2,1,0:T(8,128)(2,1)}, bf16[32,32,384]{2,1,0:T(8,128)(2,1)}, bf16[4,32,1024]{2,1,0:T(8,128)(2,1)}, bf16[32,16,128]{2,1,0:T(8,128)(2,1)}) custom-call(bf16[128,1024]{1,0:T(8,128)(2,1)} %refs_0_.1, bf16[32,3072]{1,0:T(8,128)(2,1)} %refs_1_.2, bf16[32,1024]{1,0:T(8,128)(2,1)} %refs_2_.2, bf16[16,128]{1,0:T(8,128)(2,1)} %pad_bitcast_fusion.1.refs_3_), custom_call_target="tpu_custom_call" | custom-call | tf_op jit(solution)/shard_map/gather_first/pallas_call | solution.py:90
  50.3 1.1 copy.31
  51.6 1.9 convert_reduce_fusion.4
  55.6 1.9 add_convert_fusion.2
  57.6 27.4 %spread_heads.1 = (bf16[2,64,4096]{2,1,0:T(8,128)(2,1)}, bf16[64,2048]{1,0:T(8,128)(2,1)}, bf16[4,8,32,1024]{3,2,1,0:T(8,128)(2,1)}) custom-call(bf16[3,2,64,1024]{3,2,1,0:T(8,128)(2,1)} %bitcast.82, bf16[4,32,1024]{2,1,0:T(8,128)(2,1)} %get-tuple-element.44.refs_1_), custom_call_target="tpu_custom_call" | custom-call | tf_op jit(solution)/shard_map/spread_heads/pallas_call | solution.py:90
  84.9 20.7 %attend.1 = (bf16[64,2048]{1,0:T(8,128)(2,1)}, f32[1,2048]{1,0:T(1,128)}) custom-call(bf16[64,2048]{1,0:T(8,128)(2,1)} %get-tuple-element.45.query_ref, bf16[2,64,4096]{2,1,0:T(8,128)(2,1)} %get-tuple-element.46.pair_ref), custom_call_target="tpu_custom_call" | custom-call | tf_op jit(solution)/shard_map/attend/pallas_call | solution.py:197
  105.7 15.0 %send_attended.1.refs_3_ = bf16[1024,128]{1,0:T(8,128)(2,1)} custom-call(bf16[64,2048]{1,0:T(8,128)(2,1)} %get-tuple-element.47.refs_0_.out_ref), custom_call_target="tpu_custom_call" | custom-call | tf_op jit(solution)/shard_map/send_attended/pallas_call | solution.py:90
  120.8 2.2 fusion.31
  124.3 94.8 %gather_second.1 = (bf16[8,128,1024]{2,1,0:T(8,128)(2,1)}, bf16[8,128,1024]{2,1,0:T(8,128)(2,1)}, bf16[32,32,512]{2,1,0:T(8,128)(2,1)}, bf16[4,128,1024]{2,1,0:T(8,128)(2,1)}) custom-call(bf16[128,1024]{1,0:T(8,128)(2,1)} %add_convert_fusion.4.refs_0_, bf16[128,1024]{1,0:T(8,128)(2,1)} %refs_1_.3, bf16[32,4096]{1,0:T(8,128)(2,1)} %refs_2_.3, ...), custom_call_target="tpu_custom_call" | custom-call | tf_op jit(solution)/shard_map/gather_second/pallas_call | solution.py:90
  219.1 4.4 fusion.33
  223.7 4.7 convolution_convert_fusion.2
  228.5 2.4 fusion.32
  230.9 2.3 convolution_convert_fusion.3
  233.2 2.8 convolution_convert_fusion
  236.0 2.6 convolution_convert_fusion.1
  238.6 85.9 %scatter_second.1 = (bf16[8,128,1024]{2,1,0:T(8,128)(2,1)}, bf16[8,128,1024]{2,1,0:T(8,128)(2,1)}, bf16[4,32,4096]{2,1,0:T(8,128)(2,1)}, bf16[4,128,1024]{2,1,0:T(8,128)(2,1)}) custom-call(bf16[8,128,1024]{2,1,0:T(8,128)(2,1)} %bitcast.69, bf16[8,128,1024]{2,1,0:T(8,128)(2,1)} %bitcast.68, bf16[32,32,512]{2,1,0:T(8,128)(2,1)} %bitcast.81, ...), custom_call_target="tpu_custom_call" | custom-call | tf_op jit(solution)/shard_map/scatter_second/pallas_call | solution.py:90
  324.5 4.2 convert_reduce_fusion
  329.0 2.2 fusion.27
  332.1 1.4 convolution_convert_fusion.6.refs_0_
  333.5 12.4 %send_grad.1.grad_ref = bf16[64,2048]{1,0:T(8,128)(2,1)} custom-call(bf16[1024,128]{1,0:T(8,128)(2,1)} %convolution_convert_fusion.6.refs_0_), custom_call_target="tpu_custom_call" | custom-call | tf_op jit(solution)/shard_map/send_grad/pallas_call | solution.py:90
  345.9 24.4 %attend_back.1 = (bf16[64,2048]{1,0:T(8,128)(2,1)}, bf16[2,64,4096]{2,1,0:T(8,128)(2,1)}) custom-call(bf16[64,2048]{1,0:T(8,128)(2,1)} %get-tuple-element.45.query_ref, bf16[2,64,4096]{2,1,0:T(8,128)(2,1)} %get-tuple-element.46.pair_ref, bf16[64,2048]{1,0:T(8,128)(2,1)} %send_grad.1.grad_ref, bf16[64,2048]{1,0:T(8,128)(2,1)} %get-tuple-element.47.refs_0_.out_ref, ...), custom_call_target="tpu_custom_call" | custom-call | tf_op jit(solution)/shard_map/attend_back/pallas_call | solution.py:272
  370.3 34.0 %return_heads.1 = (bf16[2,64,1024]{2,1,0:T(8,128)(2,1)}, bf16[2,2,2,64,1024]{4,3,2,1,0:T(8,128)(2,1)}, bf16[8,128,1024]{2,1,0:T(8,128)(2,1)}, bf16[128,1024]{1,0:T(8,128)(2,1)}) custom-call(bf16[64,2048]{1,0:T(8,128)(2,1)} %get-tuple-element.56.refs_0_, bf16[2,64,4096]{2,1,0:T(8,128)(2,1)} %get-tuple-element.57.refs_1_, bf16[128,1024]{1,0:T(8,128)(2,1)} %copy-done.5, ...), custom_call_target="tpu_custom_call" | custom-call | tf_op jit(solution)/shard_map/return_heads/pallas_call | solution.py:90
  404.3 1.5 convert_reduce_fusion.7
  407.2 5.3 %fusion.26 = (f32[1024]{0:T(1024)S(1)}, f32[1024]{0:T(1024)S(1)}, bf16[1024,1024]{1,0:T(8,128)(2,1)}, bf16[1024,1024]{1,0:T(8,128)(2,1)}) fusion(f32[1024]{0:T(1024)S(1)} %get-tuple-element.101, f32[1024]{0:T(1024)S(1)} %get-tuple-element.99, bf16[8,128,1024]{2,1,0:T(8,128)(2,1)S(1)} %copy-done, f32[1024]{0:T(1024)S(1)} %reshape.297, ...), kind=kOutput, calls=%fused_computation.89 | convolution fusion | flops 818149376 | bytes 8675328 | tf_op jit(solution)/shard_map/dot_general | solution.py:132
  414.0 2.8 convolution_convert_fusion.5
  416.8 2.2 convolution_convert_fusion.4
  419.0 46.5 %scatter_first.1 = (bf16[8,128,1024]{2,1,0:T(8,128)(2,1)}, bf16[4,32,3072]{2,1,0:T(8,128)(2,1)}, bf16[4,32,1024]{2,1,0:T(8,128)(2,1)}, f32[32,8,128]{2,1,0:T(8,128)}) custom-call(bf16[8,128,1024]{2,1,0:T(8,128)(2,1)} %bitcast.71, bf16[32,32,384]{2,1,0:T(8,128)(2,1)} %bitcast.83, bf16[4,32,1024]{2,1,0:T(8,128)(2,1)} %bitcast.79, f32[32,8,128]{2,1,0:T(8,128)} %bitcast.84), custom_call_target="tpu_custom_call" | custom-call | tf_op jit(solution)/shard_map/scatter_first/pallas_call | solution.py:90
  465.5 2.0 convert_reduce_fusion.2
  468.2 1.0 fusion.17
  472.6 1.0 convert_reduce_fusion.5
  473.6 0.9 convert_reduce_fusion.6
  (100 shorter events, 12.3 us)
Async XLA Ops:
  50.3 3.3 copy-start
  54.5 1.1 copy-start.18
  57.6 63.2 %copy-start.1 = (bf16[128,1024]{1,0:T(8,128)(2,1)S(1)}, bf16[128,1024]{1,0:T(8,128)(2,1)}, u32[]{:S(2)}) copy-start(bf16[128,1024]{1,0:T(8,128)(2,1)} %refs_0_.1) | copy-start | bytes 786436
  223.7 4.7 %copy-start.15 = (bf16[8,128,1024]{2,1,0:T(8,128)(2,1)S(1)}, bf16[8,128,1024]{2,1,0:T(8,128)(2,1)}, u32[]{:S(2)}) copy-start(bf16[8,128,1024]{2,1,0:T(8,128)(2,1)} %get-tuple-element.49) | copy-start | bytes 6291460
  223.7 4.7 %copy-start.17 = (bf16[4,128,1024]{2,1,0:T(8,128)(2,1)S(1)}, bf16[4,128,1024]{2,1,0:T(8,128)(2,1)}, u32[]{:S(2)}) copy-start(bf16[4,128,1024]{2,1,0:T(8,128)(2,1)} %get-tuple-element.50) | copy-start | bytes 3145732
  223.7 4.7 %copy-start.20 = (f32[1024,512]{1,0:T(8,128)S(1)}, f32[1024,512]{1,0:T(8,128)}, u32[]{:S(2)}) copy-start(f32[1024,512]{1,0:T(8,128)} %fusion.33) | copy-start | bytes 6291460
  228.5 2.4 copy-start.14
  233.2 2.8 copy-start.16
  329.0 3.1 copy-start.2
  331.2 0.8 copy-start.3
  332.1 38.2 %copy-start.5 = (bf16[128,1024]{1,0:T(8,128)(2,1)}, bf16[128,1024]{1,0:T(8,128)(2,1)S(1)}, u32[]{:S(2)}) copy-start(bf16[128,1024]{1,0:T(8,128)(2,1)S(1)} %convert_element_type.203.refs_2_) | copy-start | bytes 786436
  404.3 1.7 copy-start.11
  405.9 0.8 copy-start.6
  412.5 4.3 copy-start.7
  413.2 3.6 copy-start.19
  465.5 2.7 copy-start.4
  467.6 1.7 copy-start.10
  467.7 2.4 copy-start.12
  467.9 2.9 copy-start.13
  467.9 4.7 copy-start.9
  469.3 4.3 copy-start.8

commit v2 on v1

v2 whole, which is shorter than its diff:
```python
import math

import jax
import jax.numpy as jnp
from jax import lax
from jax.experimental import pallas as pl
from jax.experimental.pallas import tpu as pltpu
from jax.sharding import PartitionSpec as P

H = 16
G = 8
UNITS = 128
EPSILON = 1e-05
GELU_SCALE = 0.7978845608028654
GELU_CUBIC = 0.044715
LOG2E = 1.4426950408889634
MESH = pl.DeviceIdType.MESH
BF16 = jnp.bfloat16
F32 = jnp.float32
VMEM = pl.BlockSpec(memory_space=pltpu.VMEM)
ANY = pl.BlockSpec(memory_space=pl.ANY)


def position(fsdp):
    return lax.axis_index("ctx") * fsdp + lax.axis_index("fsdp")


def flip(number, bit):
    return number + bit - 2 * bit * lax.rem(number // bit, 2)


def span(index, size):
    return pl.ds(pl.multiple_of(index * size, size), size)


def loop(low, high, step):
    def turn(index, carry):
        step(index)
        return carry

    lax.fori_loop(low, high, turn, 0)


def dot(left, right, left_dim, right_dim):
    return lax.dot_general(
        left, right, (((left_dim,), (right_dim,)), ((), ())), preferred_element_type=F32
    )


class Sizes:
    def __init__(self, n, fsdp):
        self.n, self.fsdp = n, fsdp
        self.groups = n // G
        self.parts = self.groups // 2
        self.chips = self.groups // 4
        self.per_group = G // self.parts


class Wire:
    def __init__(self, sizes, send, recv, local):
        self.sizes = sizes
        self.n, self.fsdp = sizes.n, sizes.fsdp
        self.send, self.recv, self.local = send, recv, local
        self.me = position(self.fsdp)
        self.t, self.m = self.me // G, lax.rem(self.me, G)
        self.core = lax.rem(self.m // 2, 2)
        self.sibling = flip(self.me, 2)
        self.peers = [flip(self.m, 1), flip(self.m, 4), flip(flip(self.m, 1), 4)]
        self.quarter = self.t // sizes.chips
        self.part = lax.rem(self.t, sizes.chips) * 2 + self.core
        self.source_core = self.quarter // 2
        self.source_m = self.m + 2 * (self.source_core - self.core)
        self.which = lax.rem(self.quarter, 2)
        self.head = 2 * self.source_m + self.which

    def where(self, device):
        return (device // self.fsdp, lax.rem(device, self.fsdp))

    def greet(self):
        barrier = pltpu.get_barrier_semaphore()

        def hello(step):
            other = lax.rem(self.me + step, self.n)
            pl.semaphore_signal(barrier, inc=1, device_id=self.where(other), device_id_type=MESH)

        loop(1, self.n, hello)
        pl.semaphore_wait(barrier, self.n - 1)

    def put(self, lane, source, target, device):
        pltpu.make_async_remote_copy(
            src_ref=source,
            dst_ref=target,
            send_sem=self.send.at[lane],
            recv_sem=self.recv.at[lane],
            device_id=self.where(device),
            device_id_type=MESH,
        ).start()

    def keep(self, lane, source, target):
        pltpu.make_async_copy(source, target, self.local.at[lane]).start()

    def give(self, lane, source, target, device):
        @pl.when(device != self.me)
        def _():
            self.put(lane, source, target, device)

        @pl.when(device == self.me)
        def _():
            self.keep(lane, source, target)

    def kept(self, lane, like):
        pltpu.make_async_copy(like, like, self.local.at[lane]).wait()

    def sent(self, lane, like):
        pltpu.make_async_copy(like, like, self.send.at[lane]).wait()

    def came(self, lane, like):
        pltpu.make_async_copy(like, like, self.recv.at[lane]).wait()

    def settle(self, lane, like):
        self.came(lane, like)
        self.sent(lane, like)

    def settle_given(self, lane, mine, less, whole):
        @pl.when(mine)
        def _():
            self.kept(lane, whole[0])
            self.settle(lane, less)

        @pl.when(jnp.logical_not(mine))
        def _():
            self.settle(lane, whole[1])

    def group(self, step):
        m = lax.rem(self.m + step, G)
        return m, self.t * G + m

    def column(self, step):
        t = lax.rem(self.t + step, self.sizes.groups)
        return t, t * G + self.m


class Gather:
    LANES = 4

    def __init__(self, wire, lane, block, place, four):
        self.wire, self.lane, self.block, self.place, self.four = wire, lane, block, place, four

    def start(self):
        wire, mine = self.wire, self.place(self.wire.m)
        for k, m in enumerate(wire.peers):
            wire.put(self.lane + k, self.block, mine, wire.t * G + m)
        wire.put(self.lane + 3, self.block, mine, wire.sibling)
        wire.keep(self.lane, self.block, mine)

    def forward(self):
        wire = self.wire
        for k, m in enumerate(wire.peers):
            wire.came(self.lane + k, self.place(m))
            wire.put(self.lane + 3, self.place(m), self.place(m), wire.sibling)

    def finish(self):
        wire = self.wire
        wire.kept(self.lane, self.place(wire.m))
        for k in range(3):
            wire.sent(self.lane + k, self.place(wire.m))
        wire.settle(self.lane + 3, self.four)


class Scatter:
    LANES = 4

    def __init__(self, wire, lane, parts, got, summed, result):
        self.wire, self.lane = wire, lane
        self.parts, self.got, self.summed, self.result = parts, got, summed, result

    def start(self):
        wire = self.wire
        for k, m in enumerate([wire.m] + wire.peers):
            wire.put(self.lane + 3, self.parts.at[flip(m, 2)], self.got.at[k], wire.sibling)

    def forward(self):
        wire = self.wire
        wire.came(self.lane + 3, self.got)
        rows = self.got.shape[1]
        step = 16
        for k, m in reversed(list(enumerate([wire.m] + wire.peers))):

            def add(i, k=k, m=m):
                at = span(i, step)
                total = self.parts[m, at, :].astype(F32) + self.got[k, at, :].astype(F32)
                self.summed[k, at, :] = total.astype(BF16)

            loop(0, rows // step, add)
            if k:
                wire.put(self.lane + k - 1, self.summed.at[k], self.result.at[k], wire.t * G + m)
            else:
                wire.keep(self.lane, self.summed.at[0], self.result.at[0])

    def finish(self):
        wire = self.wire
        wire.sent(self.lane + 3, self.got)
        wire.kept(self.lane, self.result.at[0])
        for k in range(3):
            wire.settle(self.lane + k, self.result.at[k + 1])


def scatter_scratch(rows, width):
    return [pltpu.VMEM((4, rows, width), BF16), pltpu.VMEM((4, rows, width), BF16)]


def exchange(body, name, number, sizes, lanes, inputs, outs, scratch=(), vmem_outs=0):
    def kernel(*refs):
        ins = refs[: len(inputs)]
        results = refs[len(inputs) : len(inputs) + len(outs)]
        extra = refs[len(inputs) + len(outs) : len(refs) - 3]
        wire = Wire(sizes, *refs[len(refs) - 3 :])
        wire.greet()
        body(wire, *ins, *results, *extra)

    kernel.__name__ = name
    return pl.pallas_call(
        kernel,
        out_shape=[jax.ShapeDtypeStruct(shape, kind) for shape, kind in outs],
        in_specs=[VMEM] * len(inputs),
        out_specs=[VMEM] * vmem_outs + [ANY] * (len(outs) - vmem_outs),
        scratch_shapes=[*scratch, *([pltpu.SemaphoreType.DMA((lanes,))] * 3)],
        compiler_params=pltpu.CompilerParams(collective_id=number, has_side_effects=True),
        name=name,
    )(*inputs)


def normalize(inputs):
    centred = inputs - jnp.mean(inputs, axis=1, keepdims=True)
    inverse = lax.rsqrt(jnp.mean(centred * centred, axis=1, keepdims=True) + EPSILON)
    return centred * inverse, inverse


def normalize_back(grad_norm, scaled, inverse, gain_row):
    grad_scaled = grad_norm * gain_row
    mean_one = jnp.mean(grad_scaled, axis=1, keepdims=True)
    mean_two = jnp.mean(grad_scaled * scaled, axis=1, keepdims=True)
    return inverse * (grad_scaled - mean_one - scaled * mean_two)


def gelu_pair(pre_act):
    tangent = jnp.tanh(GELU_SCALE * (pre_act + GELU_CUBIC * pre_act * pre_act * pre_act))
    activated = 0.5 * pre_act * (1.0 + tangent)
    derivative = 0.5 * (1.0 + tangent) + 0.5 * pre_act * (1.0 - tangent * tangent) * GELU_SCALE * (
        1.0 + 3.0 * GELU_CUBIC * pre_act * pre_act
    )
    return (activated, derivative)


def tiles_of(queries, parts):
    wide = min(256, queries)
    deep = min(512, wide * parts)
    return wide, deep, wide * parts // deep


def query_places(tile, wide, parts, part):
    column = lax.broadcasted_iota(jnp.int32, (1, wide), 1)
    block = tile * (wide // 128) + column // 128
    return (block * parts + part) * 128 + lax.rem(column, 128)


def attend_tiles(wire, query_ref, pair_ref, out_ref, total_ref, key_ref, after):
    width, queries = query_ref.shape
    keys = pair_ref.shape[2]
    parts = wire.sizes.parts
    wide, deep, band = tiles_of(queries, parts)
    factor = LOG2E / math.sqrt(width)

    def turn(j):
        at = span(j, deep)
        key_ref[at, :] = pair_ref[0, :, at].T

    loop(0, keys // deep, turn)

    def tile_step(tile):
        mine = span(tile, wide)
        query = query_ref[:, mine]
        places = query_places(tile, wide, parts, wire.part)

        def step(j, carry, masked):
            best, total, summed = carry
            at = span(j, deep)
            scores = dot(key_ref[at, :], query, 1, 0)
            if masked:
                key_places = j * deep + lax.broadcasted_iota(jnp.int32, (deep, wide), 0)
                scores = jnp.where(key_places <= places, scores, -1e30)
            higher = jnp.maximum(best, jnp.max(scores, axis=0, keepdims=True))
            weights = jnp.exp2((scores - higher) * factor)
            shrunk = jnp.exp2((best - higher) * factor)
            total = total * shrunk + jnp.sum(weights, axis=0, keepdims=True)
            summed = summed * shrunk + dot(pair_ref[1, :, at], weights.astype(BF16), 1, 0)
            return higher, total, summed

        carry = (
            jnp.full((1, wide), -1e30, F32),
            jnp.zeros((1, wide), F32),
            jnp.zeros((width, wide), F32),
        )
        carry = lax.fori_loop(0, tile * band, lambda j, c: step(j, c, False), carry)
        for extra in range(band):
            carry = step(tile * band + extra, carry, True)
        best, total, summed = carry
        out_ref[:, mine] = (summed / total).astype(BF16)
        total_ref[:, mine] = best * factor + jnp.log2(total)
        after(tile)

    loop(0, queries // wide, tile_step)


def attend_back_tiles(
    wire, query_ref, pair_ref, grad_ref, out_ref, total_ref, dq_ref, dpair_ref, query_rows, grad_rows, delta_ref, dq_sum, after
):
    width, queries = query_ref.shape
    keys = pair_ref.shape[2]
    parts = wire.sizes.parts
    wide, deep, band = tiles_of(queries, parts)
    scale = 1.0 / math.sqrt(width)
    factor = LOG2E * scale

    def prepare(tile):
        mine = span(tile, wide)
        grad = grad_ref[:, mine]
        query_rows[mine, :] = query_ref[:, mine].T
        grad_rows[mine, :] = grad.T
        delta_ref[:, mine] = jnp.sum(grad.astype(F32) * out_ref[:, mine].astype(F32), axis=0, keepdims=True)
        dq_sum[:, mine] = jnp.zeros((width, wide), F32)

    loop(0, queries // wide, prepare)

    def key_step(j):
        at = span(j, deep)
        key_t, value_t = pair_ref[0, :, at], pair_ref[1, :, at]
        key, value = key_t.T, value_t.T
        key_places = j * deep + lax.broadcasted_iota(jnp.int32, (deep, wide), 0)

        def step(tile, carry, masked):
            dkey, dvalue = carry
            mine = span(tile, wide)
            scores = dot(key, query_ref[:, mine], 1, 0) * factor
            if masked:
                places = query_places(tile, wide, parts, wire.part)
                scores = jnp.where(key_places <= places, scores, -1e30)
            probs = jnp.exp2(scores - total_ref[:, mine])
            dvalue = dvalue + dot(probs.astype(BF16), grad_rows[mine, :], 1, 0)
            grad_probs = dot(value, grad_ref[:, mine], 1, 0)
            grad_scores = (probs * (grad_probs - delta_ref[:, mine]) * scale).astype(BF16)
            dkey = dkey + dot(grad_scores, query_rows[mine, :], 1, 0)
            dq_sum[:, mine] += dot(key_t, grad_scores, 1, 0)
            return dkey, dvalue

        first = j // band
        carry = (jnp.zeros((deep, width), F32), jnp.zeros((deep, width), F32))
        carry = step(first, carry, True)
        dkey, dvalue = lax.fori_loop(first + 1, queries // wide, lambda i, c: step(i, c, False), carry)
        dpair_ref[0, :, at] = dkey.T.astype(BF16)
        dpair_ref[1, :, at] = dvalue.T.astype(BF16)

        @pl.when(lax.rem(j, band) == band - 1)
        def _():
            mine = span(first, wide)
            dq_ref[:, mine] = dq_sum[:, mine].astype(BF16)

        after(j, first, lax.rem(j, band) == band - 1)

    loop(0, keys // deep, key_step)


def layer(n, fsdp):
    sizes = Sizes(n, fsdp)
    groups, parts, per_group = sizes.groups, sizes.parts, sizes.per_group

    def on_device(
        residual_in,
        first_gain,
        first_shift,
        attend_weight,
        attend_bias,
        merge_weight,
        merge_bias,
        second_gain,
        second_shift,
        expand_weight,
        expand_bias,
        shrink_weight,
        shrink_bias,
        cotangent,
    ):
        rows, width = residual_in.shape
        depth = width // n
        hidden_rows = shrink_weight.shape[0]
        hidden_units = expand_weight.shape[1]
        slice_width = width // G
        slice_units = hidden_units // G
        blocks = slice_units // UNITS
        shares = UNITS // hidden_rows
        head = width // H
        group_rows = rows * G
        half = group_rows // 2
        tokens = rows * n
        queries = tokens // parts
        chunk = per_group * rows
        me = position(fsdp)
        member = lax.rem(me, G)

        small = (first_gain, first_shift, attend_bias, merge_bias, second_gain, second_shift, expand_bias, shrink_bias)
        counts = [s.shape[0] for s in small]
        packed_rows = -(-sum(counts) // 2048) * 16
        packed = jnp.pad(jnp.concatenate(small), (0, packed_rows * 128 - sum(counts))).reshape(packed_rows, 128)

        def unit_block(q, m):
            return span(q * G + m, UNITS)

        def gather_first(wire, x, attend, merge, vec, expand, x_all, attend_all, merge_all, vec_all, expand_all):
            me, t, m = wire.me, wire.t, wire.m
            x_gather = Gather(wire, 4, x, lambda k: x_all.at[k], x_all.at[pl.ds(0, 4)])
            x_gather.start()

            def attend_to(other, move):
                for p in range(3):
                    columns = pl.ds(pl.multiple_of(p * width + other * slice_width, 128), slice_width)
                    move(0, attend.at[:, columns], attend_all.at[me, :, pl.ds(p * slice_width, slice_width)])

            def to_all(step):
                device = lax.rem(me + step, n)
                attend_to(lax.rem(device, G), lambda lane, s, d: wire.put(lane, s, d, device))
                wire.put(1, vec, vec_all.at[me], device)

            def expand_to(other, move):
                for q in range(blocks):
                    move(3, expand.at[:, unit_block(q, other)], expand_all.at[m, :, pl.ds(q * UNITS, UNITS)])

            def to_group(step):
                other, device = wire.group(step)
                expand_to(other, lambda lane, s, d: wire.put(lane, s, d, device))

            def to_column(step):
                _, device = wire.column(step)
                wire.put(2, merge, merge_all.at[t], device)

            loop(1, n, to_all)
            loop(1, groups, to_column)
            loop(1, G, to_group)
            attend_to(m, wire.keep)
            wire.keep(1, vec, vec_all.at[me])
            wire.keep(2, merge, merge_all.at[t])
            expand_to(m, wire.keep)
            wire.kept(0, attend_all.at[0])
            wire.kept(1, vec_all.at[0])
            wire.kept(2, merge_all.at[0])
            wire.kept(3, expand_all.at[0])
            x_gather.forward()
            wire.settle(0, attend_all.at[pl.ds(0, n - 1)])
            wire.settle(1, vec_all.at[pl.ds(0, n - 1)])
            wire.settle(2, merge_all.at[pl.ds(0, groups - 1)])
            wire.settle(3, expand_all.at[pl.ds(0, G - 1)])
            x_gather.finish()

        x_all, attend_all, merge_all, vec_all, expand_group = exchange(
            gather_first,
            "gather_first",
            0,
            sizes,
            8,
            (residual_in, attend_weight, merge_weight, packed, expand_weight),
            (
                ((G, rows, width), BF16),
                ((n, depth, 3 * slice_width), BF16),
                ((groups, depth, width), BF16),
                ((n, packed_rows, 128), BF16),
                ((G, depth, slice_units), BF16),
            ),
        )
        flat = vec_all.reshape(n, packed_rows * 128)
        spots = [sum(counts[:k]) for k in range(len(counts))]
        gain_one, shift_one, attend_shift, merge_shift, gain_two, shift_two, expand_shift, shrink_shift = (
            flat[:, spot : spot + count].reshape(-1).astype(F32) for spot, count in zip(spots, counts)
        )
        attend_slice = attend_all.reshape(width, 3 * slice_width)

        scaled_group, _ = normalize(x_all.reshape(group_rows, width).astype(F32))
        input_one = (scaled_group * gain_one + shift_one).astype(BF16)
        bias_mine = jnp.concatenate(
            [
                lax.dynamic_slice_in_dim(attend_shift, member * slice_width, slice_width),
                jnp.zeros((slice_width,), F32),
                lax.dynamic_slice_in_dim(attend_shift, width + member * slice_width, slice_width),
            ]
        )
        projected = (dot(attend_slice, input_one, 0, 1) + bias_mine[:, None]).astype(BF16)
        projected = projected.reshape(3, 2, head, group_rows)

        def spread_heads(wire, qkv, merge, pair, query, merge_full):
            t, m, core = wire.t, wire.m, wire.core
            chips = sizes.chips
            own = core == wire.source_core
            merge_gather = Gather(wire, 3, merge, lambda k: merge_full.at[:, k], merge_full.at[:, pl.ds(0, 4)])
            first = 7

            def to_chip(step):
                other = lax.rem(core * 2 * chips + lax.rem(t + step, 2 * chips), groups)
                which = lax.rem(other // chips, 2)
                for c in range(2):
                    device = other * G + m + 2 * (c - core)
                    mine = pl.ds(pl.multiple_of(t * group_rows + c * half, 128), half)
                    for kind in range(2):
                        wire.give(first + t, qkv.at[1 + kind, which, :, pl.ds(c * half, half)], pair.at[kind, :, mine], device)

            def queries_to(step):
                other = lax.rem(core * 2 * chips + lax.rem(t + step, 2 * chips), groups)
                which = lax.rem(other // chips, 2)
                for c in range(2):
                    device = other * G + m + 2 * (c - core)
                    part = lax.rem(other, chips) * 2 + c
                    for i in range(per_group):
                        source = span(part + i * parts, rows)
                        target = span(t * per_group + i, rows)
                        wire.give(0, qkv.at[0, which, :, source], query.at[:, target], device)

            loop(0, 2 * chips, to_chip)
            loop(0, 2 * chips, queries_to)
            merge_gather.start()

            def pass_on(step):
                other = lax.rem(t + step, groups)
                piece = pair.at[:, :, pl.ds(pl.multiple_of(other * group_rows + core * half, 128), half)]
                here = jnp.logical_and(own, other == t)

                @pl.when(here)
                def _():
                    wire.kept(first + other, piece)

                @pl.when(jnp.logical_not(here))
                def _():
                    wire.came(first + other, piece)

                wire.put(1, piece, piece, wire.sibling)

            loop(0, groups, pass_on)
            merge_gather.forward()
            all_halves = pair.at[:, :, pl.ds(0, tokens // 2)]
            wire.settle(1, all_halves)
            merge_gather.finish()

            @pl.when(own)
            def _():
                wire.sent(first + t, pair.at[:, :, pl.ds(0, (groups - 1) * half)])
                wire.kept(0, query.at[:, pl.ds(0, chunk)])
                wire.settle(0, query.at[:, pl.ds(0, queries - chunk)])

            @pl.when(jnp.logical_not(own))
            def _():
                wire.sent(first + t, all_halves)
                wire.settle(0, query)

        pair_t, query_t, merge_full = exchange(
            spread_heads,
            "spread_heads",
            1,
            sizes,
            7 + groups,
            (projected, merge_all),
            (((2, head, tokens), BF16), ((head, queries), BF16), ((groups, G, depth, width), BF16)),
        )
        merge_full = merge_full.reshape(width, width)

        def attend(wire, query, pair, expand, cot, out, total, attended, expand_all, cot_all, keys_scratch):
            me, t = wire.me, wire.t
            cot_gather = Gather(wire, 2, cot, lambda k: cot_all.at[k], cot_all.at[pl.ds(0, 4)])

            def to_column(step):
                _, device = wire.column(step)
                wire.put(1, expand, expand_all.at[t], device)

            loop(1, groups, to_column)
            cot_gather.start()
            wire.keep(1, expand, expand_all.at[t])
            place = span(wire.head, head)
            wide = tiles_of(queries, parts)[0]

            def after(tile):
                for b in range(wide // rows):
                    block = tile * (wide // rows) + b
                    wire.give(0, out.at[:, span(block, rows)], attended.at[place, :], block * parts + wire.part)

                @pl.when(tile == queries // wide - 2)
                def _():
                    cot_gather.forward()

            attend_tiles(wire, query, pair, out, total, keys_scratch, after)
            mine = lax.rem(me, parts) == wire.part

            @pl.when(mine)
            def _():
                wire.kept(0, attended.at[pl.ds(0, head), :])
                wire.came(0, attended.at[pl.ds(0, width - head), :])
                wire.sent(0, out.at[:, pl.ds(0, queries - rows)])

            @pl.when(jnp.logical_not(mine))
            def _():
                wire.came(0, attended)
                wire.sent(0, out)

            wire.kept(1, expand_all.at[0])
            wire.settle(1, expand_all.at[pl.ds(0, groups - 1)])
            cot_gather.finish()

        out_t, log_total, attended_t, expand_all, cot_all = exchange(
            attend,
            "attend",
            2,
            sizes,
            6,
            (query_t, pair_t, expand_group, cotangent),
            (
                ((head, queries), BF16),
                ((1, queries), F32),
                ((width, rows), BF16),
                ((groups, G, depth, slice_units), BF16),
                ((G, rows, width), BF16),
            ),
            scratch=[pltpu.VMEM((tokens, head), BF16)],
            vmem_outs=2,
        )

        block_in = residual_in.astype(F32)
        hidden = block_in + (dot(attended_t, merge_full, 0, 0) + merge_shift)
        scaled_two, inverse_two = normalize(hidden)
        input_two = (scaled_two * gain_two + shift_two).astype(BF16)

        def gather_second(wire, normed, shrink, normed_all, shrink_all):
            me, t = wire.me, wire.t
            block = me // shares
            user = lax.rem(block, G)
            normed_gather = Gather(wire, 1, normed, lambda k: normed_all.at[k], normed_all.at[pl.ds(0, 4)])
            normed_gather.start()

            def to_users(step):
                other = lax.rem(t + step, groups)
                wire.give(0, shrink, shrink_all.at[block // G * shares + lax.rem(me, shares)], other * G + user)

            loop(0, groups, to_users)
            normed_gather.forward()
            wire.settle_given(0, user == wire.m, shrink_all.at[pl.ds(0, groups - 1)], (shrink, shrink_all))
            normed_gather.finish()

        normed_all, shrink_all = exchange(
            gather_second,
            "gather_second",
            3,
            sizes,
            5,
            (input_two, shrink_weight),
            (((G, rows, width), BF16), ((groups, hidden_rows, width), BF16)),
        )
        group_two = normed_all.reshape(group_rows, width)
        group_cot = cot_all.reshape(group_rows, width)
        expand_slice = expand_all.reshape(width, slice_units)
        shrink_slice = shrink_all.reshape(slice_units, width)
        shift_units = lax.dynamic_index_in_dim(expand_shift.reshape(blocks, G, UNITS), member, 1, False).reshape(-1)
        activated, derivative = gelu_pair(dot(group_two, expand_slice, 1, 0) + shift_units)
        act_input = activated.astype(BF16)
        shrunk_part = dot(act_input, shrink_slice, 1, 0).astype(BF16)
        grad_shrink_part = dot(act_input, group_cot, 0, 0).astype(BF16)
        grad_pre = dot(group_cot, shrink_slice, 1, 1) * derivative
        grad_expand_shift = jnp.sum(grad_pre, axis=0)
        grad_pre_input = grad_pre.astype(BF16)
        grad_expand_part = dot(group_two, grad_pre_input, 0, 0).astype(BF16)
        grad_two_part = dot(grad_pre_input, expand_slice, 1, 1).astype(BF16)

        def scatter_second(wire, two, shrink, two_all, shrink_all, got, summed):
            me, t, m = wire.me, wire.t, wire.m
            two_scatter = Scatter(wire, 1, two, got, summed, two_all)
            two_scatter.start()

            def to_owners(step):
                piece = lax.rem(step + t, groups)
                owner = (piece // shares * G + m) * shares + lax.rem(piece, shares)
                wire.give(0, shrink.at[piece], shrink_all.at[t], owner)

            loop(0, groups, to_owners)
            two_scatter.forward()
            wire.settle_given(
                0, lax.rem(me // shares, G) == m, shrink_all.at[pl.ds(0, groups - 1)], (shrink_all.at[0], shrink_all)
            )
            two_scatter.finish()

        two_parts, shrink_parts = exchange(
            scatter_second,
            "scatter_second",
            4,
            sizes,
            5,
            (
                grad_two_part.reshape(G, rows, width),
                grad_shrink_part.reshape(groups, hidden_rows, width),
            ),
            (((4, rows, width), BF16), ((groups, hidden_rows, width), BF16)),
            scratch=scatter_scratch(rows, width),
        )
        grad_shrink_weight = jnp.sum(shrink_parts.astype(F32), axis=0)
        grad_top = cotangent.astype(F32)
        grad_shrink_shift = jnp.sum(grad_top, axis=0)
        grad_two = jnp.sum(two_parts.astype(F32), axis=0)
        grad_gain_two = jnp.sum(grad_two * scaled_two, axis=0)
        grad_shift_two = jnp.sum(grad_two, axis=0)
        grad_hidden = grad_top + normalize_back(grad_two, scaled_two, inverse_two, gain_two)
        grad_merge_shift = jnp.sum(grad_hidden, axis=0)
        grad_hidden_input = grad_hidden.astype(BF16)
        grad_attended_t = dot(merge_full, grad_hidden_input, 1, 1).astype(BF16)

        def send_grad(wire, grad, grad_out):
            me = wire.me
            part = lax.rem(me, parts)
            place = span(me // parts, rows)

            def to_head(step):
                h = lax.rem(step + me, H)
                source_m = h // 2
                quarter = lax.rem(source_m // 2, 2) * 2 + lax.rem(h, 2)
                t = quarter * sizes.chips + part // 2
                device = t * G + source_m + 2 * (lax.rem(part, 2) - lax.rem(source_m // 2, 2))
                wire.give(0, grad.at[span(h, head), :], grad_out.at[:, place], device)

            loop(0, H, to_head)
            mine = wire.part == part

            @pl.when(mine)
            def _():
                wire.kept(0, grad.at[pl.ds(0, head), :])
                wire.came(0, grad_out.at[:, pl.ds(0, queries - rows)])
                wire.sent(0, grad.at[pl.ds(0, width - head), :])

            @pl.when(jnp.logical_not(mine))
            def _():
                wire.came(0, grad_out)
                wire.sent(0, grad)

        (grad_t,) = exchange(send_grad, "send_grad", 5, sizes, 1, (grad_attended_t,), (((head, queries), BF16),))

        def attend_back(
            wire, query, pair, grad, out, total, shrunk, hidden_grad, att, expand,
            dq, dpair, dq_all, dpair_all, shrunk_all, hidden_all, att_all, expand_all,
            query_rows, grad_rows, delta, dq_sum, got, summed,
        ):
            me, t, m = wire.me, wire.t, wire.m
            shrunk_scatter = Scatter(wire, 4, shrunk, got, summed, shrunk_all)
            hidden_gather = Gather(wire, 8, hidden_grad, lambda k: hidden_all.at[k], hidden_all.at[pl.ds(0, 4)])
            shrunk_scatter.start()
            hidden_gather.start()
            place = pl.ds(pl.multiple_of(m * rows, 128), rows)

            def to_group(step):
                other, device = wire.group(step)
                wire.put(2, att.at[span(other, slice_width), :], att_all.at[:, place], device)

            loop(1, G, to_group)
            wire.keep(2, att.at[span(m, slice_width), :], att_all.at[:, place])
            shrunk_scatter.forward()
            wide, deep, band = tiles_of(queries, parts)

            def after(j, first, final):
                place_in_group = pl.ds(pl.multiple_of(lax.rem(j * deep, group_rows), deep), deep)
                device = j * deep // group_rows * G + wire.source_m
                wire.give(0, dpair.at[:, :, span(j, deep)], dpair_all.at[wire.part, wire.which, :, :, place_in_group], device)

                @pl.when(final)
                def _():
                    for b in range(wide // rows):
                        block = first * (wide // rows) + b
                        owner = block * parts + wire.part
                        wire.give(
                            1,
                            dq.at[:, span(block, rows)],
                            dq_all.at[wire.which, :, span(lax.rem(owner, G), rows)],
                            owner // G * G + wire.source_m,
                        )

                @pl.when(j == 2)
                def _():
                    def to_column(step):
                        other, device = wire.column(step)
                        wire.put(3, expand.at[other], expand_all.at[t], device)

                    loop(1, groups, to_column)
                    wire.keep(3, expand.at[t], expand_all.at[t])

                @pl.when(j == keys_tiles - 2)
                def _():
                    hidden_gather.forward()

            keys_tiles = tokens // deep
            attend_back_tiles(
                wire, query, pair, grad, out, total, dq, dpair, query_rows, grad_rows, delta, dq_sum, after
            )
            own = wire.core == wire.source_core

            @pl.when(own)
            def _():
                wire.kept(0, dpair.at[:, :, pl.ds(0, group_rows)])
                wire.kept(1, dq.at[:, pl.ds(0, chunk)])
                wire.sent(0, dpair.at[:, :, pl.ds(0, tokens - group_rows)])
                wire.sent(1, dq.at[:, pl.ds(0, queries - chunk)])
                wire.came(0, dpair.at[:, :, pl.ds(0, tokens - group_rows)])
                wire.came(1, dq.at[:, pl.ds(0, queries - chunk)])

            @pl.when(jnp.logical_not(own))
            def _():
                wire.sent(0, dpair)
                wire.sent(1, dq)
                wire.came(0, dpair)
                wire.came(1, dq)

            wire.kept(2, att_all.at[:, pl.ds(0, rows)])
            wire.settle(2, att_all.at[:, pl.ds(0, group_rows - rows)])
            wire.kept(3, expand_all.at[0])
            wire.settle(3, expand_all.at[pl.ds(0, groups - 1)])
            shrunk_scatter.finish()
            hidden_gather.finish()

        _, _, dq_all, dpair_all, shrunk_parts, grad_all, att_all, expand_parts = exchange(
            attend_back,
            "attend_back",
            6,
            sizes,
            12,
            (
                query_t,
                pair_t,
                grad_t,
                out_t,
                log_total,
                shrunk_part.reshape(G, rows, width),
                grad_hidden_input,
                attended_t,
                grad_expand_part.reshape(groups, G * depth, slice_units),
            ),
            (
                ((head, queries), BF16),
                ((2, head, tokens), BF16),
                ((2, head, group_rows), BF16),
                ((parts, 2, 2, head, group_rows), BF16),
                ((4, rows, width), BF16),
                ((G, rows, width), BF16),
                ((slice_width, group_rows), BF16),
                ((groups, G * depth, slice_units), BF16),
            ),
            scratch=[
                pltpu.VMEM((queries, head), BF16),
                pltpu.VMEM((queries, head), BF16),
                pltpu.VMEM((1, queries), F32),
                pltpu.VMEM((head, queries), F32),
                *scatter_scratch(rows, width),
            ],
            vmem_outs=2,
        )
        residual_out = (hidden + jnp.sum(shrunk_parts.astype(F32), axis=0) + shrink_shift).astype(BF16)
        grad_expand_group = jnp.sum(expand_parts.astype(F32), axis=0).astype(BF16).reshape(G, depth, slice_units)
        grad_pair = jnp.sum(dpair_all.astype(F32), axis=0)
        grad_projected = jnp.concatenate(
            [
                dq_all.astype(F32).reshape(slice_width, group_rows),
                grad_pair[:, 0].reshape(slice_width, group_rows),
                grad_pair[:, 1].reshape(slice_width, group_rows),
            ],
            axis=0,
        )
        grad_shift_mine = jnp.sum(grad_projected, axis=1)
        grad_projected = grad_projected.astype(BF16)
        grad_attend_part = dot(input_one, grad_projected, 0, 1).astype(BF16)
        grad_one_part = dot(grad_projected, attend_slice, 0, 1)
        grad_gain_one = jnp.sum(grad_one_part * scaled_group, axis=0)
        grad_shift_one = jnp.sum(grad_one_part, axis=0)
        grad_merge_part = dot(att_all, grad_all.reshape(group_rows, width), 1, 0).astype(BF16)

        grad_attend_shift = jnp.zeros((2 * width,), F32)
        grad_attend_shift = lax.dynamic_update_slice_in_dim(
            grad_attend_shift, grad_shift_mine[:slice_width], member * slice_width, 0
        )
        grad_attend_shift = lax.dynamic_update_slice_in_dim(
            grad_attend_shift, grad_shift_mine[2 * slice_width :], width + member * slice_width, 0
        )
        grad_expand_all = lax.dynamic_update_slice_in_dim(
            jnp.zeros((blocks, G, UNITS), F32), grad_expand_shift.reshape(blocks, 1, UNITS), member, 1
        ).reshape(-1)
        grads = (
            grad_gain_one,
            grad_shift_one,
            grad_attend_shift,
            grad_merge_shift,
            grad_gain_two,
            grad_shift_two,
            grad_expand_all,
            grad_shrink_shift,
        )
        total_size = sum(counts)
        vec_rows = -(-total_size // 1024) * 8
        packed_grads = jnp.pad(
            jnp.concatenate([g.reshape(n, -1) for g in grads], axis=1), ((0, 0), (0, vec_rows * 128 - total_size))
        ).reshape(n, vec_rows, 128)

        def scatter_first(wire, one, attend, merge, vec, expand, one_all, attend_all, merge_all, vec_all, expand_all, got, summed):
            me, t, m = wire.me, wire.t, wire.m
            one_scatter = Scatter(wire, 4, one, got, summed, one_all)
            one_scatter.start()

            def attend_to(device, move):
                for p in range(3):
                    columns = pl.ds(pl.multiple_of(p * width + m * slice_width, 128), slice_width)
                    move(1, attend.at[device, :, pl.ds(p * slice_width, slice_width)], attend_all.at[t, :, columns])

            def to_all(step):
                device = lax.rem(me + step, n)
                attend_to(device, lambda lane, s, d: wire.put(lane, s, d, device))
                wire.put(3, vec.at[device], vec_all.at[me], device)

            def to_owners(slot):
                wire.give(2, merge.at[slot], merge_all.at[t], m * groups + slot)

            def expand_to(other, move):
                for q in range(blocks):
                    move(0, expand.at[other, :, pl.ds(q * UNITS, UNITS)], expand_all.at[:, unit_block(q, m)])

            def to_group(step):
                other, device = wire.group(step)
                expand_to(other, lambda lane, s, d: wire.put(lane, s, d, device))

            loop(1, n // 2, to_all)
            one_scatter.forward()
            loop(n // 2, n, to_all)
            loop(0, groups, to_owners)
            loop(1, G, to_group)
            attend_to(me, wire.keep)
            expand_to(m, wire.keep)
            wire.keep(3, vec.at[me], vec_all.at[me])
            wire.kept(0, expand.at[0])
            wire.kept(1, attend.at[0])
            wire.kept(3, vec_all.at[0])
            wire.settle(0, expand.at[pl.ds(0, G - 1)])
            wire.settle(1, attend.at[pl.ds(0, n - 1)])
            wire.settle(3, vec_all.at[pl.ds(0, n - 1)])
            wire.settle_given(2, me // groups == m, merge_all.at[pl.ds(0, groups - 1)], (merge_all.at[0], merge_all))
            one_scatter.finish()

        one_parts, attend_parts, merge_parts, vec_parts, expand_whole = exchange(
            scatter_first,
            "scatter_first",
            7,
            sizes,
            8,
            (
                grad_one_part.astype(BF16).reshape(G, rows, width),
                grad_attend_part.reshape(n, depth, 3 * slice_width),
                grad_merge_part.reshape(groups, depth, width),
                packed_grads,
                grad_expand_group,
            ),
            (
                ((4, rows, width), BF16),
                ((groups, depth, 3 * width), BF16),
                ((groups, depth, width), BF16),
                ((n, vec_rows, 128), F32),
                ((depth, hidden_units), BF16),
            ),
            scratch=scatter_scratch(rows, width),
        )
        grad_one = jnp.sum(one_parts.astype(F32), axis=0)
        scaled_one, inverse_one = normalize(block_in)
        input_grad = grad_hidden + normalize_back(grad_one, scaled_one, inverse_one, gain_one)
        grad_attend_weight = jnp.sum(attend_parts.astype(F32), axis=0)
        grad_merge_weight = jnp.sum(merge_parts.astype(F32), axis=0)
        vec_sums = jnp.sum(vec_parts, axis=0).reshape(-1)
        (g_gain_one, g_shift_one, g_attend_bias, g_merge_bias, g_gain_two, g_shift_two, g_expand_bias, g_shrink_bias) = (
            vec_sums[spot : spot + count] for spot, count in zip(spots, counts)
        )
        return (
            residual_out,
            input_grad,
            g_gain_one,
            g_shift_one,
            grad_attend_weight,
            g_attend_bias,
            grad_merge_weight,
            g_merge_bias,
            g_gain_two,
            g_shift_two,
            expand_whole.astype(F32),
            g_expand_bias,
            grad_shrink_weight,
            g_shrink_bias,
        )

    return on_device


def solution(mesh):
    rows, line = P(("ctx", "fsdp"), None), P(("ctx", "fsdp"))
    n, fsdp = mesh.shape["ctx"] * mesh.shape["fsdp"], mesh.shape["fsdp"]
    return jax.shard_map(
        layer(n, fsdp),
        mesh=mesh,
        in_specs=(rows, line, line, rows, line, rows, line, line, line, rows, line, rows, line, rows),
        out_specs=(rows, rows, line, line, rows, line, rows, line, line, line, rows, line, rows, line),
        check_vma=False,
    )
```

time: 475 us -> 349 us (0.73)
  Pallas kernels: 405 us -> 278 us
    pallas_call x8, Pallas kernels: 360 us -> 278 us  [exchange(): pl.pallas_call(kernel, out_shape=[jax.ShapeDtypeStruct(shape, kind) for s...]
    pallas_call x2 -> x0, Pallas kernels: 45.1 us -> none  [the longest x1 24.4 us: attend_back(): pl.pallas_call(kernel, grid=(queries // wide,), out_shape=[jax.ShapeDtype...]
where the time goes in v2:
time: 349 us
  Pallas kernels  278 us (80%)
  matrix products  37.5 us (11%)
  other arithmetic  18.6 us (5%)
  local copies, waits for them, and re-layouts  13.4 us (4%)
    pallas_call x8, Pallas kernels, exchange(): pl.pallas_call(kernel, out_shape=[jax.ShapeDtypeStruct(shape, kind) for s...  278 us
    dot_general x12, matrix products, dot(): lax.dot_general(left, right, (((left_dim,), (right_dim,)), ((), ())), pre...  37.5 us

profile of v2, /device:TPU:0, one launch (start us, length us, event | category | flops | bytes accessed | tf_op | source)
XLA Modules:
  0.0 348.8 jit_solution(4636659845055259724)
XLA Ops:
  0.7 5.4 %concatenate.12 = bf16[384]{0:T(512)(128)(2,1)S(1)} concatenate(bf16[32]{0:T(256)(128)(2,1)} %param.15, bf16[32]{0:T(256)(128)(2,1)} %param.16, bf16[64]{0:T(256)(128)(2,1)} %param.18, bf16[32]{0:T(256)(128)(2,1)} %param.20, bf16[32]{0:T(256)(128)(2,1)} %param.21, bf16[32]{0:T(256)(128)(2,1)} %param.22, bf16[128]{0:T(256)(128)(2,1)} %param.24, bf16[32]{0:T(256)(128)(2,1)} %param.26), dimensions={0} | concatenate | bytes 1536 | tf_op jit(solution)/shard_map/concatenate | solution.py:413
  6.7 35.1 %gather_first.1 = (bf16[8,128,1024]{2,1,0:T(8,128)(2,1)}, bf16[32,32,384]{2,1,0:T(8,128)(2,1)}, bf16[4,32,1024]{2,1,0:T(8,128)(2,1)}, bf16[32,16,128]{2,1,0:T(8,128)(2,1)}, bf16[8,32,512]{2,1,0:T(8,128)(2,1)}) custom-call(bf16[128,1024]{1,0:T(8,128)(2,1)} %refs_0_.1, bf16[32,3072]{1,0:T(8,128)(2,1)} %refs_1_.2, bf16[32,1024]{1,0:T(8,128)(2,1)} %refs_2_.1, ...), custom_call_target="tpu_custom_call" | custom-call | tf_op jit(solution)/shard_map/gather_first/pallas_call | solution.py:222
  41.9 1.1 copy.31
  43.2 1.9 convert_reduce_fusion
  46.1 0.8 add_convert_fusion.1
  47.2 1.9 add_convert_fusion.2
  49.2 21.8 %spread_heads.1 = (bf16[2,64,4096]{2,1,0:T(8,128)(2,1)}, bf16[64,2048]{1,0:T(8,128)(2,1)}, bf16[4,8,32,1024]{3,2,1,0:T(8,128)(2,1)}) custom-call(bf16[3,2,64,1024]{3,2,1,0:T(8,128)(2,1)} %bitcast.87, bf16[4,32,1024]{2,1,0:T(8,128)(2,1)} %get-tuple-element.45.refs_1_), custom_call_target="tpu_custom_call" | custom-call | tf_op jit(solution)/shard_map/spread_heads/pallas_call | solution.py:222
  71.0 35.3 %attend.1 = (bf16[64,2048]{1,0:T(8,128)(2,1)}, f32[1,2048]{1,0:T(1,128)}, bf16[1024,128]{1,0:T(8,128)(2,1)}, bf16[4,8,32,512]{3,2,1,0:T(8,128)(2,1)}, bf16[8,128,1024]{2,1,0:T(8,128)(2,1)}) custom-call(bf16[64,2048]{1,0:T(8,128)(2,1)} %get-tuple-element.46.refs_0_, bf16[2,64,4096]{2,1,0:T(8,128)(2,1)} %get-tuple-element.47.refs_1_, ...), custom_call_target="tpu_custom_call" | custom-call | tf_op jit(solution)/shard_map/attend/pallas_call | solution.py:222
  106.4 2.2 fusion.31
  109.0 0.9 add_convert_fusion.4.refs_0_
  109.9 24.4 %gather_second.1 = (bf16[8,128,1024]{2,1,0:T(8,128)(2,1)}, bf16[4,128,1024]{2,1,0:T(8,128)(2,1)}) custom-call(bf16[128,1024]{1,0:T(8,128)(2,1)} %add_convert_fusion.4.refs_0_, bf16[128,1024]{1,0:T(8,128)(2,1)} %refs_1_.3), custom_call_target="tpu_custom_call" | custom-call | tf_op jit(solution)/shard_map/gather_second/pallas_call | solution.py:222
  134.3 4.4 %fusion.33 = f32[1024,512]{1,0:T(8,128)} fusion(bf16[1024,1024]{1,0:T(8,128)(2,1)} %bitcast.104, bf16[1024,512]{1,0:T(8,128)(2,1)} %bitcast.106), kind=kOutput, calls=%fused_computation.95 | convolution fusion | flops 1073741824 | bytes 5242880 | tf_op jit(solution)/shard_map/dot_general | solution.py:45
  138.7 5.1 %fusion.32 = (f32[512]{0:T(512)S(1)}, bf16[1024,512]{1,0:T(8,128)(2,1)S(1)}) fusion(f32[1024,512]{1,0:T(8,128)} %fusion.33, f32[512]{0:T(512)S(1)} %bitcast.98, bf16[1024,1024]{1,0:T(8,128)(2,1)} %bitcast.102, bf16[512,1024]{1,0:T(8,128)(2,1)} %bitcast.108), kind=kOutput, calls=%fused_computation.94 | convolution fusion | flops 1084751360 | bytes 6295552 | tf_op jit(solution)/shard_map/dot_general | solution.py:45
  143.9 2.3 convolution_convert_fusion.2
  146.1 2.8 convolution_convert_fusion
  149.0 2.4 convolution_convert_fusion.3
  151.4 2.6 convolution_convert_fusion.1
  154.0 29.1 %scatter_second.1 = (bf16[4,128,1024]{2,1,0:T(8,128)(2,1)}, bf16[4,128,1024]{2,1,0:T(8,128)(2,1)}) custom-call(bf16[8,128,1024]{2,1,0:T(8,128)(2,1)} %bitcast.73, bf16[4,128,1024]{2,1,0:T(8,128)(2,1)} %bitcast.82), custom_call_target="tpu_custom_call" | custom-call | tf_op jit(solution)/shard_map/scatter_second/pallas_call | solution.py:222
  183.1 2.9 convert_reduce_fusion.1
  187.6 1.4 convolution_convert_fusion.6.refs_0_
  189.1 16.2 %send_grad.1.refs_2_ = bf16[64,2048]{1,0:T(8,128)(2,1)} custom-call(bf16[1024,128]{1,0:T(8,128)(2,1)} %convolution_convert_fusion.6.refs_0_), custom_call_target="tpu_custom_call" | custom-call | tf_op jit(solution)/shard_map/send_grad/pallas_call | solution.py:222
  205.3 63.7 %attend_back.1 = (bf16[64,2048]{1,0:T(8,128)(2,1)}, bf16[2,64,4096]{2,1,0:T(8,128)(2,1)}, bf16[2,64,1024]{2,1,0:T(8,128)(2,1)}, bf16[2,2,2,64,1024]{4,3,2,1,0:T(...) custom-call(bf16[64,2048]{1,0:T(8,128)(2,1)} %get-tuple-element.46.r, ...), custom_call_target="tpu_custom_call" | custom-call | tf_op jit(solution)/shard_map/attend_back/pallas_call | solution.py:222
  269.0 1.5 convert_reduce_fusion.5
  270.8 0.9 copy-done.4
  272.1 5.7 %fusion.26 = (f32[1024]{0:T(1024)S(1)}, f32[1024]{0:T(1024)S(1)}, bf16[1024,1024]{1,0:T(8,128)(2,1)}, bf16[1024,1024]{1,0:T(8,128)(2,1)}) fusion(f32[1024]{0:T(1024)S(1)} %get-tuple-element.102, f32[1024]{0:T(1024)S(1)} %get-tuple-element.100, bf16[8,128,1024]{2,1,0:T(8,128)(2,1)S(1)} %copy-done, f32[1024]{0:T(1024)S(1)} %reshape.304, ...), kind=kOutput, calls=%fused_computation.88 | convolution fusion | flops 818149376 | bytes 8675328 | tf_op jit(solution)/shard_map/dot_general | solution.py:45
  279.1 2.8 convolution_convert_fusion.5
  282.0 3.8 %convolution_convert_fusion.4 = bf16[1024,384]{1,0:T(8,128)(2,1)} fusion(bf16[1024,1024]{1,0:T(8,128)(2,1)} %get-tuple-element.82, f32[128,1024]{1,0:T(8,128)S(1)} %bitcast.81, f32[128,1024]{1,0:T(8,128)S(1)} %bitcast.78, f32[128,1024]{1,0:T(8,128)S(1)} %copy-done.5), kind=kOutput, calls=%fused_computation.29 | convolution fusion | flops 808058880 | bytes 4456448 | tf_op jit(solution)/shard_map/dot_general | solution.py:45
  285.8 2.2 reduce_sum.265
  287.9 52.4 %scatter_first.1 = (bf16[4,128,1024]{2,1,0:T(8,128)(2,1)}, bf16[4,32,3072]{2,1,0:T(8,128)(2,1)}, bf16[4,32,1024]{2,1,0:T(8,128)(2,1)}, f32[32,8,128]{2,1,0:T(8,128)}, bf16[32,4096]{1,0:T(8,128)(2,1)}) custom-call(bf16[8,128,1024]{2,1,0:T(8,128)(2,1)} %bitcast.72, bf16[32,32,384]{2,1,0:T(8,128)(2,1)} %bitcast.86, bf16[4,32,1024]{2,1,0:T(8,128)(2,1)} %bitcast.83, ...), custom_call_target="tpu_custom_call" | custom-call | tf_op jit(solution)/shard_map/scatter_first/pallas_call | solution.py:222
  340.3 1.5 convert_reduce_fusion.4
  342.5 1.0 fusion.17
  344.4 0.9 convert_reduce_fusion.7
  (104 shorter events, 11.0 us)
Async XLA Ops:
  41.9 3.3 copy-start
  46.1 1.1 copy-start.21
  49.2 57.2 %copy-start.1 = (bf16[128,1024]{1,0:T(8,128)(2,1)S(1)}, bf16[128,1024]{1,0:T(8,128)(2,1)}, u32[]{:S(2)}) copy-start(bf16[128,1024]{1,0:T(8,128)(2,1)} %refs_0_.1) | copy-start | bytes 786436
  138.7 5.1 %copy-start.18 = (bf16[8,128,1024]{2,1,0:T(8,128)(2,1)S(1)}, bf16[8,128,1024]{2,1,0:T(8,128)(2,1)}, u32[]{:S(2)}) copy-start(bf16[8,128,1024]{2,1,0:T(8,128)(2,1)} %get-tuple-element.53) | copy-start | bytes 6291460
  143.9 2.3 copy-start.20
  143.9 2.3 copy-start.22
  146.1 2.8 copy-start.17
  149.0 2.4 copy-start.19
  183.1 3.2 copy-start.11
  186.1 1.6 copy-start.2
  186.7 0.7 copy-start.3
  269.0 1.7 copy-start.14
  270.7 1.1 copy-start.6
  270.7 1.1 copy-start.8
  270.8 0.9 copy-start.4
  277.8 4.1 %copy-start.5 = (f32[128,1024]{1,0:T(8,128)S(1)}, f32[128,1024]{1,0:T(8,128)}, u32[]{:S(2)}) copy-start(f32[128,1024]{1,0:T(8,128)} %copy-done.4) | copy-start | bytes 1572868
  277.8 4.1 %copy-start.7 = (f32[2,1,64,1024]{3,2,1,0:T(8,128)S(1)}, f32[2,1,64,1024]{3,2,1,0:T(8,128)}, u32[]{:S(2)}) copy-start(f32[2,1,64,1024]{3,2,1,0:T(8,128)} %copy-done.6) | copy-start | bytes 1572868
  277.8 4.1 %copy-start.9 = (f32[2,1,64,1024]{3,2,1,0:T(8,128)S(1)}, f32[2,1,64,1024]{3,2,1,0:T(8,128)}, u32[]{:S(2)}) copy-start(f32[2,1,64,1024]{3,2,1,0:T(8,128)} %copy-done.8) | copy-start | bytes 1572868
  340.3 3.2 copy-start.13
  341.8 2.5 copy-start.12
  342.5 2.8 copy-start.15
  342.5 3.4 copy-start.16
  342.5 5.2 %copy-start.10 = (bf16[4,128,1024]{2,1,0:T(8,128)(2,1)S(1)}, bf16[4,128,1024]{2,1,0:T(8,128)(2,1)}, u32[]{:S(2)}) copy-start(bf16[4,128,1024]{2,1,0:T(8,128)(2,1)} %get-tuple-element.58) | copy-start | bytes 3145732

commit v3 on v2

--- a/solution.py
+++ b/solution.py
@@ -357,8 +357,8 @@
         carry = (jnp.zeros((deep, width), F32), jnp.zeros((deep, width), F32))
         carry = step(first, carry, True)
         dkey, dvalue = lax.fori_loop(first + 1, queries // wide, lambda i, c: step(i, c, False), carry)
-        dpair_ref[0, :, at] = dkey.T.astype(BF16)
-        dpair_ref[1, :, at] = dvalue.T.astype(BF16)
+        dpair_ref[0, :, at] = dkey.T
+        dpair_ref[1, :, at] = dvalue.T
 
         @pl.when(lax.rem(j, band) == band - 1)
         def _():
@@ -627,129 +627,227 @@
             vmem_outs=2,
         )
 
-        block_in = residual_in.astype(F32)
-        hidden = block_in + (dot(attended_t, merge_full, 0, 0) + merge_shift)
-        scaled_two, inverse_two = normalize(hidden)
-        input_two = (scaled_two * gain_two + shift_two).astype(BF16)
-
-        def gather_second(wire, normed, shrink, normed_all, shrink_all):
-            me, t = wire.me, wire.t
+        lines = jnp.stack([merge_shift, gain_two, shift_two])
+        shift_units = lax.dynamic_index_in_dim(expand_shift.reshape(blocks, G, UNITS), member, 1, False).reshape(1, -1)
+        pair_rows = 2 * rows
+
+        def feed(
+            wire, att, merge, x, cot, cot_all, expand, shrink, lines, shift,
+            hidden, grad_hidden, grad_input, grad_att, shrunk, grad_expand, sums, unit_sums, shrink_grads,
+            normed, normed_all, shrink_all, act, slope, grad_pre, scaled, inverse, two_send, got, two_own, summed, two_all, shrink_part,
+        ):
+            me, t, m = wire.me, wire.t, wire.m
             block = me // shares
             user = lax.rem(block, G)
-            normed_gather = Gather(wire, 1, normed, lambda k: normed_all.at[k], normed_all.at[pl.ds(0, 4)])
-            normed_gather.start()
+            here = lax.rem(m, 2)
+            pair = m // 2
+            pairs = [pair, flip(pair, 2)]
+            theirs = [flip(p, 1) for p in pairs]
 
             def to_users(step):
                 other = lax.rem(t + step, groups)
-                wire.give(0, shrink, shrink_all.at[block // G * shares + lax.rem(me, shares)], other * G + user)
+                slot = block // G * shares + lax.rem(me, shares)
+                wire.give(0, shrink, shrink_all.at[span(slot, hidden_rows), :], other * G + user)
 
             loop(0, groups, to_users)
-            normed_gather.forward()
-            wire.settle_given(0, user == wire.m, shrink_all.at[pl.ds(0, groups - 1)], (shrink, shrink_all))
-            normed_gather.finish()
-
-        normed_all, shrink_all = exchange(
-            gather_second,
-            "gather_second",
+            step = min(32, rows)
+            hidden[...] = dot(att[...].T, merge[...], 1, 0)
+
+            def first_norm(i):
+                at = span(i, step)
+                value = x[at, :].astype(F32) + (hidden[at, :] + lines[0:1, :])
+                centred = value - jnp.mean(value, axis=1, keepdims=True)
+                inv = lax.rsqrt(jnp.mean(centred * centred, axis=1, keepdims=True) + EPSILON)
+                hidden[at, :] = value
+                scaled[at, :] = centred * inv
+                inverse[at, :] = inv
+                normed[at, :] = (centred * inv * lines[1:2, :] + lines[2:3, :]).astype(BF16)
+
+            loop(0, rows // step, first_norm)
+            place = lambda k: normed_all.at[span(k, rows), :]
+            for k, other in enumerate(wire.peers):
+                wire.put(1 + k, normed, place(m), t * G + other)
+            wire.put(4, normed, place(m), wire.sibling)
+            wire.keep(1, normed, place(m))
+
+            def enter(p):
+                at = span(p, pair_rows)
+                pre_act = dot(normed_all[at, :], expand[...], 1, 0) + shift[...]
+                activated, derivative = gelu_pair(pre_act)
+                act[at, :] = activated.astype(BF16)
+                slope[at, :] = derivative
+
+            def passed(k):
+                other = wire.peers[k]
+                wire.came(1 + k, place(other))
+                wire.put(4, place(other), place(other), wire.sibling)
+
+            wire.kept(1, place(m))
+            passed(0)
+            enter(pairs[0])
+            passed(1)
+            passed(2)
+            enter(pairs[1])
+            wire.came(4, normed_all.at[pl.ds(0, 4 * rows), :])
+            enter(theirs[0])
+            enter(theirs[1])
+
+            def shrink_gradient(q):
+                columns = span(q, UNITS)
+                shrink_part[columns, :] = dot(act[:, columns].T, cot_all[...], 1, 0).astype(BF16)
+                for s in range(shares):
+                    piece = shrink_part.at[pl.ds(pl.multiple_of(q * UNITS + s * hidden_rows, hidden_rows), hidden_rows), :]
+                    wire.give(5, piece, shrink_grads.at[t], (q * G + m) * shares + s)
+
+            loop(0, blocks, shrink_gradient)
+            wire.settle_given(
+                0, user == m, shrink_all.at[pl.ds(0, slice_units - hidden_rows), :], (shrink, shrink_all)
+            )
+            unit_sums[...] = jnp.zeros((1, slice_units), F32)
+
+            def leave(p):
+                at = span(p, pair_rows)
+                grad = dot(cot_all[at, :], shrink_all[...], 1, 1) * slope[at, :]
+                unit_sums[...] += jnp.sum(grad, axis=0, keepdims=True)
+                grad_pre[at, :] = grad.astype(BF16)
+                return dot(grad_pre[at, :], expand[...], 1, 1)
+
+            for a in (1, 0):
+                two_send[a] = leave(theirs[a]).astype(BF16)
+                wire.put(6 + a, two_send.at[a], got.at[a], wire.sibling)
+            two_own[...] = leave(pairs[1])
+            wire.came(7, got.at[1])
+            summed[1] = (two_own[...] + got[1].astype(F32)).astype(BF16)
+            wire.put(8, summed.at[1, span(here, rows), :], two_all.at[0], t * G + wire.peers[1])
+            wire.put(9, summed.at[1, span(1 - here, rows), :], two_all.at[1], t * G + wire.peers[2])
+            two_own[...] = leave(pairs[0])
+            wire.came(6, got.at[0])
+            away = span(1 - here, rows)
+            summed[0, away, :] = (two_own[away, :] + got[0, away, :].astype(F32)).astype(BF16)
+            wire.put(10, summed.at[0, away, :], two_all.at[2], t * G + wire.peers[0])
+
+            def expand_gradient(c):
+                columns = span(c, 256)
+                grad_expand[columns, :] = dot(normed_all[:, columns].T, grad_pre[...], 1, 0).astype(BF16)
+
+            loop(0, width // 256, expand_gradient)
+
+            def forward_out(p):
+                at = span(p, pair_rows)
+                shrunk[at, :] = dot(act[at, :], shrink_all[...], 1, 0).astype(BF16)
+
+            loop(0, 4, forward_out)
+            for k in range(3):
+                wire.came(8 + k, two_all.at[k])
+            sums[...] = jnp.zeros(sums.shape, F32)
+
+            def second_norm(i):
+                at = span(i, step)
+                mine = pl.ds(pl.multiple_of(here * rows + i * step, step), step)
+                grad_two = two_own[mine, :] + got[0, mine, :].astype(F32)
+                for k in range(3):
+                    grad_two = grad_two + two_all[k, at, :].astype(F32)
+                top = cot[at, :].astype(F32)
+                unit = scaled[at, :]
+                grad_scaled = grad_two * lines[1:2, :]
+                mean_one = jnp.mean(grad_scaled, axis=1, keepdims=True)
+                mean_two = jnp.mean(grad_scaled * unit, axis=1, keepdims=True)
+                result = top + inverse[at, :] * (grad_scaled - mean_one - unit * mean_two)
+                grad_hidden[at, :] = result
+                grad_input[at, :] = result.astype(BF16)
+                sums[0:1, :] += jnp.sum(result, axis=0, keepdims=True)
+                sums[1:2, :] += jnp.sum(grad_two * unit, axis=0, keepdims=True)
+                sums[2:3, :] += jnp.sum(grad_two, axis=0, keepdims=True)
+                sums[3:4, :] += jnp.sum(top, axis=0, keepdims=True)
+
+            loop(0, rows // step, second_norm)
+            grad_att[...] = dot(merge[...], grad_input[...], 1, 1).astype(BF16)
+            for k in range(3):
+                wire.sent(1 + k, normed)
+                wire.sent(8 + k, two_all.at[k])
+            wire.sent(4, normed_all.at[pl.ds(0, 4 * rows), :])
+            wire.sent(6, got.at[0])
+            wire.sent(7, got.at[1])
+            wire.settle_given(
+                5, lax.rem(me // shares, G) == m, shrink_grads.at[pl.ds(0, groups - 1)], (shrink_grads.at[0], shrink_grads)
+            )
+
+        (
+            hidden, grad_hidden, grad_hidden_input, grad_attended_t, shrunk_part, grad_expand_part, second_sums, grad_expand_shift, shrink_parts,
+        ) = exchange(
+            feed,
+            "feed",
             3,
             sizes,
-            5,
-            (input_two, shrink_weight),
-            (((G, rows, width), BF16), ((groups, hidden_rows, width), BF16)),
-        )
-        group_two = normed_all.reshape(group_rows, width)
-        group_cot = cot_all.reshape(group_rows, width)
-        expand_slice = expand_all.reshape(width, slice_units)
-        shrink_slice = shrink_all.reshape(slice_units, width)
-        shift_units = lax.dynamic_index_in_dim(expand_shift.reshape(blocks, G, UNITS), member, 1, False).reshape(-1)
-        activated, derivative = gelu_pair(dot(group_two, expand_slice, 1, 0) + shift_units)
-        act_input = activated.astype(BF16)
-        shrunk_part = dot(act_input, shrink_slice, 1, 0).astype(BF16)
-        grad_shrink_part = dot(act_input, group_cot, 0, 0).astype(BF16)
-        grad_pre = dot(group_cot, shrink_slice, 1, 1) * derivative
-        grad_expand_shift = jnp.sum(grad_pre, axis=0)
-        grad_pre_input = grad_pre.astype(BF16)
-        grad_expand_part = dot(group_two, grad_pre_input, 0, 0).astype(BF16)
-        grad_two_part = dot(grad_pre_input, expand_slice, 1, 1).astype(BF16)
-
-        def scatter_second(wire, two, shrink, two_all, shrink_all, got, summed):
+            11,
+            (
+                attended_t,
+                merge_full,
+                residual_in,
+                cotangent,
+                cot_all.reshape(group_rows, width),
+                expand_all.reshape(width, slice_units),
+                shrink_weight,
+                lines,
+                shift_units,
+            ),
+            (
+                ((rows, width), F32),
+                ((rows, width), F32),
+                ((rows, width), BF16),
+                ((width, rows), BF16),
+                ((group_rows, width), BF16),
+                ((width, slice_units), BF16),
+                ((4, width), F32),
+                ((1, slice_units), F32),
+                ((groups, hidden_rows, width), BF16),
+            ),
+            scratch=[
+                pltpu.VMEM((rows, width), BF16),
+                pltpu.VMEM((group_rows, width), BF16),
+                pltpu.VMEM((slice_units, width), BF16),
+                pltpu.VMEM((group_rows, slice_units), BF16),
+                pltpu.VMEM((group_rows, slice_units), F32),
+                pltpu.VMEM((group_rows, slice_units), BF16),
+                pltpu.VMEM((rows, width), F32),
+                pltpu.VMEM((rows, 1), F32),
+                pltpu.VMEM((2, pair_rows, width), BF16),
+                pltpu.VMEM((2, pair_rows, width), BF16),
+                pltpu.VMEM((pair_rows, width), F32),
+                pltpu.VMEM((2, pair_rows, width), BF16),
+                pltpu.VMEM((3, rows, width), BF16),
+                pltpu.VMEM((slice_units, width), BF16),
+            ],
+            vmem_outs=8,
+        )
+        block_in = residual_in.astype(F32)
+        grad_shrink_weight = jnp.sum(shrink_parts.astype(F32), axis=0)
+        grad_merge_shift, grad_gain_two, grad_shift_two, grad_shrink_shift = (second_sums[k] for k in range(4))
+
+        wide, deep, band = tiles_of(queries, parts)
+        pairs = tokens // deep // 2
+
+        def attend_back(
+            wire, query, pair, grad_own, out, total, shrunk, hidden_grad, att, expand,
+            dq_all, dpair_all, shrunk_all, hidden_all, att_all, expand_all,
+            grad, dq, dpair, dpair_out, query_rows, grad_rows, delta, dq_sum, pair_got, got, summed,
+        ):
             me, t, m = wire.me, wire.t, wire.m
-            two_scatter = Scatter(wire, 1, two, got, summed, two_all)
-            two_scatter.start()
-
-            def to_owners(step):
-                piece = lax.rem(step + t, groups)
-                owner = (piece // shares * G + m) * shares + lax.rem(piece, shares)
-                wire.give(0, shrink.at[piece], shrink_all.at[t], owner)
-
-            loop(0, groups, to_owners)
-            two_scatter.forward()
-            wire.settle_given(
-                0, lax.rem(me // shares, G) == m, shrink_all.at[pl.ds(0, groups - 1)], (shrink_all.at[0], shrink_all)
-            )
-            two_scatter.finish()
-
-        two_parts, shrink_parts = exchange(
-            scatter_second,
-            "scatter_second",
-            4,
-            sizes,
-            5,
-            (
-                grad_two_part.reshape(G, rows, width),
-                grad_shrink_part.reshape(groups, hidden_rows, width),
-            ),
-            (((4, rows, width), BF16), ((groups, hidden_rows, width), BF16)),
-            scratch=scatter_scratch(rows, width),
-        )
-        grad_shrink_weight = jnp.sum(shrink_parts.astype(F32), axis=0)
-        grad_top = cotangent.astype(F32)
-        grad_shrink_shift = jnp.sum(grad_top, axis=0)
-        grad_two = jnp.sum(two_parts.astype(F32), axis=0)
-        grad_gain_two = jnp.sum(grad_two * scaled_two, axis=0)
-        grad_shift_two = jnp.sum(grad_two, axis=0)
-        grad_hidden = grad_top + normalize_back(grad_two, scaled_two, inverse_two, gain_two)
-        grad_merge_shift = jnp.sum(grad_hidden, axis=0)
-        grad_hidden_input = grad_hidden.astype(BF16)
-        grad_attended_t = dot(merge_full, grad_hidden_input, 1, 1).astype(BF16)
-
-        def send_grad(wire, grad, grad_out):
-            me = wire.me
-            part = lax.rem(me, parts)
-            place = span(me // parts, rows)
+            shrunk_scatter = Scatter(wire, 5, shrunk, got, summed, shrunk_all)
+            hidden_gather = Gather(wire, 9, hidden_grad, lambda k: hidden_all.at[k], hidden_all.at[pl.ds(0, 4)])
+            first_pair = 13
+            own_part = lax.rem(me, parts)
+            own_place = span(me // parts, rows)
 
             def to_head(step):
                 h = lax.rem(step + me, H)
                 source_m = h // 2
-                quarter = lax.rem(source_m // 2, 2) * 2 + lax.rem(h, 2)
-                t = quarter * sizes.chips + part // 2
-                device = t * G + source_m + 2 * (lax.rem(part, 2) - lax.rem(source_m // 2, 2))
-                wire.give(0, grad.at[span(h, head), :], grad_out.at[:, place], device)
+                source_core = lax.rem(source_m // 2, 2)
+                chip = (source_core * 2 + lax.rem(h, 2)) * sizes.chips + own_part // 2
+                device = chip * G + source_m + 2 * (lax.rem(own_part, 2) - source_core)
+                wire.give(4, grad_own.at[span(h, head), :], grad.at[:, own_place], device)
 
             loop(0, H, to_head)
-            mine = wire.part == part
-
-            @pl.when(mine)
-            def _():
-                wire.kept(0, grad.at[pl.ds(0, head), :])
-                wire.came(0, grad_out.at[:, pl.ds(0, queries - rows)])
-                wire.sent(0, grad.at[pl.ds(0, width - head), :])
-
-            @pl.when(jnp.logical_not(mine))
-            def _():
-                wire.came(0, grad_out)
-                wire.sent(0, grad)
-
-        (grad_t,) = exchange(send_grad, "send_grad", 5, sizes, 1, (grad_attended_t,), (((head, queries), BF16),))
-
-        def attend_back(
-            wire, query, pair, grad, out, total, shrunk, hidden_grad, att, expand,
-            dq, dpair, dq_all, dpair_all, shrunk_all, hidden_all, att_all, expand_all,
-            query_rows, grad_rows, delta, dq_sum, got, summed,
-        ):
-            me, t, m = wire.me, wire.t, wire.m
-            shrunk_scatter = Scatter(wire, 4, shrunk, got, summed, shrunk_all)
-            hidden_gather = Gather(wire, 8, hidden_grad, lambda k: hidden_all.at[k], hidden_all.at[pl.ds(0, 4)])
             shrunk_scatter.start()
             hidden_gather.start()
             place = pl.ds(pl.multiple_of(m * rows, 128), rows)
@@ -761,12 +859,48 @@
             loop(1, G, to_group)
             wire.keep(2, att.at[span(m, slice_width), :], att_all.at[:, place])
             shrunk_scatter.forward()
-            wide, deep, band = tiles_of(queries, parts)
-
-            def after(j, first, final):
+            mine = wire.part == own_part
+
+            @pl.when(mine)
+            def _():
+                wire.kept(4, grad_own.at[pl.ds(0, head), :])
+                wire.came(4, grad.at[:, pl.ds(0, queries - rows)])
+                wire.sent(4, grad_own.at[pl.ds(0, width - head), :])
+
+            @pl.when(jnp.logical_not(mine))
+            def _():
+                wire.came(4, grad)
+                wire.sent(4, grad_own)
+
+            def to_column(step):
+                other, device = wire.column(step)
+                wire.put(3, expand.at[other], expand_all.at[t], device)
+
+            loop(1, groups, to_column)
+            wire.keep(3, expand.at[t], expand_all.at[t])
+            chip = lax.rem(t, sizes.chips)
+
+            def hand_over(j):
+                at = span(j, deep)
+                dpair_out[:, :, at] = dpair[:, :, at].astype(BF16)
+                wire.put(first_pair + j // 2, dpair_out.at[:, :, at], pair_got.at[j // 2], wire.sibling)
+
+            def add_up(j):
+                at = span(j, deep)
+                wire.came(first_pair + j // 2, pair_got.at[j // 2])
+                dpair_out[:, :, at] = (dpair[:, :, at] + pair_got[j // 2].astype(F32)).astype(BF16)
                 place_in_group = pl.ds(pl.multiple_of(lax.rem(j * deep, group_rows), deep), deep)
                 device = j * deep // group_rows * G + wire.source_m
-                wire.give(0, dpair.at[:, :, span(j, deep)], dpair_all.at[wire.part, wire.which, :, :, place_in_group], device)
+                wire.give(0, dpair_out.at[:, :, at], dpair_all.at[chip, wire.which, :, :, place_in_group], device)
+
+            def after(j, first, final):
+                @pl.when(lax.rem(j, 2) != wire.core)
+                def _():
+                    hand_over(j)
+
+                @pl.when(jnp.logical_and(lax.rem(j + 1, 2) == wire.core, j > 0))
+                def _():
+                    add_up(j - 1)
 
                 @pl.when(final)
                 def _():
@@ -780,41 +914,34 @@
                             owner // G * G + wire.source_m,
                         )
 
-                @pl.when(j == 2)
-                def _():
-                    def to_column(step):
-                        other, device = wire.column(step)
-                        wire.put(3, expand.at[other], expand_all.at[t], device)
-
-                    loop(1, groups, to_column)
-                    wire.keep(3, expand.at[t], expand_all.at[t])
-
-                @pl.when(j == keys_tiles - 2)
+                @pl.when(j == 2 * pairs - 2)
                 def _():
                     hidden_gather.forward()
 
-            keys_tiles = tokens // deep
             attend_back_tiles(
                 wire, query, pair, grad, out, total, dq, dpair, query_rows, grad_rows, delta, dq_sum, after
             )
+
+            @pl.when(wire.core == 1)
+            def _():
+                add_up(2 * pairs - 1)
+
             own = wire.core == wire.source_core
+            wire_half = dpair_out.at[:, :, pl.ds(0, tokens // 2)]
 
             @pl.when(own)
             def _():
-                wire.kept(0, dpair.at[:, :, pl.ds(0, group_rows)])
+                wire.kept(0, dpair_out.at[:, :, pl.ds(0, deep)])
                 wire.kept(1, dq.at[:, pl.ds(0, chunk)])
-                wire.sent(0, dpair.at[:, :, pl.ds(0, tokens - group_rows)])
-                wire.sent(1, dq.at[:, pl.ds(0, queries - chunk)])
-                wire.came(0, dpair.at[:, :, pl.ds(0, tokens - group_rows)])
-                wire.came(1, dq.at[:, pl.ds(0, queries - chunk)])
+                wire.settle(0, dpair_out.at[:, :, pl.ds(0, tokens // 2 - deep)])
+                wire.settle(1, dq.at[:, pl.ds(0, queries - chunk)])
 
             @pl.when(jnp.logical_not(own))
             def _():
-                wire.sent(0, dpair)
-                wire.sent(1, dq)
-                wire.came(0, dpair)
-                wire.came(1, dq)
-
+                wire.settle(0, wire_half)
+                wire.settle(1, dq)
+
+            loop(0, pairs, lambda k: wire.sent(first_pair + k, pair_got.at[0]))
             wire.kept(2, att_all.at[:, pl.ds(0, rows)])
             wire.settle(2, att_all.at[:, pl.ds(0, group_rows - rows)])
             wire.kept(3, expand_all.at[0])
@@ -822,16 +949,16 @@
             shrunk_scatter.finish()
             hidden_gather.finish()
 
-        _, _, dq_all, dpair_all, shrunk_parts, grad_all, att_all, expand_parts = exchange(
+        dq_all, dpair_all, shrunk_parts, grad_all, att_all, expand_parts = exchange(
             attend_back,
             "attend_back",
             6,
             sizes,
-            12,
+            13 + pairs,
             (
                 query_t,
                 pair_t,
-                grad_t,
+                grad_attended_t,
                 out_t,
                 log_total,
                 shrunk_part.reshape(G, rows, width),
@@ -840,23 +967,25 @@
                 grad_expand_part.reshape(groups, G * depth, slice_units),
             ),
             (
-                ((head, queries), BF16),
-                ((2, head, tokens), BF16),
                 ((2, head, group_rows), BF16),
-                ((parts, 2, 2, head, group_rows), BF16),
+                ((sizes.chips, 2, 2, head, group_rows), BF16),
                 ((4, rows, width), BF16),
                 ((G, rows, width), BF16),
                 ((slice_width, group_rows), BF16),
                 ((groups, G * depth, slice_units), BF16),
             ),
             scratch=[
+                pltpu.VMEM((head, queries), BF16),
+                pltpu.VMEM((head, queries), BF16),
+                pltpu.VMEM((2, head, tokens), F32),
+                pltpu.VMEM((2, head, tokens), BF16),
                 pltpu.VMEM((queries, head), BF16),
                 pltpu.VMEM((queries, head), BF16),
                 pltpu.VMEM((1, queries), F32),
                 pltpu.VMEM((head, queries), F32),
+                pltpu.VMEM((pairs, 2, head, deep), BF16),
                 *scatter_scratch(rows, width),
             ],
-            vmem_outs=2,
         )
         residual_out = (hidden + jnp.sum(shrunk_parts.astype(F32), axis=0) + shrink_shift).astype(BF16)
         grad_expand_group = jnp.sum(expand_parts.astype(F32), axis=0).astype(BF16).reshape(G, depth, slice_units)

time: 349 us -> 291 us (0.83)
  Pallas kernels: 278 us -> 248 us
  matrix products: 37.5 us -> 12.3 us
    pallas_call x8 -> x6, Pallas kernels: 278 us -> 248 us  [exchange(): pl.pallas_call(kernel, out_shape=[jax.ShapeDtypeStruct(shape, kind) for s...]
    dot_general x12 -> x4, matrix products: 37.5 us -> 12.3 us  [dot(): lax.dot_general(left, right, (((left_dim,), (right_dim,)), ((), ())), pre...]
where the time goes in v3:
time: 291 us; the launch traced here: 290 us
  Pallas kernels  248 us (85%)
  other arithmetic  16.4 us (6%)
  local copies, waits for them, and re-layouts  12.3 us (4%)
  matrix products  12.3 us (4%)
    pallas_call x6, Pallas kernels, exchange(): pl.pallas_call(kernel, out_shape=[jax.ShapeDtypeStruct(shape, kind) for s...  248 us
    dot_general x4, matrix products, dot(): lax.dot_general(left, right, (((left_dim,), (right_dim,)), ((), ())), pre...  12.3 us

profile of v3, /device:TPU:0, one launch (start us, length us, event | category | flops | bytes accessed | tf_op | source)
XLA Modules:
  0.0 290.2 jit_solution(10687611362659587288)
XLA Ops:
  0.7 5.4 %concatenate.12 = bf16[384]{0:T(512)(128)(2,1)S(1)} concatenate(bf16[32]{0:T(256)(128)(2,1)} %param.15, bf16[32]{0:T(256)(128)(2,1)} %param.16, bf16[64]{0:T(256)(128)(2,1)} %param.18, bf16[32]{0:T(256)(128)(2,1)} %param.20, bf16[32]{0:T(256)(128)(2,1)} %param.21, bf16[32]{0:T(256)(128)(2,1)} %param.22, bf16[128]{0:T(256)(128)(2,1)} %param.24, bf16[32]{0:T(256)(128)(2,1)} %param.26), dimensions={0} | concatenate | bytes 1536 | tf_op jit(solution)/shard_map/concatenate | solution.py:413
  6.1 0.6 pad_bitcast_fusion.1.refs_3_
  6.7 35.1 %gather_first.1 = (bf16[8,128,1024]{2,1,0:T(8,128)(2,1)}, bf16[32,32,384]{2,1,0:T(8,128)(2,1)}, bf16[4,32,1024]{2,1,0:T(8,128)(2,1)}, bf16[32,16,128]{2,1,0:T(8,128)(2,1)}, bf16[8,32,512]{2,1,0:T(8,128)(2,1)}) custom-call(bf16[128,1024]{1,0:T(8,128)(2,1)} %refs_2_.3, bf16[32,3072]{1,0:T(8,128)(2,1)} %refs_1_.1, bf16[32,1024]{1,0:T(8,128)(2,1)} %refs_2_.2, ...), custom_call_target="tpu_custom_call" | custom-call | tf_op jit(solution)/shard_map/gather_first/pallas_call | solution.py:222
  41.9 1.1 copy.33
  43.2 1.9 convert_reduce_fusion
  45.1 0.7 multiply_reduce_fusion.1
  46.1 0.8 add_convert_fusion.1
  47.2 1.9 add_convert_fusion.2
  49.2 21.7 %spread_heads.1 = (bf16[2,64,4096]{2,1,0:T(8,128)(2,1)}, bf16[64,2048]{1,0:T(8,128)(2,1)}, bf16[4,8,32,1024]{3,2,1,0:T(8,128)(2,1)}) custom-call(bf16[3,2,64,1024]{3,2,1,0:T(8,128)(2,1)} %bitcast.74, bf16[4,32,1024]{2,1,0:T(8,128)(2,1)} %get-tuple-element.50.refs_1_), custom_call_target="tpu_custom_call" | custom-call | tf_op jit(solution)/shard_map/spread_heads/pallas_call | solution.py:222
  70.9 35.3 %attend.1 = (bf16[64,2048]{1,0:T(8,128)(2,1)}, f32[1,2048]{1,0:T(1,128)}, bf16[1024,128]{1,0:T(8,128)(2,1)}, bf16[4,8,32,512]{3,2,1,0:T(8,128)(2,1)}, bf16[8,128,1024]{2,1,0:T(8,128)(2,1)}) custom-call(bf16[64,2048]{1,0:T(8,128)(2,1)} %get-tuple-element.51.refs_0_, bf16[2,64,4096]{2,1,0:T(8,128)(2,1)} %get-tuple-element.52.refs_1_, ...), custom_call_target="tpu_custom_call" | custom-call | tf_op jit(solution)/shard_map/attend/pallas_call | solution.py:222
  106.4 0.6 fusion.12.refs_8_
  107.2 0.6 maximum_convert_fusion.refs_7_
  107.8 51.1 %feed.1 = (f32[128,1024]{1,0:T(8,128)}, f32[128,1024]{1,0:T(8,128)}, bf16[128,1024]{1,0:T(8,128)(2,1)}, bf16[1024,128]{1,0:T(8,128)(2,1)}, bf16[1024,1024]{1,0:T...) custom-call(bf16[1024,128]{1,0:T(8,128)(2,1)} %get-tuple-element.54., ...), custom_call_target="tpu_custom_call" | custom-call | tf_op jit(solution)/shard_map/feed/pallas_call | solution.py:222
  158.9 54.3 %attend_back.1 = (bf16[2,64,1024]{2,1,0:T(8,128)(2,1)}, bf16[1,2,2,64,1024]{4,3,2,1,0:T(8,128)(2,1)}, bf16[4,128,1024]{2,1,0:T(8,128)(2,1)}, bf16[8,128,1024]{2,...) custom-call(bf16[64,2048]{1,0:T(8,128)(2,1)} %get-tuple-element.51.refs_0_, ...), custom_call_target="tpu_custom_call" | custom-call | tf_op jit(solution)/shard_map/attend_back/pallas_call | solution.py:222
  213.2 1.2 bitcast_convert_fusion
  214.5 0.7 copy-done.2
  215.7 5.4 %fusion.18 = (f32[1024]{0:T(1024)S(1)}, f32[1024]{0:T(1024)S(1)}, bf16[1024,1024]{1,0:T(8,128)(2,1)}, bf16[1024,1024]{1,0:T(8,128)(2,1)}) fusion(f32[1024]{0:T(1024)S(1)} %get-tuple-element.108, f32[1024]{0:T(1024)S(1)} %get-tuple-element.106, bf16[8,128,1024]{2,1,0:T(8,128)(2,1)S(1)} %copy-done, f32[1024]{0:T(1024)S(1)} %reshape.272, ...), kind=kOutput, calls=%fused_computation.59 | convolution fusion | flops 818149376 | bytes 8675328 | tf_op jit(solution)/shard_map/dot_general | solution.py:45
  221.8 0.7 copy.31
  222.5 2.7 convolution_convert_fusion.1
  225.2 2.2 convolution_convert_fusion
  227.4 0.9 reduce_sum.165
  228.3 50.7 %scatter_first.1 = (bf16[4,128,1024]{2,1,0:T(8,128)(2,1)}, bf16[4,32,3072]{2,1,0:T(8,128)(2,1)}, bf16[4,32,1024]{2,1,0:T(8,128)(2,1)}, f32[32,8,128]{2,1,0:T(8,128)}, bf16[32,4096]{1,0:T(8,128)(2,1)}) custom-call(bf16[8,128,1024]{2,1,0:T(8,128)(2,1)} %bitcast.58, bf16[32,32,384]{2,1,0:T(8,128)(2,1)} %bitcast.73, bf16[4,32,1024]{2,1,0:T(8,128)(2,1)} %bitcast.69, ...), custom_call_target="tpu_custom_call" | custom-call | tf_op jit(solution)/shard_map/scatter_first/pallas_call | solution.py:222
  279.0 1.5 convert_reduce_fusion.2
  281.2 0.5 broadcast_multiply_fusion.1
  282.5 2.5 fusion.10
  285.0 0.8 convert_element_type.172
  285.8 0.9 convert_reduce_fusion.4
  286.7 0.7 convert_reduce_fusion.6
  287.4 0.6 fusion.21
  288.0 0.6 slice.90
  288.6 0.6 slice.94
  289.2 1.0 convert_reduce_fusion.1
  (74 shorter events, 3.7 us)
Async XLA Ops:
  41.9 3.3 %copy-start = (bf16[8,128,1024]{2,1,0:T(8,128)(2,1)S(1)}, bf16[8,128,1024]{2,1,0:T(8,128)(2,1)}, u32[]{:S(2)}) copy-start(bf16[8,128,1024]{2,1,0:T(8,128)(2,1)} %get-tuple-element.48) | copy-start | bytes 6291460
  46.1 1.1 copy-start.15
  213.2 1.3 copy-start.10
  214.5 0.8 copy-start.2
  215.7 5.5 %copy-start.14 = (f32[1,512]{1,0:T(1,128)S(1)}, f32[1,512]{1,0:T(1,128)}, u32[]{:S(2)}) copy-start(f32[1,512]{1,0:T(1,128)} %get-tuple-element.72) | copy-start | bytes 6148
  215.7 5.6 %copy-start.13 = (f32[4,1024]{1,0:T(4,128)S(1)}, f32[4,1024]{1,0:T(4,128)}, u32[]{:S(2)}) copy-start(f32[4,1024]{1,0:T(4,128)} %get-tuple-element.71) | copy-start | bytes 49156
  215.7 6.7 %copy-start.8 = (bf16[128,1024]{1,0:T(8,128)(2,1)S(1)}, bf16[128,1024]{1,0:T(8,128)(2,1)}, u32[]{:S(2)}) copy-start(bf16[128,1024]{1,0:T(8,128)(2,1)} %get-tuple-element.69) | copy-start | bytes 786436
  221.1 4.1 %copy-start.3 = (f32[2,1,64,1024]{3,2,1,0:T(8,128)S(1)}, f32[2,1,64,1024]{3,2,1,0:T(8,128)}, u32[]{:S(2)}) copy-start(f32[2,1,64,1024]{3,2,1,0:T(8,128)} %copy-done.2) | copy-start | bytes 1572868
  221.7 3.5 %copy-start.16 = (bf16[1024,1024]{1,0:T(8,128)(2,1)S(1)}, bf16[1024,1024]{1,0:T(8,128)(2,1)}, u32[]{:S(2)}) copy-start(bf16[1024,1024]{1,0:T(8,128)(2,1)} %get-tuple-element.89) | copy-start | bytes 6291460
  225.2 2.2 copy-start.6
  228.3 52.3 %copy-start.1 = (bf16[128,1024]{1,0:T(8,128)(2,1)S(1)}, bf16[128,1024]{1,0:T(8,128)(2,1)}, u32[]{:S(2)}) copy-start(bf16[128,1024]{1,0:T(8,128)(2,1)} %refs_2_.3) | copy-start | bytes 786436
  279.0 3.2 %copy-start.5 = (bf16[4,128,1024]{2,1,0:T(8,128)(2,1)S(1)}, bf16[4,128,1024]{2,1,0:T(8,128)(2,1)}, u32[]{:S(2)}) copy-start(bf16[4,128,1024]{2,1,0:T(8,128)(2,1)} %get-tuple-element.65) | copy-start | bytes 3145732
  282.2 2.8 copy-start.9
  282.4 3.4 %copy-start.7 = (bf16[4,32,3072]{2,1,0:T(8,128)(2,1)S(1)}, bf16[4,32,3072]{2,1,0:T(8,128)(2,1)}, u32[]{:S(2)}) copy-start(bf16[4,32,3072]{2,1,0:T(8,128)(2,1)} %get-tuple-element.76) | copy-start | bytes 2359300
  282.5 4.2 %copy-start.11 = (bf16[4,32,1024]{2,1,0:T(8,128)(2,1)S(1)}, bf16[4,32,1024]{2,1,0:T(8,128)(2,1)}, u32[]{:S(2)}) copy-start(bf16[4,32,1024]{2,1,0:T(8,128)(2,1)} %get-tuple-element.77) | copy-start | bytes 786436
  282.5 4.9 %copy-start.12 = (f32[32,8,128]{2,1,0:T(8,128)S(1)}, f32[32,8,128]{2,1,0:T(8,128)}, u32[]{:S(2)}) copy-start(f32[32,8,128]{2,1,0:T(8,128)} %get-tuple-element.75) | copy-start | bytes 393220
  282.5 6.7 %copy-start.4 = (bf16[4,128,1024]{2,1,0:T(8,128)(2,1)S(1)}, bf16[4,128,1024]{2,1,0:T(8,128)(2,1)}, u32[]{:S(2)}) copy-start(bf16[4,128,1024]{2,1,0:T(8,128)(2,1)} %get-tuple-element.79) | copy-start | bytes 3145732

commit v4 on v3

--- a/solution.py
+++ b/solution.py
@@ -165,6 +165,155 @@
         for k in range(3):
             wire.sent(self.lane + k, self.place(wire.m))
         wire.settle(self.lane + 3, self.four)
+
+
+class Relay:
+    def __init__(self, wire, lane, shard, place):
+        self.wire, self.lane, self.shard, self.place = wire, lane, shard, place
+        self.groups = wire.sizes.groups
+        self.upper = lax.rem(wire.t, 2)
+        self.mate = flip(wire.t, 1)
+
+    def start(self):
+        wire, t = self.wire, self.wire.t
+        mine = self.place(t)
+        wire.put(self.lane + t, self.shard, mine, self.mate * G + wire.m)
+
+        def to_pair(step):
+            pair = lax.rem(t // 2 + step, self.groups // 2)
+            near = 2 * pair + jnp.where(pair < t // 2, 1, 0)
+            wire.put(self.lane + t, self.shard, mine, near * G + wire.m)
+
+        loop(1, self.groups // 2, to_pair)
+        wire.keep(self.lane, self.shard, mine)
+
+    def passes(self, distance):
+        source = self.wire.t + jnp.where(self.upper == 1, distance, -distance)
+        return source, jnp.logical_and(source >= 0, source < self.groups)
+
+    def forward(self, low, high):
+        def one(distance):
+            source, there = self.passes(distance)
+
+            @pl.when(there)
+            def _():
+                here = self.place(source)
+                self.wire.came(self.lane + source, here)
+                self.wire.put(self.lane + source, here, here, self.mate * G + self.wire.m)
+
+        loop(low, high, one)
+
+    def arrive(self):
+        wire, t = self.wire, self.wire.t
+        wire.kept(self.lane, self.place(t))
+
+        def one(step):
+            source = lax.rem(t + step, self.groups)
+            passed = jnp.where(self.upper == 1, source > t, source < t)
+
+            @pl.when(jnp.logical_not(passed))
+            def _():
+                wire.came(self.lane + source, self.place(source))
+
+        loop(1, self.groups, one)
+
+    def finish(self, half):
+        self.wire.sent(self.lane + self.wire.t, half)
+
+        def one(distance):
+            source, there = self.passes(distance)
+
+            @pl.when(there)
+            def _():
+                self.wire.sent(self.lane + source, self.place(source))
+
+        loop(1, self.groups, one)
+
+
+class Collect:
+    def __init__(self, wire, lane, parts, got, summed, result):
+        self.wire, self.lane = wire, lane
+        self.parts, self.got, self.summed, self.result = parts, got, summed, result
+        self.groups = wire.sizes.groups
+        self.upper = lax.rem(wire.t, 2)
+        self.mate = flip(wire.t, 1)
+        self.pair = wire.t // 2
+        self.out = lane + self.groups + self.pair
+
+    def passes(self, distance):
+        target = self.wire.t + jnp.where(self.upper == 1, distance, -distance)
+        return target, jnp.logical_and(target >= 0, target < self.groups)
+
+    def leaves(self, distance):
+        target = self.mate + jnp.where(self.upper == 1, -distance, distance)
+        return target, jnp.logical_and(target >= 0, target < self.groups)
+
+    def start(self, make=lambda target: None):
+        wire = self.wire
+
+        def one(distance):
+            target, there = self.leaves(distance)
+
+            @pl.when(there)
+            def _():
+                make(target)
+                wire.put(self.lane + target, self.parts.at[target], self.got.at[target], self.mate * G + wire.m)
+
+        loop(1, self.groups, one)
+        make(self.mate)
+        wire.put(self.out, self.parts.at[self.mate], self.result.at[self.pair], self.mate * G + wire.m)
+
+        def other(distance):
+            target, there = self.passes(distance)
+
+            @pl.when(there)
+            def _():
+                make(target)
+
+        loop(1, self.groups, other)
+        make(wire.t)
+
+    def forward(self, low, high):
+        wire = self.wire
+        rows = self.parts.shape[1]
+        step = math.gcd(rows, 32)
+
+        def one(distance):
+            target, there = self.passes(distance)
+
+            @pl.when(there)
+            def _():
+                wire.came(self.lane + target, self.got.at[target])
+
+                def add(i):
+                    at = span(i, step)
+                    total = self.parts[target, at, :].astype(F32) + self.got[target, at, :].astype(F32)
+                    self.summed[target, at, :] = total.astype(BF16)
+
+                loop(0, rows // step, add)
+                wire.put(self.out, self.summed.at[target], self.result.at[self.pair], target * G + wire.m)
+
+        loop(low, high, one)
+
+    def finish(self):
+        wire = self.wire
+        loop(0, self.groups // 2, lambda q: wire.came(self.lane + self.groups + q, self.result.at[q]))
+        wire.sent(self.out, self.result.at[0])
+
+        def one(distance):
+            target, there = self.passes(distance)
+
+            @pl.when(there)
+            def _():
+                wire.sent(self.out, self.result.at[0])
+
+            gone, was = self.leaves(distance)
+
+            @pl.when(was)
+            def _():
+                wire.sent(self.lane + gone, self.result.at[0])
+
+        loop(1, self.groups, one)
 
 
 class Scatter:
@@ -409,26 +558,25 @@
 
         small = (first_gain, first_shift, attend_bias, merge_bias, second_gain, second_shift, expand_bias, shrink_bias)
         counts = [s.shape[0] for s in small]
-        packed_rows = -(-sum(counts) // 2048) * 16
-        packed = jnp.pad(jnp.concatenate(small), (0, packed_rows * 128 - sum(counts))).reshape(packed_rows, 128)
+        packed_rows = -(-sum(counts) // 1024) * 8
+        packed = jnp.zeros((packed_rows * 128,), F32)
+        for k, vector in enumerate(small):
+            low = sum(counts[:k])
+            packed = packed + jnp.pad(vector.astype(F32), (low, packed_rows * 128 - low - counts[k]))
+        packed = packed.astype(BF16).reshape(packed_rows, 128)
 
         def unit_block(q, m):
             return span(q * G + m, UNITS)
 
-        def gather_first(wire, x, attend, merge, vec, expand, x_all, attend_all, merge_all, vec_all, expand_all):
+        def gather_first(
+            wire, x, attend, merge, vec, expand, x_all, attend_all, merge_all, vec_all, expand_all, attend_group
+        ):
             me, t, m = wire.me, wire.t, wire.m
-            x_gather = Gather(wire, 4, x, lambda k: x_all.at[k], x_all.at[pl.ds(0, 4)])
-            x_gather.start()
 
             def attend_to(other, move):
                 for p in range(3):
                     columns = pl.ds(pl.multiple_of(p * width + other * slice_width, 128), slice_width)
-                    move(0, attend.at[:, columns], attend_all.at[me, :, pl.ds(p * slice_width, slice_width)])
-
-            def to_all(step):
-                device = lax.rem(me + step, n)
-                attend_to(lax.rem(device, G), lambda lane, s, d: wire.put(lane, s, d, device))
-                wire.put(1, vec, vec_all.at[me], device)
+                    move(0, attend.at[:, columns], attend_group.at[m, :, pl.ds(p * slice_width, slice_width)])
 
             def expand_to(other, move):
                 for q in range(blocks):
@@ -436,44 +584,59 @@
 
             def to_group(step):
                 other, device = wire.group(step)
+                attend_to(other, lambda lane, s, d: wire.put(lane, s, d, device))
+
+            def to_all(step):
+                device = lax.rem(me + step, n)
+                wire.put(1, vec, vec_all.at[me], device)
+
+            def more_to_group(step):
+                other, device = wire.group(step)
                 expand_to(other, lambda lane, s, d: wire.put(lane, s, d, device))
 
-            def to_column(step):
-                _, device = wire.column(step)
-                wire.put(2, merge, merge_all.at[t], device)
-
+            loop(1, G, to_group)
+            merge_relay = Relay(wire, 8, merge, lambda k: merge_all.at[k])
+            merge_relay.start()
+            x_gather = Gather(wire, 4, x, lambda k: x_all.at[k], x_all.at[pl.ds(0, 4)])
+            x_gather.start()
+            attend_to(m, wire.keep)
             loop(1, n, to_all)
-            loop(1, groups, to_column)
-            loop(1, G, to_group)
-            attend_to(m, wire.keep)
+            loop(1, G, more_to_group)
             wire.keep(1, vec, vec_all.at[me])
-            wire.keep(2, merge, merge_all.at[t])
             expand_to(m, wire.keep)
-            wire.kept(0, attend_all.at[0])
+            wire.kept(0, attend_group.at[0])
+            wire.settle(0, attend_group.at[pl.ds(0, G - 1)])
+            attend_relay = Relay(wire, 8 + groups, attend_group, lambda k: attend_all.at[k])
+            attend_relay.start()
+            merge_relay.forward(1, groups)
             wire.kept(1, vec_all.at[0])
-            wire.kept(2, merge_all.at[0])
             wire.kept(3, expand_all.at[0])
+            attend_relay.forward(1, 2)
             x_gather.forward()
-            wire.settle(0, attend_all.at[pl.ds(0, n - 1)])
+            attend_relay.forward(2, groups)
             wire.settle(1, vec_all.at[pl.ds(0, n - 1)])
-            wire.settle(2, merge_all.at[pl.ds(0, groups - 1)])
             wire.settle(3, expand_all.at[pl.ds(0, G - 1)])
             x_gather.finish()
+            merge_relay.arrive()
+            attend_relay.arrive()
+            merge_relay.finish(merge_all.at[pl.ds(0, groups // 2)])
+            attend_relay.finish(attend_all.at[pl.ds(0, groups // 2)])
 
         x_all, attend_all, merge_all, vec_all, expand_group = exchange(
             gather_first,
             "gather_first",
             0,
             sizes,
-            8,
+            8 + 2 * groups,
             (residual_in, attend_weight, merge_weight, packed, expand_weight),
             (
                 ((G, rows, width), BF16),
-                ((n, depth, 3 * slice_width), BF16),
+                ((groups, G, depth, 3 * slice_width), BF16),
                 ((groups, depth, width), BF16),
                 ((n, packed_rows, 128), BF16),
                 ((G, depth, slice_units), BF16),
             ),
+            scratch=[pltpu.VMEM((G, depth, 3 * slice_width), BF16)],
         )
         flat = vec_all.reshape(n, packed_rows * 128)
         spots = [sum(counts[:k]) for k in range(len(counts))]
@@ -484,6 +647,7 @@
 
         scaled_group, _ = normalize(x_all.reshape(group_rows, width).astype(F32))
         input_one = (scaled_group * gain_one + shift_one).astype(BF16)
+        input_one, scaled_group = lax.optimization_barrier((input_one, scaled_group.astype(BF16)))
         bias_mine = jnp.concatenate(
             [
                 lax.dynamic_slice_in_dim(attend_shift, member * slice_width, slice_width),
@@ -572,13 +736,9 @@
             me, t = wire.me, wire.t
             cot_gather = Gather(wire, 2, cot, lambda k: cot_all.at[k], cot_all.at[pl.ds(0, 4)])
 
-            def to_column(step):
-                _, device = wire.column(step)
-                wire.put(1, expand, expand_all.at[t], device)
-
-            loop(1, groups, to_column)
+            relay = Relay(wire, 6, expand, lambda k: expand_all.at[k])
+            relay.start()
             cot_gather.start()
-            wire.keep(1, expand, expand_all.at[t])
             place = span(wire.head, head)
             wide = tiles_of(queries, parts)[0]
 
@@ -587,6 +747,12 @@
                     block = tile * (wide // rows) + b
                     wire.give(0, out.at[:, span(block, rows)], attended.at[place, :], block * parts + wire.part)
 
+                for k in (1, 2):
+
+                    @pl.when(tile == queries // wide - 4 + k)
+                    def _(k=k):
+                        relay.forward(k, k + 1)
+
                 @pl.when(tile == queries // wide - 2)
                 def _():
                     cot_gather.forward()
@@ -605,8 +771,9 @@
                 wire.came(0, attended)
                 wire.sent(0, out)
 
-            wire.kept(1, expand_all.at[0])
-            wire.settle(1, expand_all.at[pl.ds(0, groups - 1)])
+            relay.forward(3, groups)
+            relay.arrive()
+            relay.finish(expand_all.at[pl.ds(0, groups // 2)])
             cot_gather.finish()
 
         out_t, log_total, attended_t, expand_all, cot_all = exchange(
@@ -614,7 +781,7 @@
             "attend",
             2,
             sizes,
-            6,
+            6 + groups,
             (query_t, pair_t, expand_group, cotangent),
             (
                 ((head, queries), BF16),
@@ -633,8 +800,9 @@
 
         def feed(
             wire, att, merge, x, cot, cot_all, expand, shrink, lines, shift,
-            hidden, grad_hidden, grad_input, grad_att, shrunk, grad_expand, sums, unit_sums, shrink_grads,
+            hidden, grad_hidden, grad_input, grad_att, shrunk, grad_expand, sums, unit_sums, shrink_own, shrink_grads,
             normed, normed_all, shrink_all, act, slope, grad_pre, scaled, inverse, two_send, got, two_own, summed, two_all, shrink_part,
+            part_got, part_sum,
         ):
             me, t, m = wire.me, wire.t, wire.m
             block = me // shares
@@ -649,7 +817,12 @@
                 slot = block // G * shares + lax.rem(me, shares)
                 wire.give(0, shrink, shrink_all.at[span(slot, hidden_rows), :], other * G + user)
 
-            loop(0, groups, to_users)
+            if shares == 1:
+                relay = Relay(wire, 11, shrink, lambda k: shrink_all.at[span(k, hidden_rows), :])
+                collect = Collect(wire, 11 + groups, shrink_part, part_got, part_sum, shrink_grads)
+                relay.start()
+            else:
+                loop(0, groups, to_users)
             step = min(32, rows)
             hidden[...] = dot(att[...].T, merge[...], 1, 0)
 
@@ -684,9 +857,13 @@
 
             wire.kept(1, place(m))
             passed(0)
+            if shares == 1:
+                relay.forward(1, 2)
             enter(pairs[0])
             passed(1)
             passed(2)
+            if shares == 1:
+                relay.forward(2, groups)
             enter(pairs[1])
             wire.came(4, normed_all.at[pl.ds(0, 4 * rows), :])
             enter(theirs[0])
@@ -694,15 +871,21 @@
 
             def shrink_gradient(q):
                 columns = span(q, UNITS)
-                shrink_part[columns, :] = dot(act[:, columns].T, cot_all[...], 1, 0).astype(BF16)
+                total = dot(act[:, columns].T, cot_all[...], 1, 0)
                 for s in range(shares):
-                    piece = shrink_part.at[pl.ds(pl.multiple_of(q * UNITS + s * hidden_rows, hidden_rows), hidden_rows), :]
-                    wire.give(5, piece, shrink_grads.at[t], (q * G + m) * shares + s)
+                    piece = q * shares + s
+                    shrink_part[piece] = total[s * hidden_rows : (s + 1) * hidden_rows, :].astype(BF16)
+                    if shares > 1:
+                        wire.give(5, shrink_part.at[piece], shrink_grads.at[t], (q * G + m) * shares + s)
 
             loop(0, blocks, shrink_gradient)
-            wire.settle_given(
-                0, user == m, shrink_all.at[pl.ds(0, slice_units - hidden_rows), :], (shrink, shrink_all)
-            )
+            if shares == 1:
+                collect.start()
+                relay.arrive()
+            else:
+                wire.settle_given(
+                    0, user == m, shrink_all.at[pl.ds(0, slice_units - hidden_rows), :], (shrink, shrink_all)
+                )
             unit_sums[...] = jnp.zeros((1, slice_units), F32)
 
             def leave(p):
@@ -715,6 +898,8 @@
             for a in (1, 0):
                 two_send[a] = leave(theirs[a]).astype(BF16)
                 wire.put(6 + a, two_send.at[a], got.at[a], wire.sibling)
+            if shares == 1:
+                collect.forward(1, 2)
             two_own[...] = leave(pairs[1])
             wire.came(7, got.at[1])
             summed[1] = (two_own[...] + got[1].astype(F32)).astype(BF16)
@@ -725,6 +910,9 @@
             away = span(1 - here, rows)
             summed[0, away, :] = (two_own[away, :] + got[0, away, :].astype(F32)).astype(BF16)
             wire.put(10, summed.at[0, away, :], two_all.at[2], t * G + wire.peers[0])
+
+            if shares == 1:
+                collect.forward(2, groups)
 
             def expand_gradient(c):
                 columns = span(c, 256)
@@ -768,18 +956,25 @@
             wire.sent(4, normed_all.at[pl.ds(0, 4 * rows), :])
             wire.sent(6, got.at[0])
             wire.sent(7, got.at[1])
-            wire.settle_given(
-                5, lax.rem(me // shares, G) == m, shrink_grads.at[pl.ds(0, groups - 1)], (shrink_grads.at[0], shrink_grads)
-            )
-
+            if shares == 1:
+                relay.finish(shrink_all.at[pl.ds(0, groups // 2 * hidden_rows), :])
+                collect.finish()
+                shrink_own[...] = shrink_part[t]
+            else:
+                shrink_own[...] = jnp.zeros(shrink_own.shape, BF16)
+                wire.settle_given(
+                    5, lax.rem(me // shares, G) == m, shrink_grads.at[pl.ds(0, groups - 1)], (shrink_grads.at[0], shrink_grads)
+                )
+
+        shrink_terms = groups // 2 if shares == 1 else groups
         (
-            hidden, grad_hidden, grad_hidden_input, grad_attended_t, shrunk_part, grad_expand_part, second_sums, grad_expand_shift, shrink_parts,
+            hidden, grad_hidden, grad_hidden_input, grad_attended_t, shrunk_part, grad_expand_part, second_sums, grad_expand_shift, shrink_own, shrink_parts,
         ) = exchange(
             feed,
             "feed",
             3,
             sizes,
-            11,
+            11 + groups + groups * 3 // 2,
             (
                 attended_t,
                 merge_full,
@@ -800,7 +995,8 @@
                 ((width, slice_units), BF16),
                 ((4, width), F32),
                 ((1, slice_units), F32),
-                ((groups, hidden_rows, width), BF16),
+                ((hidden_rows, width), BF16),
+                ((shrink_terms, hidden_rows, width), BF16),
             ),
             scratch=[
                 pltpu.VMEM((rows, width), BF16),
@@ -816,21 +1012,17 @@
                 pltpu.VMEM((pair_rows, width), F32),
                 pltpu.VMEM((2, pair_rows, width), BF16),
                 pltpu.VMEM((3, rows, width), BF16),
-                pltpu.VMEM((slice_units, width), BF16),
+                *([pltpu.VMEM((groups, hidden_rows, width), BF16)] * 3),
             ],
-            vmem_outs=8,
+            vmem_outs=9,
         )
-        block_in = residual_in.astype(F32)
-        grad_shrink_weight = jnp.sum(shrink_parts.astype(F32), axis=0)
-        grad_merge_shift, grad_gain_two, grad_shift_two, grad_shrink_shift = (second_sums[k] for k in range(4))
-
         wide, deep, band = tiles_of(queries, parts)
         pairs = tokens // deep // 2
 
         def attend_back(
             wire, query, pair, grad_own, out, total, shrunk, hidden_grad, att, expand,
             dq_all, dpair_all, shrunk_all, hidden_all, att_all, expand_all,
-            grad, dq, dpair, dpair_out, query_rows, grad_rows, delta, dq_sum, pair_got, got, summed,
+            grad, dq, dpair, dpair_out, query_rows, grad_rows, delta, dq_sum, pair_got, got, summed, part_got, part_sum,
         ):
             me, t, m = wire.me, wire.t, wire.m
             shrunk_scatter = Scatter(wire, 5, shrunk, got, summed, shrunk_all)
@@ -872,12 +1064,8 @@
                 wire.came(4, grad)
                 wire.sent(4, grad_own)
 
-            def to_column(step):
-                other, device = wire.column(step)
-                wire.put(3, expand.at[other], expand_all.at[t], device)
-
-            loop(1, groups, to_column)
-            wire.keep(3, expand.at[t], expand_all.at[t])
+            collect = Collect(wire, 13 + pairs, expand, part_got, part_sum, expand_all)
+            collect.start()
             chip = lax.rem(t, sizes.chips)
 
             def hand_over(j):
@@ -914,6 +1102,12 @@
                             owner // G * G + wire.source_m,
                         )
 
+                for k in (1, 2):
+
+                    @pl.when(j == k)
+                    def _(k=k):
+                        collect.forward(k, k + 1)
+
                 @pl.when(j == 2 * pairs - 2)
                 def _():
                     hidden_gather.forward()
@@ -944,8 +1138,8 @@
             loop(0, pairs, lambda k: wire.sent(first_pair + k, pair_got.at[0]))
             wire.kept(2, att_all.at[:, pl.ds(0, rows)])
             wire.settle(2, att_all.at[:, pl.ds(0, group_rows - rows)])
-            wire.kept(3, expand_all.at[0])
-            wire.settle(3, expand_all.at[pl.ds(0, groups - 1)])
+            collect.forward(3, groups)
+            collect.finish()
             shrunk_scatter.finish()
             hidden_gather.finish()
 
@@ -954,7 +1148,7 @@
             "attend_back",
             6,
             sizes,
-            13 + pairs,
+            13 + pairs + groups * 3 // 2,
             (
                 query_t,
                 pair_t,
@@ -972,7 +1166,7 @@
                 ((4, rows, width), BF16),
                 ((G, rows, width), BF16),
                 ((slice_width, group_rows), BF16),
-                ((groups, G * depth, slice_units), BF16),
+                ((groups // 2, G * depth, slice_units), BF16),
             ),
             scratch=[
                 pltpu.VMEM((head, queries), BF16),
@@ -985,142 +1179,273 @@
                 pltpu.VMEM((head, queries), F32),
                 pltpu.VMEM((pairs, 2, head, deep), BF16),
                 *scatter_scratch(rows, width),
+                *([pltpu.VMEM((groups, G * depth, slice_units), BF16)] * 2),
             ],
         )
-        residual_out = (hidden + jnp.sum(shrunk_parts.astype(F32), axis=0) + shrink_shift).astype(BF16)
-        grad_expand_group = jnp.sum(expand_parts.astype(F32), axis=0).astype(BF16).reshape(G, depth, slice_units)
-        grad_pair = jnp.sum(dpair_all.astype(F32), axis=0)
-        grad_projected = jnp.concatenate(
-            [
-                dq_all.astype(F32).reshape(slice_width, group_rows),
-                grad_pair[:, 0].reshape(slice_width, group_rows),
-                grad_pair[:, 1].reshape(slice_width, group_rows),
-            ],
-            axis=0,
-        )
-        grad_shift_mine = jnp.sum(grad_projected, axis=1)
-        grad_projected = grad_projected.astype(BF16)
-        grad_attend_part = dot(input_one, grad_projected, 0, 1).astype(BF16)
-        grad_one_part = dot(grad_projected, attend_slice, 0, 1)
-        grad_gain_one = jnp.sum(grad_one_part * scaled_group, axis=0)
-        grad_shift_one = jnp.sum(grad_one_part, axis=0)
-        grad_merge_part = dot(att_all, grad_all.reshape(group_rows, width), 1, 0).astype(BF16)
-
-        grad_attend_shift = jnp.zeros((2 * width,), F32)
-        grad_attend_shift = lax.dynamic_update_slice_in_dim(
-            grad_attend_shift, grad_shift_mine[:slice_width], member * slice_width, 0
-        )
-        grad_attend_shift = lax.dynamic_update_slice_in_dim(
-            grad_attend_shift, grad_shift_mine[2 * slice_width :], width + member * slice_width, 0
-        )
-        grad_expand_all = lax.dynamic_update_slice_in_dim(
-            jnp.zeros((blocks, G, UNITS), F32), grad_expand_shift.reshape(blocks, 1, UNITS), member, 1
-        ).reshape(-1)
-        grads = (
-            grad_gain_one,
-            grad_shift_one,
-            grad_attend_shift,
-            grad_merge_shift,
-            grad_gain_two,
-            grad_shift_two,
-            grad_expand_all,
-            grad_shrink_shift,
-        )
-        total_size = sum(counts)
-        vec_rows = -(-total_size // 1024) * 8
-        packed_grads = jnp.pad(
-            jnp.concatenate([g.reshape(n, -1) for g in grads], axis=1), ((0, 0), (0, vec_rows * 128 - total_size))
-        ).reshape(n, vec_rows, 128)
-
-        def scatter_first(wire, one, attend, merge, vec, expand, one_all, attend_all, merge_all, vec_all, expand_all, got, summed):
+        owners = slice_width // depth
+
+        def close(
+            wire, dq, dpair, entered, unit, attend, att, grad, expand, expand_own, second, unit_sums,
+            one_own, one_all, attend_all, merge_all, main_all, bias_all, unit_all, expand_all,
+            projected, projected_rows, attend_part, part_got, part_sum, part_all, attend_own, merge_part, expand_part,
+            vec, vec_got, vec_sum, send, got, summed,
+        ):
             me, t, m = wire.me, wire.t, wire.m
-            one_scatter = Scatter(wire, 4, one, got, summed, one_all)
-            one_scatter.start()
-
-            def attend_to(device, move):
+            projected[pl.ds(0, slice_width), :] = dq[...]
+            for which in range(2):
+                for kind in range(2):
+                    total = dpair[0, which, kind].astype(F32)
+                    for chip in range(1, sizes.chips):
+                        total = total + dpair[chip, which, kind].astype(F32)
+                    projected[pl.ds((1 + kind) * slice_width + which * head, head), :] = total.astype(BF16)
+            for p in range(3):
+                part = pl.ds(p * slice_width, slice_width)
+                projected_rows[:, part] = projected[part, :].T
+
+            def attend_gradient(target):
+                size = G * depth
+                if size % 128 == 0:
+                    total = dot(entered[:, span(target, size)].T, projected_rows[...], 1, 0)
+                else:
+                    both = dot(entered[:, span(target // 2, 128)].T, projected_rows[...], 1, 0)
+                    total = jnp.where(lax.rem(target, 2) == 0, both[:size], both[size:])
+                attend_part[target] = total.astype(BF16)
+
+            collect = Collect(wire, 12, attend_part, part_got, part_sum, part_all)
+            collect.start(attend_gradient)
+            here = lax.rem(m, 2)
+            pairs = [m // 2, flip(m // 2, 2)]
+            vec[...] = jnp.zeros(vec.shape, F32)
+
+            def leave(p):
+                at = span(p, pair_rows)
+                result = dot(projected_rows[at, :], attend[...], 1, 1)
+                vec[0:1, :] += jnp.sum(result * unit[at, :].astype(F32), axis=0, keepdims=True)
+                vec[1:2, :] += jnp.sum(result, axis=0, keepdims=True)
+                return result
+
+            for a in (1, 0):
+                send[a] = leave(flip(pairs[a], 1)).astype(BF16)
+                wire.put(4 + a, send.at[a], got.at[a], wire.sibling)
+            result = leave(pairs[1])
+            wire.came(5, got.at[1])
+            collect.forward(1, 2)
+            summed[1] = (result + got[1].astype(F32)).astype(BF16)
+            wire.put(6, summed.at[1, span(here, rows), :], one_all.at[0], t * G + wire.peers[1])
+            wire.put(7, summed.at[1, span(1 - here, rows), :], one_all.at[1], t * G + wire.peers[2])
+            result = leave(pairs[0])
+            wire.came(4, got.at[0])
+            result = result + got[0].astype(F32)
+            summed[0] = result.astype(BF16)
+            wire.put(8, summed.at[0, span(1 - here, rows), :], one_all.at[2], t * G + wire.peers[0])
+
+            shift = dot(jnp.ones((8, group_rows), BF16), projected[...], 1, 1)
+            mine = span(m, 128)
+            vec[2:3, mine] = shift[0:1, :slice_width]
+            vec[3:4, mine] = shift[0:1, 2 * slice_width :]
+            vec[4:8, :] = second[...]
+            for q in range(blocks):
+                vec[8 + q : 9 + q, mine] = unit_sums[:, q * UNITS : (q + 1) * UNITS]
+
+            def lanes_to(step):
+                other, device = wire.group(step)
+                wire.put(3, vec.at[:, span(other, 128)], vec_got.at[m], device)
+
+            loop(1, G, lanes_to)
+            wire.keep(3, vec.at[:, mine], vec_got.at[m])
+            collect.forward(2, groups)
+
+            merged = dot(att[...], grad[...], 1, 0)
+            for slot in range(groups):
+                merge_part[slot] = merged[slot * depth : (slot + 1) * depth, :].astype(BF16)
+                wire.give(2, merge_part.at[slot], merge_all.at[t], m * groups + slot)
+            for other in range(G):
+                total = expand_own[t, pl.ds(other * depth, depth), :].astype(F32)
+                for k in range(groups // 2):
+                    total = total + expand[k, pl.ds(other * depth, depth), :].astype(F32)
+                expand_part[other] = total.astype(BF16)
+                for q in range(blocks):
+                    wire.give(
+                        0,
+                        expand_part.at[other, :, pl.ds(q * UNITS, UNITS)],
+                        expand_all.at[:, unit_block(q, m)],
+                        t * G + other,
+                    )
+            wire.kept(3, vec_got.at[0])
+            wire.settle(3, vec_got.at[pl.ds(0, G - 1)])
+            vec_sum[...] = jnp.sum(vec_got[...], axis=0)
+
+            def main_to(k):
+                wire.give(9, vec_sum.at[pl.ds(0, 8)], main_all.at[t], m * owners + lax.rem(k + t, owners))
+
+            def bias_to(k):
+                owner = k // (owners // 2) * (n // 2) + m * (owners // 2) + lax.rem(k, owners // 2)
+                wire.give(10, vec_sum.at[pl.ds(0, 8)], bias_all.at[t], owner)
+
+            def units_to(k):
+                wire.give(11, vec_sum.at[pl.ds(8, 8)], unit_all.at[t], (k // shares * G + m) * shares + lax.rem(k, shares))
+
+            loop(0, owners, main_to)
+            loop(0, owners, bias_to)
+            loop(0, blocks * shares, units_to)
+            one_own[...] = jnp.where(here == 0, result[:rows, :], result[rows:, :])
+            collect.finish()
+            total = attend_part[t].astype(F32)
+            for k in range(groups // 2):
+                total = total + part_all[k].astype(F32)
+            for other in range(G):
+                attend_own[other] = total[other * depth : (other + 1) * depth, :].astype(BF16)
                 for p in range(3):
                     columns = pl.ds(pl.multiple_of(p * width + m * slice_width, 128), slice_width)
-                    move(1, attend.at[device, :, pl.ds(p * slice_width, slice_width)], attend_all.at[t, :, columns])
-
-            def to_all(step):
-                device = lax.rem(me + step, n)
-                attend_to(device, lambda lane, s, d: wire.put(lane, s, d, device))
-                wire.put(3, vec.at[device], vec_all.at[me], device)
-
-            def to_owners(slot):
-                wire.give(2, merge.at[slot], merge_all.at[t], m * groups + slot)
-
-            def expand_to(other, move):
-                for q in range(blocks):
-                    move(0, expand.at[other, :, pl.ds(q * UNITS, UNITS)], expand_all.at[:, unit_block(q, m)])
-
-            def to_group(step):
-                other, device = wire.group(step)
-                expand_to(other, lambda lane, s, d: wire.put(lane, s, d, device))
-
-            loop(1, n // 2, to_all)
-            one_scatter.forward()
-            loop(n // 2, n, to_all)
-            loop(0, groups, to_owners)
-            loop(1, G, to_group)
-            attend_to(me, wire.keep)
-            expand_to(m, wire.keep)
-            wire.keep(3, vec.at[me], vec_all.at[me])
-            wire.kept(0, expand.at[0])
-            wire.kept(1, attend.at[0])
-            wire.kept(3, vec_all.at[0])
-            wire.settle(0, expand.at[pl.ds(0, G - 1)])
-            wire.settle(1, attend.at[pl.ds(0, n - 1)])
-            wire.settle(3, vec_all.at[pl.ds(0, n - 1)])
+                    wire.give(
+                        1, attend_own.at[other, :, pl.ds(p * slice_width, slice_width)], attend_all.at[:, columns], t * G + other
+                    )
+            wire.kept(0, expand_part.at[0])
+            wire.kept(1, attend_own.at[0])
+            wire.settle(0, expand_part.at[pl.ds(0, G - 1)])
+            wire.settle(1, attend_own.at[pl.ds(0, G - 1)])
+            for lane, place, given in (
+                (9, main_all, me // owners == m),
+                (10, bias_all, lax.rem(me, n // 2) // (owners // 2) == m),
+                (11, unit_all, lax.rem(me // shares, G) == m),
+            ):
+                wire.settle_given(lane, given, place.at[pl.ds(0, groups - 1)], (place.at[0], place))
             wire.settle_given(2, me // groups == m, merge_all.at[pl.ds(0, groups - 1)], (merge_all.at[0], merge_all))
-            one_scatter.finish()
-
-        one_parts, attend_parts, merge_parts, vec_parts, expand_whole = exchange(
-            scatter_first,
-            "scatter_first",
+            wire.sent(4, got.at[0])
+            wire.sent(5, got.at[1])
+            for k in range(3):
+                wire.settle(6 + k, one_all.at[k])
+
+        one_own, one_all, attend_parts, merge_parts, main_parts, bias_parts, unit_parts, expand_whole = exchange(
+            close,
+            "close",
             7,
             sizes,
-            8,
+            12 + groups * 3 // 2,
             (
-                grad_one_part.astype(BF16).reshape(G, rows, width),
-                grad_attend_part.reshape(n, depth, 3 * slice_width),
-                grad_merge_part.reshape(groups, depth, width),
-                packed_grads,
-                grad_expand_group,
+                dq_all.reshape(slice_width, group_rows),
+                dpair_all,
+                input_one,
+                scaled_group,
+                attend_slice,
+                att_all,
+                grad_all.reshape(group_rows, width),
+                expand_parts,
+                grad_expand_part.reshape(groups, G * depth, slice_units),
+                second_sums,
+                grad_expand_shift,
             ),
             (
-                ((4, rows, width), BF16),
-                ((groups, depth, 3 * width), BF16),
+                ((rows, width), F32),
+                ((3, rows, width), BF16),
+                ((depth, 3 * width), BF16),
                 ((groups, depth, width), BF16),
-                ((n, vec_rows, 128), F32),
+                *([((groups, 8, 128), F32)] * 3),
                 ((depth, hidden_units), BF16),
             ),
-            scratch=scatter_scratch(rows, width),
+            scratch=[
+                pltpu.VMEM((3 * slice_width, group_rows), BF16),
+                pltpu.VMEM((group_rows, 3 * slice_width), BF16),
+                *([pltpu.VMEM((groups, G * depth, 3 * slice_width), BF16)] * 3),
+                pltpu.VMEM((groups // 2, G * depth, 3 * slice_width), BF16),
+                pltpu.VMEM((G, depth, 3 * slice_width), BF16),
+                pltpu.VMEM((groups, depth, width), BF16),
+                pltpu.VMEM((G, depth, slice_units), BF16),
+                pltpu.VMEM((16, width), F32),
+                pltpu.VMEM((G, 16, 128), F32),
+                pltpu.VMEM((16, 128), F32),
+                pltpu.VMEM((2, pair_rows, width), BF16),
+                pltpu.VMEM((2, pair_rows, width), BF16),
+                pltpu.VMEM((2, pair_rows, width), BF16),
+            ],
+            vmem_outs=1,
         )
-        grad_one = jnp.sum(one_parts.astype(F32), axis=0)
-        scaled_one, inverse_one = normalize(block_in)
-        input_grad = grad_hidden + normalize_back(grad_one, scaled_one, inverse_one, gain_one)
-        grad_attend_weight = jnp.sum(attend_parts.astype(F32), axis=0)
-        grad_merge_weight = jnp.sum(merge_parts.astype(F32), axis=0)
-        vec_sums = jnp.sum(vec_parts, axis=0).reshape(-1)
-        (g_gain_one, g_shift_one, g_attend_bias, g_merge_bias, g_gain_two, g_shift_two, g_expand_bias, g_shrink_bias) = (
-            vec_sums[spot : spot + count] for spot, count in zip(spots, counts)
+
+        def finish(
+            one_own, one_all, x, grad_hidden, hidden, shrunk, gain, shift, attend, merge, expand, shrink, shrink_own, vec_main, vec_bias, vec_units,
+            residual_out, input_grad, attend_out, merge_out, expand_out, shrink_out, vec_out,
+        ):
+            grad_one = one_own[...]
+            for k in range(3):
+                grad_one = grad_one + one_all[k].astype(F32)
+            scaled, inverse = normalize(x[...].astype(F32))
+            input_grad[...] = grad_hidden[...] + normalize_back(grad_one, scaled, inverse, gain[...])
+            total = hidden[...]
+            for k in range(4):
+                total = total + shrunk[k].astype(F32)
+            residual_out[...] = (total + shift[...]).astype(BF16)
+            total = merge[0].astype(F32)
+            for k in range(1, groups):
+                total = total + merge[k].astype(F32)
+            merge_out[...] = total
+            attend_out[...] = attend[...].astype(F32)
+            total = shrink_own[...].astype(F32)
+            for k in range(shrink_terms):
+                total = total + shrink[k].astype(F32)
+            shrink_out[...] = total
+            expand_out[...] = expand[...].astype(F32)
+
+            @pl.when(pl.program_id(0) == 0)
+            def _():
+                for k, source in enumerate((vec_main, vec_bias, vec_units)):
+                    vec_out[k] = jnp.sum(source[...], axis=0)
+
+        turns = 4
+        by_rows = pl.BlockSpec((rows // turns, width), lambda i: (i, 0))
+        by_lanes = lambda r, c: pl.BlockSpec((r, c // turns), lambda i: (0, i))
+        terms = lambda k: pl.BlockSpec((k, rows // turns, width), lambda i: (0, i, 0))
+        terms_by_lanes = lambda k, r, c: pl.BlockSpec((k, r, c // turns), lambda i: (0, 0, i))
+        small_terms = pl.BlockSpec((groups, 8, 128), lambda i: (0, 0, 0))
+        line = pl.BlockSpec((1, width), lambda i: (0, 0))
+        (
+            residual_out, input_grad, grad_attend_weight, grad_merge_weight, grad_expand_weight, grad_shrink_weight, vec_sums,
+        ) = pl.pallas_call(
+            finish,
+            grid=(turns,),
+            out_shape=[
+                jax.ShapeDtypeStruct((rows, width), BF16),
+                jax.ShapeDtypeStruct((rows, width), F32),
+                jax.ShapeDtypeStruct((depth, 3 * width), F32),
+                jax.ShapeDtypeStruct((depth, width), F32),
+                jax.ShapeDtypeStruct((depth, hidden_units), F32),
+                jax.ShapeDtypeStruct((hidden_rows, width), F32),
+                jax.ShapeDtypeStruct((3, 8, 128), F32),
+            ],
+            in_specs=[
+                by_rows, terms(3), by_rows, by_rows, by_rows, terms(4), line, line,
+                by_lanes(depth, 3 * width), terms_by_lanes(groups, depth, width), by_lanes(depth, hidden_units),
+                terms_by_lanes(shrink_terms, hidden_rows, width), by_lanes(hidden_rows, width), small_terms, small_terms, small_terms,
+            ],
+            out_specs=[
+                by_rows, by_rows, by_lanes(depth, 3 * width), by_lanes(depth, width), by_lanes(depth, hidden_units),
+                by_lanes(hidden_rows, width), pl.BlockSpec((3, 8, 128), lambda i: (0, 0, 0)),
+            ],
+            name="finish",
+        )(
+            one_own, one_all, residual_in, grad_hidden, hidden, shrunk_parts, gain_one.reshape(1, width),
+            shrink_shift.reshape(1, width), attend_parts, merge_parts, expand_whole, shrink_parts,
+            shrink_own, main_parts, bias_parts, unit_parts,
         )
+        own = lax.dynamic_slice_in_dim(vec_sums[0], lax.rem(me, 128 // depth) * depth, depth, 1)
+        own_bias = lax.dynamic_slice_in_dim(vec_sums[1, 2:4], lax.rem(2 * me * depth, 128), 2 * depth, 1)
+        own_bias = jnp.where(me < n // 2, own_bias[0], own_bias[1])
+        own_units = lax.dynamic_slice_in_dim(vec_sums[2], lax.rem(me, shares) * hidden_rows, hidden_rows, 1)
+        own_units = lax.dynamic_index_in_dim(own_units, me // (G * shares), 0, False)
         return (
             residual_out,
             input_grad,
-            g_gain_one,
-            g_shift_one,
+            own[0],
+            own[1],
             grad_attend_weight,
-            g_attend_bias,
+            own_bias,
             grad_merge_weight,
-            g_merge_bias,
-            g_gain_two,
-            g_shift_two,
-            expand_whole.astype(F32),
-            g_expand_bias,
+            own[4],
+            own[5],
+            own[6],
+            grad_expand_weight,
+            own_units,
             grad_shrink_weight,
-            g_shrink_bias,
+            own[7],
         )
 
     return on_device

time: 291 us -> 255 us (0.88)
  matrix products: 12.3 us -> 1.97 us
  Pallas kernels: 248 us -> 238 us
  other arithmetic: 16.4 us -> 8.21 us
  local copies, waits for them, and re-layouts: 12.3 us -> 5.55 us
    pallas_call x6, Pallas kernels: 248 us -> 233 us  [exchange(): pl.pallas_call(kernel, out_shape=[jax.ShapeDtypeStruct(shape, kind) for s...]
    dot_general x4 -> x1, matrix products: 12.3 us -> 1.97 us  [dot(): lax.dot_general(left, right, (((left_dim,), (right_dim,)), ((), ())), pre...]
    reduce_sum x10 -> x0, other arithmetic: 6.78 us -> none  [the longest x1 1.54 us: on_device(): grad_one = jnp.sum(one_parts.astype(F32), axis=0)]
    concatenate x2 -> x0, local copies, waits for them, and re-layouts: 5.53 us -> none  [the longest x1 5.43 us: on_device(): jnp.concatenate(small)]
    pallas_call x0 -> x1, Pallas kernels: none -> 5.14 us  [on_device(): pl.pallas_call(finish, grid=(turns,), out_shape=[jax.ShapeDtypeStruct((ro...]
where the time goes in v4:
time: 255 us; the launch traced here: 254 us
  Pallas kernels  238 us (93%)
  other arithmetic  8.21 us (3%)
  local copies, waits for them, and re-layouts  5.55 us (2%)
    pallas_call x6, Pallas kernels, exchange(): pl.pallas_call(kernel, out_shape=[jax.ShapeDtypeStruct(shape, kind) for s...  233 us
    pallas_call x1, Pallas kernels, on_device(): pl.pallas_call(finish, grid=(turns,), out_shape=[jax.ShapeDtypeStruct((ro...  5.14 us

profile of v4, /device:TPU:0, one launch (start us, length us, event | category | flops | bytes accessed | tf_op | source)
XLA Modules:
  0.0 254.3 jit_solution(13882988979170543536)
XLA Ops:
  0.7 1.4 fusion.2.refs_3_
  2.1 31.7 %gather_first.1 = (bf16[8,128,1024]{2,1,0:T(8,128)(2,1)}, bf16[4,8,32,384]{3,2,1,0:T(8,128)(2,1)}, bf16[4,32,1024]{2,1,0:T(8,128)(2,1)}, bf16[32,8,128]{2,1,0:T(8,128)(2,1)}, bf16[8,32,512]{2,1,0:T(8,128)(2,1)}) custom-call(bf16[128,1024]{1,0:T(8,128)(2,1)} %x.17, bf16[32,3072]{1,0:T(8,128)(2,1)} %refs_1_.1, bf16[32,1024]{1,0:T(8,128)(2,1)} %refs_2_.2, ...), custom_call_target="tpu_custom_call" | custom-call | tf_op jit(solution)/shard_map/gather_first/pallas_call | solution.py:371
  33.9 1.0 copy.32
  34.9 1.9 convert_reduce_fusion
  36.8 0.7 multiply_reduce_fusion
  37.5 0.1 slice_bitcast_fusion
  37.6 0.6 fusion.3.refs_8_
  38.2 0.1 slice_convert_fusion.1
  38.3 0.1 reshape.225
  38.4 0.1 fusion.8
  38.4 0.1 slice_convert_fusion
  38.5 0.7 reshape.228.shift
  39.2 0.1 convert_element_type.149
  39.3 0.1 convert_element_type.148
  39.4 0.1 convert_element_type.147
  39.5 0.6 maximum_convert_fusion.refs_7_
  40.2 0.7 reshape.227.gain
  40.9 2.2 fusion.1
  43.2 2.0 add_convert_fusion.1
  45.1 21.0 %spread_heads.1 = (bf16[2,64,4096]{2,1,0:T(8,128)(2,1)}, bf16[64,2048]{1,0:T(8,128)(2,1)}, bf16[4,8,32,1024]{3,2,1,0:T(8,128)(2,1)}) custom-call(bf16[3,2,64,1024]{3,2,1,0:T(8,128)(2,1)} %bitcast.59, bf16[4,32,1024]{2,1,0:T(8,128)(2,1)} %get-tuple-element.64.refs_1_), custom_call_target="tpu_custom_call" | custom-call | tf_op jit(solution)/shard_map/spread_heads/pallas_call | solution.py:371
  66.2 33.5 %attend.1 = (bf16[64,2048]{1,0:T(8,128)(2,1)}, f32[1,2048]{1,0:T(1,128)}, bf16[1024,128]{1,0:T(8,128)(2,1)}, bf16[4,8,32,512]{3,2,1,0:T(8,128)(2,1)}, bf16[8,128,1024]{2,1,0:T(8,128)(2,1)}) custom-call(bf16[64,2048]{1,0:T(8,128)(2,1)} %get-tuple-element.65.refs_0_, bf16[2,64,4096]{2,1,0:T(8,128)(2,1)} %get-tuple-element.66.refs_1_, ...), custom_call_target="tpu_custom_call" | custom-call | tf_op jit(solution)/shard_map/attend/pallas_call | solution.py:371
  99.6 52.8 %feed.1 = (f32[128,1024]{1,0:T(8,128)}, f32[128,1024]{1,0:T(8,128)}, bf16[128,1024]{1,0:T(8,128)(2,1)}, bf16[1024,128]{1,0:T(8,128)(2,1)}, bf16[1024,1024]{1,0:T...) custom-call(bf16[1024,128]{1,0:T(8,128)(2,1)} %get-tuple-element.68., ...), custom_call_target="tpu_custom_call" | custom-call | tf_op jit(solution)/shard_map/feed/pallas_call | solution.py:371
  152.4 50.9 %attend_back.1 = (bf16[2,64,1024]{2,1,0:T(8,128)(2,1)}, bf16[1,2,2,64,1024]{4,3,2,1,0:T(8,128)(2,1)}, bf16[4,128,1024]{2,1,0:T(8,128)(2,1)}, bf16[8,128,1024]{2,...) custom-call(bf16[64,2048]{1,0:T(8,128)(2,1)} %get-tuple-element.65.refs_0_, ...), custom_call_target="tpu_custom_call" | custom-call | tf_op jit(solution)/shard_map/attend_back/pallas_call | solution.py:371
  203.3 42.7 %close.1 = (f32[128,1024]{1,0:T(8,128)}, bf16[3,128,1024]{2,1,0:T(8,128)(2,1)}, bf16[32,3072]{1,0:T(8,128)(2,1)}, bf16[4,32,1024]{2,1,0:T(8,128)(2,1)}, f32[4,8,...) custom-call(bf16[128,1024]{1,0:T(8,128)(2,1)} %bitcast.62, ...), custom_call_target="tpu_custom_call" | custom-call | tf_op jit(solution)/shard_map/close/pallas_call | solution.py:371
  246.0 5.1 %finish.1 = (bf16[128,1024]{1,0:T(8,128)(2,1)}, f32[128,1024]{1,0:T(8,128)}, f32[32,3072]{1,0:T(8,128)}, f32[32,1024]{1,0:T(8,128)}, f32[32,4096]{1,0:T(8,128)},...) custom-call(f32[128,1024]{1,0:T(8,128)} %get-tuple-element.86.one_own, bf16[3,128,1024]{2,1,0:T(8,128)(2,1)} %get-tuple-element.87.one_all, ...), custom_call_target="tpu_custom_call" | custom-call | tf_op jit(solution)/shard_map/finish/pallas_call | solution.py:1402
  251.2 0.7 slice.76
  251.9 0.7 fusion.7
  252.6 0.1 constant_dynamic-slice_fusion.1
  252.6 0.5 fusion.4
  253.2 0.5 fusion.5
  253.7 0.1 constant_dynamic-slice_fusion.2
  253.7 0.5 slice_bitcast_fusion.1
  (12 shorter events, 0.2 us)
Async XLA Ops:
  33.9 3.0 %copy-start = (bf16[8,128,1024]{2,1,0:T(8,128)(2,1)S(1)}, bf16[8,128,1024]{2,1,0:T(8,128)(2,1)}, u32[]{:S(2)}) copy-start(bf16[8,128,1024]{2,1,0:T(8,128)(2,1)} %get-tuple-element.61) | copy-start | bytes 6291460
  40.9 2.2 copy-start.2
  43.1 2.0 copy-start.1
